TPU v7x, 16 devices: a 4x2x1 block of a 4x4x8 slice. The times are simulated.
16 devices in a mesh: dp: 2 (over y, z), sp: 8 (over x, core).
Axes of the slice: x: 4, y: 2, z: 1, core: 2. Of those that a mesh axis runs over, the one named last changes fastest.
The devices are a block of a 4x4x8 slice.
Arguments:
- hidden: bfloat16 [32, 512, 3072], P('dp', 'sp'), parts along dimension 0
- positions: int32 [1024], P(('dp', 'sp')), parts along dimension 0
- long_factor: float32 [64], replicated
- norm_weight: float32 [3072], replicated
- w_qkv: bfloat16 [3072, 5120], replicated
- w_out: bfloat16 [3072, 3072], replicated
- grad_out: bfloat16 [32, 512, 3072], P('dp', 'sp'), parts along dimension 0
Outputs:
- output 1: bfloat16 [32, 512, 3072], P('dp', 'sp'), parts along dimension 0
- output 2: bfloat16 [32, 512, 3072], P('dp', 'sp'), parts along dimension 0
- output 3: float32 [6144], P('dp'), parts along dimension 0
- output 4: float32 [6144, 5120], P('dp'), parts along dimension 0
- output 5: float32 [6144, 3072], P('dp'), parts along dimension 0
There are 2 independent parts. A program takes and returns all parts, laid end to end along the dimension named above; an argument that names none is the same for every part.
All inputs are finite; a program needn't handle non-finite values.
Results may differ from a plain program's by a relative error of at most 0.0114191.
Values are sent between devices in bfloat16 or wider.
A program may use at most 768 MiB of HBM per device.

v0:
```python
import math
import jax
import jax.numpy as jnp
from jax import lax
from jax.sharding import PartitionSpec as P, NamedSharding

NORM_EPS = 1e-5
ROPE_BASE = 10000.0
ROPE_SCALE = math.sqrt(1.0 + math.log(32.0) / math.log(4096.0))


def rotate_half(head_vals):
    half_dim = head_vals.shape[-1] // 2
    return jnp.concatenate([-head_vals[..., half_dim:], head_vals[..., :half_dim]], axis=-1)


def rope_tables(positions, long_factor):
    head_dim = 2 * long_factor.shape[0]
    exponents = jnp.arange(0, head_dim, 2).astype(jnp.float32) / head_dim
    inv_freq = 1.0 / (long_factor * ROPE_BASE ** exponents)
    angles = positions.astype(jnp.float32)[..., None] * inv_freq
    cos_half = jnp.cos(angles) * ROPE_SCALE
    sin_half = jnp.sin(angles) * ROPE_SCALE
    return jnp.concatenate([cos_half, cos_half], axis=-1), jnp.concatenate([sin_half, sin_half], axis=-1)


def apply_rope(head_vals, cos_full, sin_full):
    vals_wide = head_vals.astype(jnp.float32)
    return (vals_wide * cos_full + rotate_half(vals_wide) * sin_full).astype(jnp.bfloat16)


def rope_back(grad_vals, cos_full, sin_full):
    grad_wide = grad_vals.astype(jnp.float32)
    return (grad_wide * cos_full - rotate_half(grad_wide * sin_full)).astype(jnp.bfloat16)


def norm_forward(hidden, norm_weight):
    hidden_wide = hidden.astype(jnp.float32)
    inv_rms = lax.rsqrt(jnp.mean(hidden_wide * hidden_wide, axis=-1, keepdims=True) + NORM_EPS)
    unit_hidden = hidden_wide * inv_rms
    return hidden_wide, inv_rms, unit_hidden, (unit_hidden * norm_weight).astype(jnp.bfloat16)


def norm_backward(grad_normed, grad_out, norm_weight, inv_rms, unit_hidden):
    grad_unit = grad_normed * norm_weight
    grad_inner = inv_rms * (grad_unit - unit_hidden * jnp.mean(grad_unit * unit_hidden, axis=-1, keepdims=True))
    return (grad_out.astype(jnp.float32) + grad_inner).astype(jnp.bfloat16)


def attention_forward(query_grp, key_all, value_all, causal):
    score_scale = query_grp.shape[-1] ** -0.5
    scores = jnp.einsum('bqkgd,bskd->bkgqs', query_grp, key_all, preferred_element_type=jnp.float32) * score_scale
    attn_probs = jax.nn.softmax(jnp.where(causal, scores, -jnp.inf), axis=-1)
    probs_low = attn_probs.astype(jnp.bfloat16)
    attn_grp = jnp.einsum('bkgqs,bskd->bqkgd', probs_low, value_all, preferred_element_type=jnp.float32).astype(jnp.bfloat16)
    return attn_grp, attn_probs, probs_low


def attention_backward(grad_grp, query_grp, key_all, value_all, attn_probs, probs_low):
    score_scale = query_grp.shape[-1] ** -0.5
    grad_probs = jnp.einsum('bqkgd,bskd->bkgqs', grad_grp, value_all, preferred_element_type=jnp.float32).astype(jnp.bfloat16)
    row_dot = jnp.sum(grad_probs * attn_probs, axis=-1, keepdims=True)
    grad_scores = (attn_probs * (grad_probs - row_dot) * score_scale).astype(jnp.bfloat16)
    grad_value = jnp.einsum('bkgqs,bqkgd->bskd', probs_low, grad_grp, preferred_element_type=jnp.float32)
    grad_key = jnp.einsum('bkgqs,bqkgd->bskd', grad_scores, query_grp, preferred_element_type=jnp.float32)
    grad_query = jnp.einsum('bkgqs,bskd->bqkgd', grad_scores, key_all, preferred_element_type=jnp.float32).astype(jnp.bfloat16)
    return grad_query, grad_key, grad_value


def block_body(hidden, positions, long_factor, norm_weight, w_qkv, w_out, grad_out):
    batch_size, seq_local, model_dim = hidden.shape
    head_dim = 2 * long_factor.shape[0]
    query_dim = w_out.shape[0]
    kv_dim = (w_qkv.shape[1] - query_dim) // 2
    num_heads = query_dim // head_dim
    kv_heads = kv_dim // head_dim
    group_size = num_heads // kv_heads
    cos_full, sin_full = rope_tables(positions, long_factor)
    cos_full = cos_full[:, None, :]
    sin_full = sin_full[:, None, :]
    hidden_wide, inv_rms, unit_hidden, normed = norm_forward(hidden, norm_weight)
    qkv_proj = jnp.einsum('bsd,de->bse', normed, w_qkv, preferred_element_type=jnp.float32).astype(jnp.bfloat16)
    query_rot = apply_rope(qkv_proj[..., :query_dim].reshape(batch_size, seq_local, num_heads, head_dim), cos_full, sin_full)
    key_rot = apply_rope(qkv_proj[..., query_dim:query_dim + kv_dim].reshape(batch_size, seq_local, kv_heads, head_dim), cos_full, sin_full)
    value_loc = qkv_proj[..., query_dim + kv_dim:].reshape(batch_size, seq_local, kv_heads, head_dim)
    query_heads = lax.all_to_all(query_rot, 'sp', 2, 1, tiled=True)
    key_heads = lax.all_to_all(key_rot, 'sp', 2, 1, tiled=True)
    value_heads = lax.all_to_all(value_loc, 'sp', 2, 1, tiled=True)
    seq_len = query_heads.shape[1]
    kv_local = key_heads.shape[2]
    query_grp = query_heads.reshape(batch_size, seq_len, kv_local, group_size, head_dim)
    row_ids = lax.broadcasted_iota(jnp.int32, (seq_len, seq_len), 0)
    col_ids = lax.broadcasted_iota(jnp.int32, (seq_len, seq_len), 1)
    attn_grp, attn_probs, probs_low = attention_forward(query_grp, key_heads, value_heads, row_ids >= col_ids)
    attn_back = lax.all_to_all(attn_grp.reshape(batch_size, seq_len, kv_local * group_size, head_dim), 'sp', 1, 2, tiled=True)
    attn_flat = attn_back.reshape(batch_size, seq_local, query_dim)
    mixed_out = jnp.einsum('bse,ed->bsd', attn_flat, w_out, preferred_element_type=jnp.float32)
    out_hidden = (hidden_wide + mixed_out).astype(jnp.bfloat16)

    grad_wout = jnp.einsum('bse,bsd->ed', attn_flat, grad_out, preferred_element_type=jnp.float32)
    grad_attn = jnp.einsum('bsd,ed->bse', grad_out, w_out, preferred_element_type=jnp.float32).astype(jnp.bfloat16)
    grad_heads = lax.all_to_all(grad_attn.reshape(batch_size, seq_local, num_heads, head_dim), 'sp', 2, 1, tiled=True)
    grad_grp = grad_heads.reshape(batch_size, seq_len, kv_local, group_size, head_dim)
    grad_query, grad_key, grad_value = attention_backward(grad_grp, query_grp, key_heads, value_heads, attn_probs, probs_low)
    grad_query_loc = lax.all_to_all(grad_query.reshape(batch_size, seq_len, kv_local * group_size, head_dim), 'sp', 1, 2, tiled=True)
    grad_key_loc = lax.all_to_all(grad_key.astype(jnp.bfloat16), 'sp', 1, 2, tiled=True)
    grad_value_loc = lax.all_to_all(grad_value.astype(jnp.bfloat16), 'sp', 1, 2, tiled=True)
    grad_qkv = jnp.concatenate([
        rope_back(grad_query_loc, cos_full, sin_full).reshape(batch_size, seq_local, query_dim),
        rope_back(grad_key_loc, cos_full, sin_full).reshape(batch_size, seq_local, kv_dim),
        grad_value_loc.reshape(batch_size, seq_local, kv_dim)], axis=-1)
    grad_wqkv = jnp.einsum('bsd,bse->de', normed, grad_qkv, preferred_element_type=jnp.float32)
    grad_normed = jnp.einsum('bse,de->bsd', grad_qkv, w_qkv, preferred_element_type=jnp.float32).astype(jnp.bfloat16)
    grad_norm = jnp.sum(grad_normed * unit_hidden, axis=(0, 1))
    grad_hidden = norm_backward(grad_normed, grad_out, norm_weight, inv_rms, unit_hidden)
    return out_hidden, grad_hidden, lax.psum(grad_norm, 'sp'), lax.psum(grad_wqkv, 'sp'), lax.psum(grad_wout, 'sp')


def solution(mesh):
    token_spec = P('dp', 'sp', None)
    return jax.shard_map(block_body, mesh=mesh,
                         in_specs=(token_spec, P(('dp', 'sp')), P(), P(), P(), P(), token_spec),
                         out_specs=(token_spec, token_spec, P('dp'), P('dp', None), P('dp', None)),
                         check_vma=False)
```

profile of v0, /device:TPU:113, one launch (start us, length us, event | category | flops | bytes accessed | tf_op | source)
XLA Modules:
  0.0 1836.8 jit_solution(15829732178201636845)
XLA Ops:
  7.2 4.1 fusion.34
  11.3 38.2 %fusion.39 = bf16[16,64,5120]{2,1,0:T(8,128)(2,1)S(1)} fusion(bf16[3072,5120]{1,0:T(8,128)(2,1)} %param.11, bf16[16,64,3072]{2,1,0:T(8,128)(2,1)} %param.7, f32[3072]{0:T(1024)} %param.10, f32[16,64]{1,0:T(8,128)S(1)} %add_rsqrt_fusion), kind=kOutput, calls=%fused_computation.58 | convolution fusion | flops 32230080512 | bytes 48250880 | tf_op jit(solution)/shard_map/bsd,de->bse/dot_general | solution.py:82
  49.5 4.0 copy-done.2
  53.5 2.8 convert_bitcast_fusion.8
  58.2 6.0 all-to-all-start
  64.3 2.9 copy.176
  72.0 18.2 all-to-all-done
  90.3 5.8 all-to-all-start.1
  96.0 24.6 %convert_bitcast_fusion.4 = bf16[16,8,24,8,128]{4,3,2,1,0:T(8,128)(2,1)S(1)} fusion(bf16[16,64,3072]{2,1,0:T(8,128)(2,1)} %param.13, bf16[3072,3072]{1,0:T(8,128)(2,1)} %param.12), kind=kOutput, calls=%fused_computation.61 | convolution fusion | flops 19330498560 | bytes 31457280 | tf_op jit(solution)/shard_map/bsd,ed->bse/dot_general | solution.py:101
  120.6 4.5 copy.175
  125.1 4.9 all-to-all-start.4
  130.0 4.5 copy_bitcast_fusion
  134.5 9.9 slice_negate_fusion.1
  144.3 11.7 fusion.38
  156.1 4.2 copy.107
  160.3 40.8 %all-to-all-done.4 = bf16[16,64,24,128]{3,1,0,2:T(8,128)(2,1)} async-done(((bf16[16,64,24,128]{3,1,0,2:T(8,128)(2,1)}), bf16[16,64,24,128]{3,1,0,2:T(8,128)(2,1)}, u32[]{:S(2)}, u32[]{:S(2)}) %all-to-all-start.4) | async-done | bytes 6291488 | tf_op jit(solution)/shard_map/all_to_all | solution.py:102
  201.0 6.1 all-to-all-start.2
  207.2 3.2 copy.103
  212.1 7.7 copy.117
  219.8 58.4 %all-to-all-done.2 = bf16[16,64,24,128]{3,1,0,2:T(8,128)(2,1)} async-done(((bf16[16,64,24,128]{3,1,0,2:T(8,128)(2,1)}), bf16[16,64,24,128]{3,1,0,2:T(8,128)(2,1)}, u32[]{:S(2)}, u32[]{:S(2)}) %all-to-all-start.2) | async-done | bytes 6291488 | tf_op jit(solution)/shard_map/all_to_all | solution.py:86
  278.2 4.3 copy.109
  282.5 22.6 %fusion.8 = (f32[16,3,512]{2,1,0:T(4,128)S(1)}, f32[16,512,512,3]{2,1,3,0:T(8,128)}) fusion(pred[512,512]{0,1:T(8,128)(4,1)S(1)} %iota_compare_fusion, bf16[16,512,128,1]{2,1,3,0:T(8,128)(2,1)} %bitcast.238, bf16[16,512,3,128]{3,1,2,0:T(8,128)(2,1)S(1)} %bitcast.230), kind=kOutput, calls=%fused_computation.11 | convolution fusion | flops 3258949632 | bytes 59080704 | tf_op jit(solution)/shard_map/bqkgd,bskd->bkgqs/dot_general | solution.py:52
  305.1 21.0 %fusion.7 = f32[16,3,512]{2,1,0:T(4,128)S(1)} fusion(f32[16,512,512,3]{2,1,3,0:T(8,128)} %get-tuple-element.22, f32[16,3,512]{2,1,0:T(4,128)S(1)} %get-tuple-element.21, pred[512,512]{0,1:T(8,128)(4,1)S(1)} %iota_compare_fusion), kind=kLoop, calls=%fused_computation.10 | loop fusion | flops 50307072 | bytes 50790400 | tf_op jit(solution)/shard_map/reduce_sum | solution.py:53
  326.1 23.6 %fusion.60 = bf16[16,512,1,128]{1,3,0,2:T(8,128)(2,1)} fusion(bf16[16,512,3,128]{3,1,2,0:T(8,128)(2,1)} %bitcast.246, f32[16,3,512]{2,1,0:T(4,128)S(1)} %fusion.7, f32[16,3,512]{2,1,0:T(4,128)S(1)} %get-tuple-element.21, f32[16,512,512,3]{2,1,3,0:T(8,128)} %get-tuple-element.22, pred[512,512]{0,1:T(8,128)(4,1)S(1)} %iota_compare_fusion), kind=kOutput, calls=%fused_computation.83 | convolution fusion | flops 3285188608 | bytes 59179008 | tf_op jit(solution)/shard_map/bkgqs,bqkgd->bskd/dot_general | solution.py:64
  349.7 4.5 copy.133
  354.2 5.9 all-to-all-start.7
  360.1 34.0 %fusion.2 = (f32[16,3,512]{2,1,0:T(4,128)S(1)}, bf16[16,512,512,3]{2,1,3,0:T(8,128)(2,1)}) fusion(f32[16,3,512]{2,1,0:T(4,128)S(1)} %fusion.7, f32[16,3,512]{2,1,0:T(4,128)S(1)} %get-tuple-element.21, f32[16,512,512,3]{2,1,3,0:T(8,128)} %get-tuple-element.22, pred[512,512]{0,1:T(8,128)(4,1)S(1)} %iota_compare_fusion, ...), kind=kOutput, calls=%fused_computation.4 | convolution fusion | flops 3321864192 | bytes 84443136 | tf_op jit(solution)/shard_map/bqkgd,bskd->bkgqs/dot_general | solution.py:61
  394.1 33.7 %fusion.13 = bf16[16,3,512,512]{2,3,1,0:T(8,128)(2,1)} fusion(bf16[16,512,512,3]{2,1,3,0:T(8,128)(2,1)} %get-tuple-element.24, f32[16,3,512]{2,1,0:T(4,128)S(1)} %get-tuple-element.23, f32[16,3,512]{2,1,0:T(4,128)S(1)} %fusion.7, f32[16,3,512]{2,1,0:T(4,128)S(1)} %get-tuple-element.21, f32[16,512,512,3]{2,1,3,0:T(8,128)} %get-tuple-element.22, ...), kind=kLoop, calls=%fused_computation.17 | loop fusion | flops 113246208 | bytes 101220352 | tf_op jit(solution)/shard_map/reshape.28
  427.7 15.4 fusion.59
  443.2 4.6 copy.127
  447.8 5.2 all-to-all-start.6
  453.0 14.5 convert_bitcast_fusion.3
  467.5 9.1 copy.120
  476.6 2.4 all-to-all-done.6
  478.9 5.7 all-to-all-start.5
  484.7 24.0 %convert_bitcast_fusion.5 = bf16[16,512,3,128]{1,3,2,0:T(8,128)(2,1)} fusion(bf16[16,512,128,1]{2,1,3,0:T(8,128)(2,1)S(1)} %bitcast.251, f32[16,3,512]{2,1,0:T(4,128)S(1)} %fusion.7, f32[16,3,512]{2,1,0:T(4,128)S(1)} %get-tuple-element.21, f32[16,512,512,3]{2,1,3,0:T(8,128)} %get-tuple-element.22, pred[512,512]{0,1:T(8,128)(4,1)S(1)} %iota_compare_fusion), kind=kOutput, calls=%fused_computation.62 | convolution fusion | flops 3287285760 | bytes 59179008 | tf_op jit(solution)/shard_map/bkgqs,bskd->bqkgd/dot_general | solution.py:55
  508.7 9.0 copy.112
  517.7 38.1 %all-to-all-done.5 = bf16[16,512,3,128]{3,0,2,1:T(8,128)(2,1)} async-done(((bf16[16,512,3,128]{3,0,2,1:T(8,128)(2,1)}), bf16[16,512,3,128]{3,0,2,1:T(8,128)(2,1)}, u32[]{:S(2)}, u32[]{:S(2)}) %all-to-all-start.5) | async-done | bytes 6291488 | tf_op jit(solution)/shard_map/all_to_all | solution.py:105
  555.8 5.7 all-to-all-start.3
  562.1 2.1 copy.134
  566.0 2.3 reshape.154
  570.9 5.3 copy.129
  576.2 5.1 reshape.159
  583.6 2.9 fusion.52
  586.5 4.4 copy.121
  590.9 6.3 convert_bitcast_fusion.1
  597.3 11.8 copy.123
  609.1 18.5 %copy.122 = f32[16,64,8,3,128]{4,3,2,1,0:T(4,128)} copy(f32[16,64,8,3,128]{4,1,2,3,0:T(8,128)} %convert_bitcast_fusion.1) | data formatting | bytes 25165824 | tf_op jit(solution)/shard_map/convert_element_type | solution.py:33
  627.6 5.1 all-to-all-done.3
  632.7 10.2 copy.114
  642.9 16.5 reshape.149
  659.4 12.1 broadcast_multiply_fusion
  671.5 20.1 %reshape.157 = f32[16,64,3072]{2,1,0:T(8,128)} reshape(f32[16,64,8,3,128]{4,3,2,1,0:T(4,128)} %copy.122) | data formatting | bytes 25165824 | tf_op jit(solution)/shard_map/convert_element_type | solution.py:33
  691.6 20.4 %slice_negate_fusion = (f32[16,64,24,64]{3,1,2,0:T(8,128)}, f32[16,64,24,64]{3,1,2,0:T(8,128)}) fusion(f32[16,64,24,128]{3,1,2,0:T(8,128)} %broadcast_multiply_fusion), kind=kLoop, calls=%fused_computation.49 | loop fusion | flops 1572864 | bytes 25165824 | tf_op jit(solution)/shard_map/neg | solution.py:14
  712.0 26.4 %convolution_bitcast_fusion.1 = f32[3072,3072]{1,0:T(8,128)} fusion(bf16[16,64,3072]{2,1,0:T(8,128)(2,1)S(1)} %bitcast.245, bf16[16,64,3072]{2,1,0:T(8,128)(2,1)} %param.13), kind=kOutput, calls=%fused_computation.23 | convolution fusion | flops 19327352832 | bytes 50331648 | tf_op jit(solution)/shard_map/bse,bsd->ed/dot_general | solution.py:100
  738.5 13.5 fusion.36
  752.0 44.6 %convolution_bitcast_fusion = f32[3072,5120]{1,0:T(8,128)} fusion(bf16[16,64,3072]{2,1,0:T(8,128)(2,1)} %param.7, f32[3072]{0:T(1024)S(1)} %copy-done.14, f32[16,64]{1,0:T(8,128)S(1)} %copy-done.13, bf16[16,64,1024]{2,1,0:T(8,128)(2,1)} %reshape.154, bf16[16,64,1024]{2,1,0:T(8,128)(2,1)S(1)} %copy-done.5, bf16[16,64,3072]{2,1,0:T(8,128)(2,1)} %fusion.36), kind=kOutput, calls=%fused_computation.12 | convolution fusion | flops 32256294912 | bytes 79708160 | tf_op jit(solution)/shard_map/bsd,bse->de/dot_general | solution.py:112
  796.7 46.0 %fusion.33 = (f32[3072]{0:T(1024)S(1)}, f32[16,64]{1,0:T(8,128)S(1)}, bf16[16,64,3072]{2,1,0:T(8,128)(2,1)}) fusion(bf16[16,64,3072]{2,1,0:T(8,128)(2,1)} %param.7, f32[16,64]{1,0:T(8,128)S(1)} %copy-done.13, f32[3072]{0:T(1024)S(1)} %copy-done.14, bf16[3072,5120]{1,0:T(8,128)(2,1)} %param.11, bf16[16,64,1024]{2,1,0:T(8,128)(2,1)} %reshape.154, ...), kind=kOutput, calls=%fused_computation.43 | convolution fusion | flops 32272019456 | bytes 54558720 | tf_op jit(solution)/shard_map/bse,de->bsd/dot_general | solution.py:113
  842.7 21.8 %psum.21 = f32[3072]{0:T(1024)} all-reduce(f32[3072]{0:T(1024)S(1)} %get-tuple-element.5), channel_id=1, replica_groups=mesh['dp'=2,'sp'=8] {'sp'}, use_global_device_ids=true, to_apply=%region_6.7 | all-reduce | flops 3072 | bytes 24576 | tf_op jit(solution)/shard_map/psum | solution.py:116
  864.5 11.4 fusion.30
  875.9 26.0 %fusion.35 = bf16[16,64,3072]{2,1,0:T(8,128)(2,1)} fusion(bf16[16,64,3072]{2,1,0:T(8,128)(2,1)} %param.7, bf16[16,64,3072]{2,1,0:T(8,128)(2,1)} %reshape.149, bf16[3072,3072]{1,0:T(8,128)(2,1)} %param.12), kind=kOutput, calls=%fused_computation.45 | convolution fusion | flops 19336790016 | bytes 37748736 | tf_op jit(solution)/shard_map/bse,ed->bsd/dot_general | solution.py:97
  901.9 857.5 %all-reduce.3.cloned.1.call-done = (f32[3072,5120]{1,0:T(8,128)}, f32[3072,3072]{1,0:T(8,128)}) async-done(((f32[3072,5120]{1,0:T(8,128)}, f32[3072,3072]{1,0:T(8,128)}), (f32[3072,5120]{1,0:T(8,128)}, f32[3072,3072]{1,0:T(8,128)})) %all-reduce.3.cloned.1.call-update) | async-done | bytes 100663312 | tf_op jit(solution)/shard_map/psum | solution.py:116
  1759.4 42.2 %copy.182 = f32[3072,5120]{1,0:T(8,128)} copy(f32[3072,5120]{1,0:T(8,128)} %get-tuple-element.31) | data formatting | bytes 125829120
  1801.5 27.9 %copy.183 = f32[3072,3072]{1,0:T(8,128)} copy(f32[3072,3072]{1,0:T(8,128)} %get-tuple-element.32) | data formatting | bytes 75497472
  (70 shorter events, 15.6 us)
Async XLA Ops:
  11.3 38.2 %copy-start.12 = (f32[16,64]{1,0:T(8,128)}, f32[16,64]{1,0:T(8,128)S(1)}, u32[]{:S(2)}) copy-start(f32[16,64]{1,0:T(8,128)S(1)} %add_rsqrt_fusion) | copy-start | bytes 12292
  49.5 4.0 copy-start.2
  53.5 10.8 copy-start.15
  53.5 13.7 copy-start.16
  58.2 32.0 %all-to-all-start = ((bf16[16,64,8,128]{3,1,0,2:T(8,128)(2,1)}), bf16[16,64,8,128]{3,1,0,2:T(8,128)(2,1)S(1)}, u32[]{:S(2)}, u32[]{:S(2)}) async-start(bf16[16,64,8,128]{3,1,0,2:T(8,128)(2,1)} %bitcast.242), calls=%async_computation | async-start | bytes 4194304 | tf_op jit(solution)/shard_map/all_to_all | solution.py:88
  64.3 5.0 copy-start.1
  67.5 76.8 %copy-start.8 = (f32[64,128]{1,0:T(8,128)}, f32[64,128]{1,0:T(8,128)S(1)}, u32[]{:S(2)}) copy-start(f32[64,128]{1,0:T(8,128)S(1)} %get-tuple-element.27) | copy-start | bytes 98308
  67.5 76.8 %copy-start.10 = (f32[64,128]{1,0:T(8,128)}, f32[64,128]{1,0:T(8,128)S(1)}, u32[]{:S(2)}) copy-start(f32[64,128]{1,0:T(8,128)S(1)} %get-tuple-element.26) | copy-start | bytes 98308
  90.3 34.9 %all-to-all-start.1 = ((bf16[16,64,8,128]{3,1,0,2:T(8,128)(2,1)}), bf16[16,64,8,128]{3,1,0,2:T(8,128)(2,1)}, u32[]{:S(2)}, u32[]{:S(2)}) async-start(bf16[16,64,8,128]{3,1,0,2:T(8,128)(2,1)} %copy.102), calls=%async_computation.1 | async-start | bytes 4194304 | tf_op jit(solution)/shard_map/all_to_all | solution.py:87
  125.1 75.9 %all-to-all-start.4 = ((bf16[16,64,24,128]{3,1,0,2:T(8,128)(2,1)}), bf16[16,64,24,128]{3,1,0,2:T(8,128)(2,1)}, u32[]{:S(2)}, u32[]{:S(2)}) async-start(bf16[16,64,24,128]{3,1,0,2:T(8,128)(2,1)} %bitcast.236), calls=%async_computation.4 | async-start | bytes 12582912 | tf_op jit(solution)/shard_map/all_to_all | solution.py:102
  201.0 77.1 %all-to-all-start.2 = ((bf16[16,64,24,128]{3,1,0,2:T(8,128)(2,1)}), bf16[16,64,24,128]{3,1,0,2:T(8,128)(2,1)}, u32[]{:S(2)}, u32[]{:S(2)}) async-start(bf16[16,64,24,128]{3,1,0,2:T(8,128)(2,1)} %copy.107), calls=%async_computation.2 | async-start | bytes 12582912 | tf_op jit(solution)/shard_map/all_to_all | solution.py:86
  282.4 22.6 %copy-start = (bf16[16,8,64,3,128]{4,2,1,3,0:T(8,128)(2,1)}, bf16[16,8,64,3,128]{4,2,1,3,0:T(8,128)(2,1)S(1)}, u32[]{:S(2)}) copy-start(bf16[16,8,64,3,128]{4,2,1,3,0:T(8,128)(2,1)S(1)} %copy.109) | copy-start | bytes 18874372
  326.0 34.0 %copy-start.6 = (bf16[16,64,8,128]{3,1,2,0:T(8,128)(2,1)S(1)}, bf16[16,64,8,128]{3,1,2,0:T(8,128)(2,1)}, u32[]{:S(2)}) copy-start(bf16[16,64,8,128]{3,1,2,0:T(8,128)(2,1)} %copy.98) | copy-start | bytes 6291460
  354.2 93.6 %all-to-all-start.7 = ((bf16[16,512,1,128]{3,0,2,1:T(8,128)(2,1)}), bf16[16,512,1,128]{3,0,2,1:T(8,128)(2,1)}, u32[]{:S(2)}, u32[]{:S(2)}) async-start(bf16[16,512,1,128]{3,0,2,1:T(8,128)(2,1)} %copy.133), calls=%async_computation.7 | async-start | bytes 4194304 | tf_op jit(solution)/shard_map/all_to_all | solution.py:107
  427.7 25.2 %copy-start.3 = (bf16[16,8,64,1,128]{4,2,1,0,3:T(8,128)(2,1)S(1)}, bf16[16,8,64,1,128]{4,2,1,0,3:T(8,128)(2,1)}, u32[]{:S(2)}) copy-start(bf16[16,8,64,1,128]{4,2,1,0,3:T(8,128)(2,1)} %copy.103) | copy-start | bytes 6291460
  447.8 31.2 %all-to-all-start.6 = ((bf16[16,512,1,128]{3,0,2,1:T(8,128)(2,1)}), bf16[16,512,1,128]{3,0,2,1:T(8,128)(2,1)}, u32[]{:S(2)}, u32[]{:S(2)}) async-start(bf16[16,512,1,128]{3,0,2,1:T(8,128)(2,1)} %copy.127), calls=%async_computation.6 | async-start | bytes 4194304 | tf_op jit(solution)/shard_map/all_to_all | solution.py:106
  467.4 17.2 copy-start.7
  478.9 76.9 %all-to-all-start.5 = ((bf16[16,512,3,128]{3,0,2,1:T(8,128)(2,1)}), bf16[16,512,3,128]{3,0,2,1:T(8,128)(2,1)}, u32[]{:S(2)}, u32[]{:S(2)}) async-start(bf16[16,512,3,128]{3,0,2,1:T(8,128)(2,1)} %copy.120), calls=%async_computation.5 | async-start | bytes 12582912 | tf_op jit(solution)/shard_map/all_to_all | solution.py:105
  508.7 53.0 %copy-start.11 = (f32[64,128]{1,0:T(8,128)S(1)}, f32[64,128]{1,0:T(8,128)}, u32[]{:S(2)}) copy-start(f32[64,128]{1,0:T(8,128)} %copy-done.10) | copy-start | bytes 98308
  555.8 76.9 %all-to-all-start.3 = ((bf16[16,512,3,128]{3,0,2,1:T(8,128)(2,1)}), bf16[16,512,3,128]{3,0,2,1:T(8,128)(2,1)}, u32[]{:S(2)}, u32[]{:S(2)}) async-start(bf16[16,512,3,128]{3,0,2,1:T(8,128)(2,1)} %copy.112), calls=%async_computation.3 | async-start | bytes 12582912 | tf_op jit(solution)/shard_map/all_to_all | solution.py:95
  561.5 1197.8 %all-reduce.3.cloned.1.call-start = ((), (), s32[]{:S(2)}) async-start(), calls=%async_computation.8 | async-start | bytes 201326592 | tf_op jit(solution)/shard_map/psum | solution.py:116
  570.4 10.9 copy-start.9
  581.3 2.3 copy-start.4
  671.5 40.5 %slice-start.3 = ((s8[6291456]{0:T(1024)(128)(4,1)}), s8[2097152]{0:T(1024)(128)(4,1)S(1)}, s32[]{:S(2)}) async-start(s8[6291456]{0:T(1024)(128)(4,1)} %bitcast.244), calls=%async_computation.12 | async-start | bytes 4194304
  691.6 20.4 %slice-start.4 = ((s8[6291456]{0:T(1024)(128)(4,1)}), s8[4194304]{0:T(1024)(128)(4,1)S(1)}, s32[]{:S(2)}) async-start(s8[6291456]{0:T(1024)(128)(4,1)} %bitcast.244), calls=%async_computation.13 | async-start | bytes 8388608
  691.6 46.9 %slice-start = ((s8[12582912]{0:T(1024)(128)(4,1)}), s8[4194304]{0:T(1024)(128)(4,1)S(1)}, s32[]{:S(2)}) async-start(s8[12582912]{0:T(1024)(128)(4,1)} %bitcast.233), calls=%async_computation.9 | async-start | bytes 8388608
  691.6 46.9 %slice-start.1 = ((s8[12582912]{0:T(1024)(128)(4,1)}), s8[4194304]{0:T(1024)(128)(4,1)S(1)}, s32[]{:S(2)}) async-start(s8[12582912]{0:T(1024)(128)(4,1)} %bitcast.233), calls=%async_computation.10 | async-start | bytes 8388608
  712.0 26.5 %slice-start.2 = ((s8[12582912]{0:T(1024)(128)(4,1)}), s8[4194304]{0:T(1024)(128)(4,1)S(1)}, s32[]{:S(2)}) async-start(s8[12582912]{0:T(1024)(128)(4,1)} %bitcast.233), calls=%async_computation.11 | async-start | bytes 8388608
  738.5 13.5 copy-start.5
  738.5 13.5 copy-start.13
  738.5 13.5 copy-start.14
Sparse Core Ops, SparseCore 0:
  796.8 962.5 all-reduce.2
where the time goes:
time: 1850 us; the launch traced here: 1840 us
  waiting for transfers between devices  1020 us (55%)
  matrix products  340 us (18%)
  local copies, waits for them, and re-layouts  234 us (13%)
  other arithmetic  160 us (9%)
  starting transfers between devices  45.5 us (2%)
  blocking collectives  21.8 us (1%)
    psum x1, waiting for transfers between devices, block_body(): lax.psum(grad_wqkv, 'sp')  857 us
    unnamed x48, local copies, waits for them, and re-layouts  74.4 us
    convert_element_type x5, local copies, waits for them, and re-layouts, rope_back(): grad_wide = grad_vals.astype(jnp.float32)  60.8 us
    all_to_all x1, waiting for transfers between devices, block_body(): query_heads = lax.all_to_all(query_rot, 'sp', 2, 1, tiled=True)  58.4 us
    dot_general x1, matrix products, block_body(): jnp.einsum('bse,de->bsd', grad_qkv, w_qkv, preferred_element_type=jnp.flo...  46 us
    dot_general x1, matrix products, block_body(): jnp.einsum('bsd,bse->de', normed, grad_qkv, preferred_element_type=jnp.fl...  44.6 us
    all_to_all x1, waiting for transfers between devices, block_body(): lax.all_to_all(grad_attn.reshape(batch_size, seq_local, num_heads, head_d...  40.8 us
    dot_general x1, matrix products, block_body(): jnp.einsum('bsd,de->bse', normed, w_qkv, preferred_element_type=jnp.float32)  38.2 us
  transfers between devices with their start and end apart: 9, of which 7 were waited for; matrix products, arithmetic and copies ran while one was open for 20% of the time, Pallas kernels for 0%

commit v1 on v0

v1 whole, which is shorter than its diff:
```python
import functools
import math
import jax
import jax.numpy as jnp
from jax import lax
from jax.experimental import pallas as pl
from jax.experimental.pallas import tpu as pltpu
from jax.sharding import PartitionSpec as P

NORM_EPS = 1e-5
ROPE_BASE = 10000.0
ROPE_SCALE = math.sqrt(1.0 + math.log(32.0) / math.log(4096.0))
F32 = jnp.float32
BF16 = jnp.bfloat16
VMEM_LIMIT = 62 * 1024 * 1024
QB = 128


def rope_tables(positions, long_factor):
    head_dim = 2 * long_factor.shape[0]
    exponents = jnp.arange(0, head_dim, 2).astype(F32) / head_dim
    inv_freq = 1.0 / (long_factor * ROPE_BASE ** exponents)
    angles = positions.astype(F32)[..., None] * inv_freq
    cos_half = jnp.cos(angles) * ROPE_SCALE
    sin_half = jnp.sin(angles) * ROPE_SCALE
    return jnp.concatenate([cos_half, cos_half], axis=-1), jnp.concatenate([-sin_half, sin_half], axis=-1)


def norm_forward(hidden, norm_weight):
    hidden_wide = hidden.astype(F32)
    inv_rms = lax.rsqrt(jnp.mean(hidden_wide * hidden_wide, axis=-1, keepdims=True) + NORM_EPS)
    unit_hidden = hidden_wide * inv_rms
    return hidden_wide, inv_rms, unit_hidden, (unit_hidden * norm_weight).astype(BF16)


def dot_nn(a, b):
    return lax.dot_general(a, b, (((1,), (0,)), ((), ())), preferred_element_type=F32)


def dot_nt(a, b):
    return lax.dot_general(a, b, (((1,), (1,)), ((), ())), preferred_element_type=F32)


def dot_tn(a, b):
    return lax.dot_general(a, b, (((0,), (0,)), ((), ())), preferred_element_type=F32)


def attend_kernel(slots, group, hd, r_ref, dy_ref, wq_ref, wo_ref, cos_ref, sin_ref, o_ref, dqkv_ref,
                  qkv_s, do_s, qs, dos, ks, ps, dss):
    ranks, _, _, tl, dim = r_ref.shape
    seq = ranks * tl
    q_cols = slots * group * hd
    k_cols = slots * hd
    nblk = seq // QB
    rpb = QB // tl
    rows_blk = group * QB
    score_scale = hd ** -0.5
    exp_scale = score_scale * math.log2(math.e)

    r = r_ref[...].reshape(seq, dim)
    qkv_s[...] = dot_nn(r, wq_ref[...]).astype(BF16)
    dy = dy_ref[...].reshape(seq, dim)
    do_s[...] = dot_nn(dy, wo_ref[...]).astype(BF16)

    row_ids = lax.broadcasted_iota(jnp.int32, (rows_blk, QB), 0) % QB
    col_ids = lax.broadcasted_iota(jnp.int32, (rows_blk, QB), 1)
    causal = row_ids >= col_ids

    def rope(vals, rows):
        wide = vals.astype(F32)
        return (wide * cos_ref[rows] + pltpu.roll(wide, hd // 2, 1) * sin_ref[rows]).astype(BF16)

    def rope_back(vals, rows):
        wide = vals.astype(BF16).astype(F32)
        return (wide * cos_ref[rows] - pltpu.roll(wide, hd // 2, 1) * sin_ref[rows]).astype(BF16)

    def one_slot(slot, carry):
        q_at = [pl.ds(pl.multiple_of((slot * group + g) * hd, hd), hd) for g in range(group)]
        k_at = pl.ds(pl.multiple_of(q_cols + slot * hd, hd), hd)
        v_at = pl.ds(pl.multiple_of(q_cols + k_cols + slot * hd, hd), hd)
        ks[...] = rope(qkv_s[:, k_at], pl.ds(0, seq))
        for g in range(group):
            for blk in range(nblk):
                rows = pl.ds(blk * QB, QB)
                dst = pl.ds(blk * rows_blk + g * QB, QB)
                qs[dst] = rope(qkv_s[rows, q_at[g]], rows)
                dos[dst] = do_s[rows, q_at[g]]
        for blk in range(nblk):
            span = (blk + 1) * QB
            rows = pl.ds(blk * rows_blk, rows_blk)
            keys = ks[:span]
            vals = qkv_s[:span, v_at]
            scores = dot_nt(qs[rows], keys)
            diag = jnp.where(causal, scores[:, span - QB:], -jnp.inf)
            scores = diag if blk == 0 else jnp.concatenate([scores[:, :span - QB], diag], axis=1)
            top = jnp.max(scores, axis=1, keepdims=True)
            ex = jnp.exp2((scores - top) * exp_scale)
            probs = ex * (1.0 / jnp.sum(ex, axis=1, keepdims=True))
            low = probs.astype(BF16)
            ps[rows, :span] = low
            outs = dot_nn(low, vals).astype(BF16)
            gp = dot_nt(dos[rows], vals).astype(BF16).astype(F32)
            rdot = jnp.sum(gp * probs, axis=1, keepdims=True)
            gs = (probs * (gp - rdot) * score_scale).astype(BF16)
            dss[rows, :span] = gs
            gq = dot_nn(gs, keys)
            for g in range(group):
                part = outs[g * QB:(g + 1) * QB].reshape(rpb, tl, hd)
                o_ref[blk * rpb:(blk + 1) * rpb, 0, :, q_at[g]] = part
                back = rope_back(gq[g * QB:(g + 1) * QB], pl.ds(blk * QB, QB)).reshape(rpb, tl, hd)
                dqkv_ref[blk * rpb:(blk + 1) * rpb, 0, :, q_at[g]] = back
        for blk in range(nblk):
            rows = pl.ds(blk * rows_blk, (nblk - blk) * rows_blk)
            cols = slice(blk * QB, (blk + 1) * QB)
            gv = dot_tn(ps[rows, cols], dos[rows]).astype(BF16).reshape(rpb, tl, hd)
            gk = rope_back(dot_tn(dss[rows, cols], qs[rows]), pl.ds(blk * QB, QB)).reshape(rpb, tl, hd)
            dqkv_ref[blk * rpb:(blk + 1) * rpb, 0, :, v_at] = gv
            dqkv_ref[blk * rpb:(blk + 1) * rpb, 0, :, k_at] = gk
        return carry

    lax.fori_loop(0, slots, one_slot, 0)


def attend_chunk(gathered, wq_own, wo_own_t, cos_full, sin_full, slots):
    ranks, _, nb, tl, dim = gathered.shape
    seq, hd = cos_full.shape
    q_cols = wo_own_t.shape[1]
    cols = wq_own.shape[1]
    group = q_cols // (slots * hd)
    flops = 2 * nb * seq * dim * (cols + q_cols) + 2 * 6 * nb * slots * group * seq * seq * hd
    token = lambda which: pl.BlockSpec((ranks, 1, 1, tl, dim), lambda b: (0, which, b, 0, 0))
    whole = lambda shape: pl.BlockSpec(shape, lambda b: (0, 0), pipeline_mode=pl.Buffered(1))
    return pl.pallas_call(
        functools.partial(attend_kernel, slots, group, hd),
        grid=(nb,),
        in_specs=[token(0), token(1), whole(wq_own.shape), whole(wo_own_t.shape), whole((seq, hd)), whole((seq, hd))],
        out_specs=[pl.BlockSpec((ranks, 1, tl, q_cols), lambda b: (0, b, 0, 0)),
                   pl.BlockSpec((ranks, 1, tl, cols), lambda b: (0, b, 0, 0))],
        out_shape=[jax.ShapeDtypeStruct((ranks, nb, tl, q_cols), BF16),
                   jax.ShapeDtypeStruct((ranks, nb, tl, cols), BF16)],
        scratch_shapes=[pltpu.VMEM((seq, cols), BF16), pltpu.VMEM((seq, q_cols), BF16),
                        pltpu.VMEM((group * seq, hd), BF16), pltpu.VMEM((group * seq, hd), BF16),
                        pltpu.VMEM((seq, hd), BF16),
                        pltpu.VMEM((group * seq, seq), BF16), pltpu.VMEM((group * seq, seq), BF16)],
        compiler_params=pltpu.CompilerParams(dimension_semantics=("arbitrary",), vmem_limit_bytes=VMEM_LIMIT),
        cost_estimate=pl.CostEstimate(flops=flops, bytes_accessed=2 * nb * seq * (2 * dim + cols + q_cols),
                                      transcendentals=nb * slots * group * seq * seq),
        name="attend",
    )(gathered, gathered, wq_own, wo_own_t, cos_full, sin_full)


def weight_grad_kernel(bounds, which, pieces, n_out, *refs):
    chunks = len(bounds) - 1
    lefts, rights = refs[:chunks], refs[chunks:2 * chunks]
    outs = refs[len(refs) - 4 - n_out:len(refs) - 4]
    lbuf, rbuf, acc, sems = refs[len(refs) - 4:]
    total = bounds[-1]

    def fetch(step, slot, go):
        for c in range(chunks):
            def pair():
                at = step - bounds[c]
                out = []
                for side, (ref, buf, sel) in enumerate(((lefts[c], lbuf, which[0]), (rights[c], rbuf, which[1]))):
                    kind, val, width = sel
                    src = ref.at[:, val, at] if kind == "plane" else ref.at[:, at, :, pl.ds(val, width)]
                    out.append(pltpu.make_async_copy(src, buf.at[slot], sems.at[side, slot]))
                return out
            if go:
                @pl.when((step >= bounds[c]) & (step < bounds[c + 1]))
                def _():
                    for copy in pair():
                        copy.start()
            elif c == 0:
                for side, buf in ((0, lbuf), (1, rbuf)):
                    pltpu.make_async_copy(buf.at[slot], buf.at[slot], sems.at[side, slot]).wait()

    fetch(0, 0, True)
    acc[...] = jnp.zeros_like(acc)

    def body(step, carry):
        slot = lax.rem(step, 2)

        @pl.when(step + 1 < total)
        def _():
            fetch(step + 1, 1 - slot, True)
        fetch(step, slot, False)
        left = lbuf[slot]
        right = rbuf[slot]
        acc[...] += dot_tn(left.reshape(-1, left.shape[-1]), right.reshape(-1, right.shape[-1]))
        return carry

    lax.fori_loop(0, total, body, 0)
    copies = []
    for n, (out, src_rows, src_cols, dst_rows, dst_cols) in enumerate(pieces):
        copy = pltpu.make_async_copy(acc.at[pl.ds(*src_rows), pl.ds(*src_cols)],
                                     outs[out].at[pl.ds(*dst_rows()), pl.ds(*dst_cols())], sems.at[2, n])
        copy.start()
        copies.append(copy)
    for copy in copies:
        copy.wait()


def weight_grad(lefts, rights, which, bounds, acc_shape, pieces, out_structs, carried, name):
    chunks = len(lefts)
    any_spec = pl.BlockSpec(memory_space=pl.ANY)

    def buf(ref, sel):
        return (2, ref.shape[0], ref.shape[-2], ref.shape[-1] if sel[0] == "plane" else sel[2])
    operands = list(lefts) + list(rights) + ([] if carried is None else [carried])
    rows = bounds[-1] * lefts[0].shape[0] * lefts[0].shape[-2]
    return pl.pallas_call(
        functools.partial(weight_grad_kernel, bounds, which, pieces, len(out_structs)),
        in_specs=[any_spec] * len(operands),
        out_specs=[any_spec] * len(out_structs),
        out_shape=out_structs,
        scratch_shapes=[pltpu.VMEM(buf(lefts[0], which[0]), BF16), pltpu.VMEM(buf(rights[0], which[1]), BF16),
                        pltpu.VMEM(acc_shape, F32), pltpu.SemaphoreType.DMA((3, max(2, len(pieces))))],
        input_output_aliases={} if carried is None else {2 * chunks: 0},
        compiler_params=pltpu.CompilerParams(vmem_limit_bytes=VMEM_LIMIT),
        cost_estimate=pl.CostEstimate(flops=2 * rows * acc_shape[0] * acc_shape[1],
                                      bytes_accessed=2 * rows * (acc_shape[0] + acc_shape[1]) + 8 * acc_shape[0] * acc_shape[1],
                                      transcendentals=0),
        name=name,
    )(*operands)


def place_kernel(src_ref, full_ref, out_ref):
    del full_ref
    out_ref[...] = src_ref[...]


def place(full, src, block, grid, src_map, dst_map, name):
    return pl.pallas_call(
        place_kernel,
        grid=grid,
        in_specs=[pl.BlockSpec(block, src_map), pl.BlockSpec(memory_space=pl.ANY)],
        out_specs=pl.BlockSpec(block, dst_map),
        out_shape=jax.ShapeDtypeStruct(full.shape, full.dtype),
        input_output_aliases={1: 0},
        compiler_params=pltpu.CompilerParams(vmem_limit_bytes=VMEM_LIMIT),
        cost_estimate=pl.CostEstimate(flops=src.size, bytes_accessed=8 * src.size, transcendentals=0),
        name=name,
    )(src, full)


def block_body(ranks, hidden, positions, long_factor, norm_weight, w_qkv, w_out, grad_out):
    batch, tl, dim = hidden.shape
    hd = 2 * long_factor.shape[0]
    q_dim = w_out.shape[0]
    kv_dim = (w_qkv.shape[1] - q_dim) // 2
    group = q_dim // kv_dim
    me = lax.axis_index('sp')
    core = lax.rem(me, 2)
    pair = [(i, i ^ 1) for i in range(ranks)]
    qh, kh = q_dim // 2, kv_dim // 2
    slots = kh // hd

    hidden_wide, inv_rms, unit_hidden, normed = norm_forward(hidden, norm_weight)
    sizes = [1, 1] + [2] * ((batch - 2) // 2)
    bounds = [sum(sizes[:i]) for i in range(len(sizes) + 1)]
    both = jnp.stack([normed, grad_out])
    gathered = [lax.all_gather(both[:, bounds[i]:bounds[i + 1]], 'sp') for i in range(len(sizes))]
    pos_all = lax.all_gather(positions, 'sp', tiled=True)
    cos_full, sin_full = rope_tables(pos_all, long_factor)

    wq_own = jnp.concatenate([lax.dynamic_slice_in_dim(w_qkv, core * qh, qh, 1),
                              lax.dynamic_slice_in_dim(w_qkv, q_dim + core * kh, kh, 1),
                              lax.dynamic_slice_in_dim(w_qkv, q_dim + kv_dim + core * kh, kh, 1)], axis=1)
    wo_own_t = lax.dynamic_slice_in_dim(w_out, core * qh, qh, 0).T

    o_parts, g_parts = [], []
    for chunk in gathered:
        o_c, g_c = attend_chunk(chunk, wq_own, wo_own_t, cos_full, sin_full, slots)
        o_parts.append(o_c)
        g_parts.append(g_c)

    def tokens_of(parts, who):
        return jnp.concatenate([lax.dynamic_index_in_dim(p, who, 0, keepdims=False) for p in parts], axis=0)

    other = me + 1 - 2 * core
    o_mine, g_mine = tokens_of(o_parts, me), tokens_of(g_parts, me)
    o_pair = lax.ppermute(tokens_of(o_parts, other), 'sp', pair)
    g_pair = lax.ppermute(tokens_of(g_parts, other), 'sp', pair)

    def in_order(mine, peer, widths):
        lo = jnp.where(core == 0, mine, peer)
        hi = jnp.where(core == 0, peer, mine)
        cols, at = [], 0
        for w in widths:
            cols += [lo[..., at:at + w], hi[..., at:at + w]]
            at += w
        return jnp.concatenate(cols, axis=-1)

    attn_flat = in_order(o_mine, o_pair, [qh])
    grad_qkv = in_order(g_mine, g_pair, [qh, kh, kh])

    half = (qh + 2 * kh) // 2
    q_left = qh - half
    core_id = lambda: lax.rem(lax.axis_index('sp'), 2)
    full_rows = lambda n: (lambda: (0, n))
    at = lambda base, step, width: (lambda: (pl.multiple_of(base + core_id() * step, 128), width))
    full_struct = jax.ShapeDtypeStruct((dim, q_dim + 2 * kv_dim), F32)
    send_struct = jax.ShapeDtypeStruct((dim, half), F32)
    all_rows = (0, dim)
    dwq, send_a = weight_grad(
        gathered, g_parts, (("plane", 0, dim), ("cols", 0, half)), bounds, (dim, half),
        [(0, all_rows, (0, half), full_rows(dim), at(0, qh, half)), (1, all_rows, (0, half), full_rows(dim), full_rows(half))],
        [full_struct, send_struct], None, "wgrad_qkv_a")
    dwq, send_b = weight_grad(
        gathered, g_parts, (("plane", 0, dim), ("cols", half, half)), bounds, (dim, half),
        [(0, all_rows, (0, q_left), full_rows(dim), at(half, qh, q_left)),
         (0, all_rows, (q_left, kh), full_rows(dim), at(q_dim, kh, kh)),
         (0, all_rows, (q_left + kh, kh), full_rows(dim), at(q_dim + kv_dim, kh, kh)),
         (1, all_rows, (0, half), full_rows(dim), full_rows(half))],
        [full_struct, send_struct], dwq, "wgrad_qkv_b")
    dwo, send_o = weight_grad(
        o_parts, gathered, (("cols", 0, qh), ("plane", 1, dim)), bounds, (qh, dim),
        [(0, (0, qh), (0, dim), at(0, qh, qh), full_rows(dim)), (1, (0, qh), (0, dim), full_rows(qh), full_rows(dim))],
        [jax.ShapeDtypeStruct((q_dim, dim), F32), jax.ShapeDtypeStruct((qh, dim), F32)], None, "wgrad_out")
    recv_a = lax.ppermute(send_a, 'sp', pair)
    recv_b = lax.ppermute(send_b, 'sp', pair)
    recv_o = lax.ppermute(send_o, 'sp', pair)

    mixed_out = jnp.einsum('bse,ed->bsd', attn_flat, w_out, preferred_element_type=F32)
    out_hidden = (hidden_wide + mixed_out).astype(BF16)
    grad_normed = jnp.einsum('bse,de->bsd', grad_qkv, w_qkv, preferred_element_type=F32).astype(BF16)
    grad_norm = jnp.sum(grad_normed * unit_hidden, axis=(0, 1))
    grad_unit = grad_normed * norm_weight
    grad_inner = inv_rms * (grad_unit - unit_hidden * jnp.mean(grad_unit * unit_hidden, axis=-1, keepdims=True))
    grad_hidden = (grad_out.astype(F32) + grad_inner).astype(BF16)
    hop = 1
    while hop < ranks:
        grad_norm = grad_norm + lax.ppermute(grad_norm, 'sp', [(i, i ^ hop) for i in range(ranks)])
        hop *= 2

    peer = lambda: 1 - core_id()
    tile = 256
    qt, kt, ht = qh // tile, kh // tile, half // tile
    rows_b = dim // 2

    def place_cols(full, recv, first, name):
        def dst(i, j):
            at_col = first + j
            return i, jnp.where(at_col < qt, peer() * qt + at_col,
                                jnp.where(at_col < qt + kt, q_dim // tile + peer() * kt + at_col - qt,
                                          (q_dim + kv_dim) // tile + peer() * kt + at_col - qt - kt))
        return place(full, recv, (rows_b, tile), (2, ht), lambda i, j: (i, j), dst, name)
    dwq = place_cols(dwq, recv_a, 0, "place_qkv_a")
    dwq = place_cols(dwq, recv_b, ht, "place_qkv_b")
    dwo = place(dwo, recv_o, (tile, dim), (qh // tile,), lambda i: (i, 0), lambda i: (peer() * qt + i, 0), "place_out")
    return out_hidden, grad_hidden, grad_norm, dwq, dwo


def solution(mesh):
    token_spec = P('dp', 'sp', None)
    return jax.shard_map(functools.partial(block_body, mesh.shape['sp']), mesh=mesh,
                         in_specs=(token_spec, P(('dp', 'sp')), P(), P(), P(), P(), token_spec),
                         out_specs=(token_spec, token_spec, P('dp'), P('dp', None), P('dp', None)),
                         check_vma=False)
```

time: 1850 us -> 1110 us (0.60)
  waiting for transfers between devices: 1020 us -> 7.26 us
  Pallas kernels: 0 us -> 856 us
  matrix products: 340 us -> 68.1 us
  local copies, waits for them, and re-layouts: 234 us -> 88.5 us
  other arithmetic: 160 us -> 55.4 us
  starting transfers between devices: 45.5 us -> 4.19 us
    psum x1 -> x0, waiting for transfers between devices: 857 us -> none  [block_body(): lax.psum(grad_wqkv, 'sp')]
    pallas_call x0 -> x15, Pallas kernels: none -> 856 us  [the longest x9 546 us: attend_chunk(): pl.pallas_call(functools.partial(attend_kernel, slots, group, hd), grid=(...]
    dot_general x12 -> x2, matrix products: 340 us -> 68.1 us  [the longest x1 42.4 us: block_body(): jnp.einsum('bse,de->bsd', grad_qkv, w_qkv, preferred_element_type=F32)]
    all_to_all x8 -> x0, waiting for transfers between devices: 163 us -> none  [the longest x1 58.4 us: block_body(): query_heads = lax.all_to_all(query_rot, 'sp', 2, 1, tiled=True)]
    convert_element_type x10 -> x0, local copies, waits for them, and re-layouts: 78.5 us -> none  [the longest x5 60.8 us: rope_back(): grad_wide = grad_vals.astype(jnp.float32)]
    convert_element_type x9 -> x2, other arithmetic: 51.9 us -> 5.51 us  [the longest x1 5.51 us: block_body(): grad_hidden = (grad_out.astype(F32) + grad_inner).astype(BF16)]
    all_to_all x8 -> x0, starting transfers between devices: 45.3 us -> none  [the longest x1 6.1 us: block_body(): query_heads = lax.all_to_all(query_rot, 'sp', 2, 1, tiled=True)]
    reshape x6 -> x0, local copies, waits for them, and re-layouts: 43.3 us -> none  [the longest x1 16.5 us: block_body(): attn_flat = attn_back.reshape(batch_size, seq_local, query_dim)]
  transfers between devices with their start and end apart: 9 -> 17, of which waited for: 7 -> 1; matrix products, arithmetic and copies ran while one was open for 20% -> 17% of each run, Pallas kernels for 0% -> 61%
where the time goes in v1:
time: 1110 us; the launch traced here: 1100 us
  Pallas kernels  856 us (77%)
  local copies, waits for them, and re-layouts  88.5 us (8%)
  matrix products  68.1 us (6%)
  other arithmetic  55.4 us (5%)
  between operations  15.2 us (1%)
    pallas_call x9, Pallas kernels, attend_chunk(): pl.pallas_call(functools.partial(attend_kernel, slots, group, hd), grid=(...  546 us
    pallas_call x3, Pallas kernels, weight_grad(): pl.pallas_call(functools.partial(weight_grad_kernel, bounds, which, piece...  267 us
    unnamed x61, local copies, waits for them, and re-layouts  61.4 us
    dot_general x1, matrix products, block_body(): jnp.einsum('bse,de->bsd', grad_qkv, w_qkv, preferred_element_type=F32)  42.4 us
    pallas_call x3, Pallas kernels, place(): pl.pallas_call(place_kernel, grid=grid, in_specs=[pl.BlockSpec(block, src...  42.1 us
    dot_general x1, matrix products, block_body(): jnp.einsum('bse,ed->bsd', attn_flat, w_out, preferred_element_type=F32)  25.7 us
  transfers between devices with their start and end apart: 17, of which 1 were waited for; matrix products, arithmetic and copies ran while one was open for 17% of the time, Pallas kernels for 61%

profile of v1, /device:TPU:113, one launch (start us, length us, event | category | flops | bytes accessed | tf_op | source)
XLA Modules:
  0.0 1103.5 jit_solution(14007293770181150076)
XLA Ops:
  7.3 4.2 fusion.15
  11.9 5.5 fusion.17
  17.3 2.5 pad_maximum_fusion.8
  19.9 0.7 all-gather.21.cloned.1.call-update
  20.7 7.7 pad_maximum_fusion.1
  30.5 0.7 all-gather.31.cloned.1.call-update
  31.3 0.7 all-gather.33.cloned.1.call-update
  32.1 0.7 all-gather.35.cloned.1.call-update
  32.9 8.3 constant_dynamic-slice_fusion
  41.1 12.7 %copy.18 = bf16[1536,3072]{0,1:T(8,128)(2,1)} copy(bf16[1536,3072]{1,0:T(8,128)(2,1)} %constant_dynamic-slice_fusion) | data formatting | bytes 18874368
  53.9 0.6 dynamic-slice
  55.4 9.0 all-reduce
  64.5 8.2 constant_dynamic-slice_fusion.3
  72.6 4.9 constant_dynamic-slice_fusion.2
  77.6 1.8 fusion.30
  79.4 11.9 %pad_maximum_fusion.wq_ref = bf16[3072,2560]{1,0:T(8,128)(2,1)} fusion(bf16[3072,512]{1,0:T(8,128)(2,1)} %get-tuple-element.56, bf16[3072,512]{1,0:T(8,128)(2,1)S(1)} %get-tuple-element.55, bf16[3072,1536]{1,0:T(8,128)(2,1)} %constant_dynamic-slice_fusion.3), kind=kLoop, calls=%fused_computation.11 | loop fusion | flops 47185920 | bytes 31457280 | tf_op jit(solution)/shard_map/concatenate | solution.py:267
  91.3 1.0 pad_maximum_fusion.10
  92.3 39.3 %attend.9 = (bf16[8,1,64,1536]{3,2,1,0:T(8,128)(2,1)}, bf16[8,1,64,2560]{3,2,1,0:T(8,128)(2,1)}) custom-call(bf16[8,2,1,64,3072]{4,3,2,1,0:T(8,128)(2,1)} %bitcast.151, bf16[8,2,1,64,3072]{4,3,2,1,0:T(8,128)(2,1)} %bitcast.152, bf16[3072,2560]{1,0:T(8,128)(2,1)} %pad_maximum_fusion.wq_ref, bf16[3072,1536]{1,0:T(8,128)(2,1)} %bitcast.107, ...), custom_call_target="tpu_custom_call" | custom-call | flops 17716740096 | bytes 10485760 | tf_op jit(solution)/shard_map/attend/pallas_call | solution.py:133
  131.6 1.8 bitcast_dynamic-update-slice_fusion.35
  133.4 38.7 %attend.10 = (bf16[8,1,64,1536]{3,2,1,0:T(8,128)(2,1)}, bf16[8,1,64,2560]{3,2,1,0:T(8,128)(2,1)}) custom-call(bf16[8,2,1,64,3072]{4,3,2,1,0:T(8,128)(2,1)} %bitcast.156, bf16[8,2,1,64,3072]{4,3,2,1,0:T(8,128)(2,1)} %bitcast.157, bf16[3072,2560]{1,0:T(8,128)(2,1)} %pad_maximum_fusion.wq_ref, bf16[3072,1536]{1,0:T(8,128)(2,1)} %bitcast.108, ...), custom_call_target="tpu_custom_call" | custom-call | flops 17716740096 | bytes 10485760 | tf_op jit(solution)/shard_map/attend/pallas_call | solution.py:133
  172.1 1.8 bitcast_dynamic-update-slice_fusion.34
  173.9 2.0 bitcast_dynamic-update-slice_fusion.29
  175.9 2.0 bitcast_dynamic-update-slice_fusion.28
  177.9 66.9 %attend.11 = (bf16[8,2,64,1536]{3,2,1,0:T(8,128)(2,1)}, bf16[8,2,64,2560]{3,2,1,0:T(8,128)(2,1)}) custom-call(bf16[8,2,2,64,3072]{4,3,2,1,0:T(8,128)(2,1)} %bitcast.116, bf16[8,2,2,64,3072]{4,3,2,1,0:T(8,128)(2,1)} %bitcast.117, bf16[3072,2560]{1,0:T(8,128)(2,1)} %pad_maximum_fusion.wq_ref, bf16[3072,1536]{1,0:T(8,128)(2,1)} %bitcast.109, ...), custom_call_target="tpu_custom_call" | custom-call | flops 35433480192 | bytes 20971520 | tf_op jit(solution)/shard_map/attend/pallas_call | solution.py:133
  244.8 66.8 %attend.12 = (bf16[8,2,64,1536]{3,2,1,0:T(8,128)(2,1)}, bf16[8,2,64,2560]{3,2,1,0:T(8,128)(2,1)}) custom-call(bf16[8,2,2,64,3072]{4,3,2,1,0:T(8,128)(2,1)} %bitcast.121, bf16[8,2,2,64,3072]{4,3,2,1,0:T(8,128)(2,1)} %bitcast.122, bf16[3072,2560]{1,0:T(8,128)(2,1)} %pad_maximum_fusion.wq_ref, bf16[3072,1536]{1,0:T(8,128)(2,1)} %bitcast.110, ...), custom_call_target="tpu_custom_call" | custom-call | flops 35433480192 | bytes 20971520 | tf_op jit(solution)/shard_map/attend/pallas_call | solution.py:133
  311.6 66.7 %attend.13 = (bf16[8,2,64,1536]{3,2,1,0:T(8,128)(2,1)}, bf16[8,2,64,2560]{3,2,1,0:T(8,128)(2,1)}) custom-call(bf16[8,2,2,64,3072]{4,3,2,1,0:T(8,128)(2,1)} %bitcast.126, bf16[8,2,2,64,3072]{4,3,2,1,0:T(8,128)(2,1)} %bitcast.127, bf16[3072,2560]{1,0:T(8,128)(2,1)} %pad_maximum_fusion.wq_ref, bf16[3072,1536]{1,0:T(8,128)(2,1)} %bitcast.111, ...), custom_call_target="tpu_custom_call" | custom-call | flops 35433480192 | bytes 20971520 | tf_op jit(solution)/shard_map/attend/pallas_call | solution.py:133
  378.3 67.1 %attend.14 = (bf16[8,2,64,1536]{3,2,1,0:T(8,128)(2,1)}, bf16[8,2,64,2560]{3,2,1,0:T(8,128)(2,1)}) custom-call(bf16[8,2,2,64,3072]{4,3,2,1,0:T(8,128)(2,1)} %bitcast.131, bf16[8,2,2,64,3072]{4,3,2,1,0:T(8,128)(2,1)} %bitcast.132, bf16[3072,2560]{1,0:T(8,128)(2,1)} %pad_maximum_fusion.wq_ref, bf16[3072,1536]{1,0:T(8,128)(2,1)} %bitcast.112, ...), custom_call_target="tpu_custom_call" | custom-call | flops 35433480192 | bytes 20971520 | tf_op jit(solution)/shard_map/attend/pallas_call | solution.py:133
  445.4 66.9 %attend.15 = (bf16[8,2,64,1536]{3,2,1,0:T(8,128)(2,1)}, bf16[8,2,64,2560]{3,2,1,0:T(8,128)(2,1)}) custom-call(bf16[8,2,2,64,3072]{4,3,2,1,0:T(8,128)(2,1)} %bitcast.136, bf16[8,2,2,64,3072]{4,3,2,1,0:T(8,128)(2,1)} %bitcast.137, bf16[3072,2560]{1,0:T(8,128)(2,1)} %pad_maximum_fusion.wq_ref, bf16[3072,1536]{1,0:T(8,128)(2,1)} %bitcast.113, ...), custom_call_target="tpu_custom_call" | custom-call | flops 35433480192 | bytes 20971520 | tf_op jit(solution)/shard_map/attend/pallas_call | solution.py:133
  512.3 66.7 %attend.16 = (bf16[8,2,64,1536]{3,2,1,0:T(8,128)(2,1)}, bf16[8,2,64,2560]{3,2,1,0:T(8,128)(2,1)}) custom-call(bf16[8,2,2,64,3072]{4,3,2,1,0:T(8,128)(2,1)} %bitcast.141, bf16[8,2,2,64,3072]{4,3,2,1,0:T(8,128)(2,1)} %bitcast.142, bf16[3072,2560]{1,0:T(8,128)(2,1)} %pad_maximum_fusion.wq_ref, bf16[3072,1536]{1,0:T(8,128)(2,1)} %bitcast.114, ...), custom_call_target="tpu_custom_call" | custom-call | flops 35433480192 | bytes 20971520 | tf_op jit(solution)/shard_map/attend/pallas_call | solution.py:133
  579.0 67.2 %attend.17 = (bf16[8,2,64,1536]{3,2,1,0:T(8,128)(2,1)}, bf16[8,2,64,2560]{3,2,1,0:T(8,128)(2,1)}) custom-call(bf16[8,2,2,64,3072]{4,3,2,1,0:T(8,128)(2,1)} %bitcast.146, bf16[8,2,2,64,3072]{4,3,2,1,0:T(8,128)(2,1)} %bitcast.147, bf16[3072,2560]{1,0:T(8,128)(2,1)} %pad_maximum_fusion.wq_ref, bf16[3072,1536]{1,0:T(8,128)(2,1)} %bitcast.115, ...), custom_call_target="tpu_custom_call" | custom-call | flops 35433480192 | bytes 20971520 | tf_op jit(solution)/shard_map/attend/pallas_call | solution.py:133
  646.3 2.1 bitcast_dynamic-update-slice_fusion.27
  648.3 2.1 bitcast_dynamic-update-slice_fusion.26
  650.4 2.1 bitcast_dynamic-update-slice_fusion.25
  652.4 2.0 bitcast_dynamic-update-slice_fusion.24
  654.5 2.1 bitcast_dynamic-update-slice_fusion.23
  656.6 97.3 %wgrad_out.1 = (f32[3072,3072]{1,0:T(8,128)}, f32[1536,3072]{1,0:T(8,128)}) custom-call(bf16[8,1,64,1536]{3,2,1,0:T(8,128)(2,1)} %get-tuple-element.29.refs_0_, bf16[8,1,64,1536]{3,2,1,0:T(8,128)(2,1)} %get-tuple-element.30.refs_1_, bf16[8,2,64,1536]{3,2,1,0:T(8,128)(2,1)} %get-tuple-element.31.refs_2_, bf16[8,2,64,1536]{3,2,1,0:T(8,128)(2,1)} %get-tuple-element.32.refs_3_, ...), custom_call_target="tpu_custom_call" | custom-call | flops 77309411328 | bytes 113246208 | tf_op jit(solution)/shard_map/wgrad_out/pallas_call | solution.py:212
  753.9 2.1 bitcast_dynamic-update-slice_fusion.22
  755.9 2.1 bitcast_dynamic-update-slice_fusion.21
  758.0 2.1 collective-permute-start
  760.1 2.5 bitcast_dynamic-update-slice_fusion.6
  762.6 2.4 bitcast_dynamic-update-slice_fusion.5
  765.0 2.5 bitcast_dynamic-update-slice_fusion.4
  767.5 2.4 bitcast_dynamic-update-slice_fusion.3
  769.9 2.5 bitcast_dynamic-update-slice_fusion.2
  772.4 85.3 %wgrad_qkv_a.1 = (f32[3072,5120]{1,0:T(8,128)}, f32[3072,1280]{1,0:T(8,128)}) custom-call(bf16[8,2,1,64,3072]{4,3,2,1,0:T(8,128)(2,1)} %bitcast.154, bf16[8,2,1,64,3072]{4,3,2,1,0:T(8,128)(2,1)} %bitcast.159, bf16[8,2,2,64,3072]{4,3,2,1,0:T(8,128)(2,1)} %bitcast.119, bf16[8,2,2,64,3072]{4,3,2,1,0:T(8,128)(2,1)} %bitcast.124, ...), custom_call_target="tpu_custom_call" | custom-call | flops 64424509440 | bytes 102760448 | tf_op jit(solution)/shard_map/wgrad_qkv_a/pallas_call | solution.py:212
  857.7 2.4 bitcast_dynamic-update-slice_fusion.1
  860.1 2.4 bitcast_dynamic-update-slice_fusion
  862.6 84.9 %wgrad_qkv_b.1 = (f32[3072,5120]{1,0:T(8,128)}, f32[3072,1280]{1,0:T(8,128)}) custom-call(bf16[8,2,1,64,3072]{4,3,2,1,0:T(8,128)(2,1)} %bitcast.155, bf16[8,2,1,64,3072]{4,3,2,1,0:T(8,128)(2,1)} %bitcast.160, bf16[8,2,2,64,3072]{4,3,2,1,0:T(8,128)(2,1)} %bitcast.120, bf16[8,2,2,64,3072]{4,3,2,1,0:T(8,128)(2,1)} %bitcast.125, ...), custom_call_target="tpu_custom_call", output_to_operand_aliasing={{0}: (18, {})} | custom-call | flops 64424509440 | bytes 102760448 | tf_op jit(solution)/shard_map/wgrad_qkv_b/pallas_call | solution.py:212
  948.6 5.9 broadcast_select_fusion.3
  954.4 8.8 broadcast_select_fusion
  963.3 4.1 slice_dynamic-update-slice_fusion.1
  967.3 2.0 slice_dynamic-update-slice_fusion
  969.4 2.7 slice_dynamic-update-slice_fusion.5
  972.1 1.2 slice_dynamic-update-slice_fusion.4
  973.3 2.8 slice_dynamic-update-slice_fusion.3
  976.1 1.1 slice_dynamic-update-slice_fusion.2
  977.3 42.4 %fusion.14 = (f32[3072]{0:T(1024)S(1)}, f32[16,64]{1,0:T(8,128)S(1)}, bf16[16,64,3072]{2,1,0:T(8,128)(2,1)}) fusion(bf16[16,64,3072]{2,1,0:T(8,128)(2,1)S(1)} %bitcast.100, f32[16,64]{1,0:T(8,128)S(1)} %copy-done.6, f32[3072]{0:T(1024)S(1)} %copy-done.8, bf16[16,64,5120]{2,1,0:T(8,128)(2,1)} %slice_dynamic-update-slice_fusion.2, bf16[3072,5120]{1,0:T(8,128)(2,1)} %param.11), kind=kOutput, calls=%fused_computation.19 | convolution fusion | flops 32240562176 | bytes 54558720 | tf_op jit(solution)/shard_map/bse,de->bsd/dot_general | solution.py:327
  1019.7 25.7 %fusion.16 = bf16[16,64,3072]{2,1,0:T(8,128)(2,1)} fusion(bf16[16,64,3072]{2,1,0:T(8,128)(2,1)S(1)} %bitcast.100, bf16[3072,3072]{1,0:T(8,128)(2,1)} %param.12, bf16[16,64,1536]{2,1,0:T(8,128)(2,1)} %get-tuple-element.69, bf16[16,64,1536]{2,1,0:T(8,128)(2,1)} %get-tuple-element.68), kind=kOutput, calls=%fused_computation.21 | convolution fusion | flops 19349372928 | bytes 37748736 | tf_op jit(solution)/shard_map/bse,ed->bsd/dot_general | solution.py:325
  1045.5 2.5 collective-permute-done.3
  1048.3 5.5 fusion.11
  1053.8 0.6 add.106
  1054.4 14.1 %place_qkv_a.1.full_ref = f32[3072,5120]{1,0:T(8,128)} custom-call(f32[3072,1280]{1,0:T(8,128)} %collective-permute-done.6.src_ref, f32[3072,5120]{1,0:T(8,128)} %get-tuple-element.50.full_ref), custom_call_target="tpu_custom_call", output_to_operand_aliasing={{}: (1, {})} | custom-call | flops 3932160 | bytes 31457280 | tf_op jit(solution)/shard_map/place_qkv_a/pallas_call | solution.py:234
  1068.6 14.1 %place_qkv_b.1 = f32[3072,5120]{1,0:T(8,128)} custom-call(f32[3072,1280]{1,0:T(8,128)} %collective-permute-done.5.src_ref, f32[3072,5120]{1,0:T(8,128)} %place_qkv_a.1.full_ref), custom_call_target="tpu_custom_call", output_to_operand_aliasing={{}: (1, {})} | custom-call | flops 3932160 | bytes 31457280 | tf_op jit(solution)/shard_map/place_qkv_b/pallas_call | solution.py:234
  1082.7 13.9 %place_out.1 = f32[3072,3072]{1,0:T(8,128)} custom-call(f32[1536,3072]{1,0:T(8,128)} %collective-permute-done.7.src_ref, f32[3072,3072]{1,0:T(8,128)} %get-tuple-element.52.full_ref), custom_call_target="tpu_custom_call", output_to_operand_aliasing={{}: (1, {})} | custom-call | flops 4718592 | bytes 37748736 | tf_op jit(solution)/shard_map/place_out/pallas_call | solution.py:234
  (84 shorter events, 4.6 us)
Async XLA Ops:
  7.2 4.3 copy-start.7
  7.2 85.1 %all-gather.19.cloned.1.call-start = ((), (), s32[]{:S(2)}) async-start(), calls=%async_computation | async-start | bytes 7077888 | tf_op jit(solution)/shard_map/all_gather | solution.py:263
  7.3 4.6 copy-start
  7.3 10.1 slice-start.2
  11.9 5.5 copy-start.5
  11.9 5.5 slice-start.3
  19.9 113.6 %all-gather.21.cloned.1.call-start = ((), (), s32[]{:S(2)}) async-start(), calls=%async_computation.1 | async-start | bytes 7077888 | tf_op jit(solution)/shard_map/all_gather | solution.py:263
  20.7 157.2 %all-gather.23.cloned.1.call-start = ((), (), s32[]{:S(2)}) async-start(), calls=%async_computation.2 | async-start | bytes 14155776 | tf_op jit(solution)/shard_map/all_gather | solution.py:263
  28.5 216.3 %all-gather.25.cloned.1.call-start = ((), (), s32[]{:S(2)}) async-start(), calls=%async_computation.3 | async-start | bytes 14155776 | tf_op jit(solution)/shard_map/all_gather | solution.py:263
  29.1 282.5 %all-gather.27.cloned.1.call-start = ((), (), s32[]{:S(2)}) async-start(), calls=%async_computation.4 | async-start | bytes 14155776 | tf_op jit(solution)/shard_map/all_gather | solution.py:263
  29.8 348.5 %all-gather.29.cloned.1.call-start = ((), (), s32[]{:S(2)}) async-start(), calls=%async_computation.5 | async-start | bytes 14155776 | tf_op jit(solution)/shard_map/all_gather | solution.py:263
  30.4 415.0 %all-gather.31.cloned.1.call-start = ((), (), s32[]{:S(2)}) async-start(), calls=%async_computation.6 | async-start | bytes 14155776 | tf_op jit(solution)/shard_map/all_gather | solution.py:263
  31.2 481.1 %all-gather.33.cloned.1.call-start = ((), (), s32[]{:S(2)}) async-start(), calls=%async_computation.7 | async-start | bytes 14155776 | tf_op jit(solution)/shard_map/all_gather | solution.py:263
  32.0 547.0 %all-gather.35.cloned.1.call-start = ((), (), s32[]{:S(2)}) async-start(), calls=%async_computation.8 | async-start | bytes 14155776 | tf_op jit(solution)/shard_map/all_gather | solution.py:263
  41.1 12.7 %copy-start.9 = (f32[64]{0:T(128)S(1)}, f32[64]{0:T(128)}, u32[]{:S(2)}) copy-start(f32[64]{0:T(128)} %param.9) | copy-start | bytes 772
  41.1 12.7 %copy-start.11 = (u32[16]{0:T(128)S(1)}, u32[16]{0:T(128)}, u32[]{:S(2)}) copy-start(u32[16]{0:T(128)} %constant.127) | copy-start | bytes 196
  41.1 14.0 %copy-start.10 = (s32[64]{0:T(128)S(1)}, s32[64]{0:T(128)}, u32[]{:S(2)}) copy-start(s32[64]{0:T(128)} %param.8) | copy-start | bytes 772
  79.4 11.9 %copy-start.3 = (f32[512,64]{1,0:T(8,128)S(1)}, f32[512,64]{1,0:T(8,128)}, u32[]{:S(2)}) copy-start(f32[512,64]{1,0:T(8,128)} %get-tuple-element.107) | copy-start | bytes 393220
  79.4 11.9 %copy-start.4 = (f32[512,64]{1,0:T(8,128)S(1)}, f32[512,64]{1,0:T(8,128)}, u32[]{:S(2)}) copy-start(f32[512,64]{1,0:T(8,128)} %get-tuple-element.108) | copy-start | bytes 393220
  758.0 190.6 %collective-permute-start = (bf16[16,64,1536]{2,1,0:T(8,128)(2,1)}, bf16[16,64,1536]{2,1,0:T(8,128)(2,1)}, u32[]{:S(2)}, u32[]{:S(2)}) collective-permute-start(bf16[16,64,1536]{2,1,0:T(8,128)(2,1)} %get-tuple-element.85), channel_id=1, source_target_pairs={{0,1},{1,0},{2,3},{3,2},{4,5},{5,4},{6,7},{7,6},{8,9},{9,8},{10,11... | collective-permute-start | bytes 9437192 | tf_op jit(solution)/shard_map/ppermute | solution.py:283
  862.6 91.9 %collective-permute-start.1 = (bf16[16,64,2560]{2,1,0:T(8,128)(2,1)}, bf16[16,64,2560]{2,1,0:T(8,128)(2,1)}, u32[]{:S(2)}, u32[]{:S(2)}) collective-permute-start(bf16[16,64,2560]{2,1,0:T(8,128)(2,1)} %get-tuple-element.70), channel_id=1, source_target_pairs={{0,1},{1,0},{2,3},{3,2},{4,5},{5,4},{6,7},{7,6},{8,9},{9,8},{10,11... | collective-permute-start | bytes 15728648 | tf_op jit(solution)/shard_map/ppermute | solution.py:284
  947.5 121.1 %collective-permute-start.5 = (f32[3072,1280]{1,0:T(8,128)}, f32[3072,1280]{1,0:T(8,128)}, u32[]{:S(2)}, u32[]{:S(2)}) collective-permute-start(f32[3072,1280]{1,0:T(8,128)} %get-tuple-element.48), channel_id=1, source_target_pairs={{0,1},{1,0},{2,3},{3,2},{4,5},{5,4},{6,7},{7,6},{8,9},{9,8},{10,11... | collective-permute-start | bytes 47185928 | tf_op jit(solution)/shard_map/ppermute | solution.py:322
  948.1 106.4 %collective-permute-start.6 = (f32[3072,1280]{1,0:T(8,128)}, f32[3072,1280]{1,0:T(8,128)}, u32[]{:S(2)}, u32[]{:S(2)}) collective-permute-start(f32[3072,1280]{1,0:T(8,128)} %get-tuple-element.49), channel_id=1, source_target_pairs={{0,1},{1,0},{2,3},{3,2},{4,5},{5,4},{6,7},{7,6},{8,9},{9,8},{10,11... | collective-permute-start | bytes 47185928 | tf_op jit(solution)/shard_map/ppermute | solution.py:321
  948.1 134.5 %collective-permute-start.7 = (f32[1536,3072]{1,0:T(8,128)}, f32[1536,3072]{1,0:T(8,128)}, u32[]{:S(2)}, u32[]{:S(2)}) collective-permute-start(f32[1536,3072]{1,0:T(8,128)} %get-tuple-element.51), channel_id=1, source_target_pairs={{0,1},{1,0},{2,3},{3,2},{4,5},{5,4},{6,7},{7,6},{8,9},{9,8},{10,11... | collective-permute-start | bytes 56623112 | tf_op jit(solution)/shard_map/ppermute | solution.py:323
  963.3 4.1 copy-start.1
  967.3 9.9 slice-start
  969.4 7.9 slice-start.1
  969.4 7.9 copy-start.6
  969.4 7.9 copy-start.8
  972.1 76.2 %slice-start.4 = ((s8[6291456]{0:T(1024)(128)(4,1)}), s8[4194304]{0:T(1024)(128)(4,1)S(1)}, s32[]{:S(2)}) async-start(s8[6291456]{0:T(1024)(128)(4,1)} %bitcast.105), calls=%async_computation.13 | async-start | bytes 8388608
  977.2 71.1 %slice-start.5 = ((s8[6291456]{0:T(1024)(128)(4,1)}), s8[2097152]{0:T(1024)(128)(4,1)S(1)}, s32[]{:S(2)}) async-start(s8[6291456]{0:T(1024)(128)(4,1)} %bitcast.105), calls=%async_computation.14 | async-start | bytes 4194304
  1019.6 25.8 %collective-permute-start.2 = (f32[3072]{0:T(1024)S(1)}, f32[3072]{0:T(1024)S(1)}, u32[]{:S(2)}, u32[]{:S(2)}) collective-permute-start(f32[3072]{0:T(1024)S(1)} %get-tuple-element.53), channel_id=1, source_target_pairs={{0,1},{1,0},{2,3},{3,2},{4,5},{5,4},{6,7},{7,6},{8,9},{9,8},{10,11... | collective-permute-start | bytes 36872 | tf_op jit(solution)/shard_map/ppermute | solution.py:334
  1019.7 28.6 %copy-start.2 = (bf16[16,64,3072]{2,1,0:T(8,128)(2,1)S(1)}, bf16[16,64,3072]{2,1,0:T(8,128)(2,1)}, u32[]{:S(2)}) copy-start(bf16[16,64,3072]{2,1,0:T(8,128)(2,1)} %get-tuple-element.109) | copy-start | bytes 18874372
  1045.4 2.6 collective-permute-start.3
  1048.0 5.8 collective-permute-start.4
Sparse Core Ops, SparseCore 0:
  20.0 39.8 all-gather.18
  61.4 36.6 all-gather.20
  99.7 63.3 all-gather.22
  165.1 63.6 all-gather.24
  230.2 63.6 all-gather.26
  295.3 63.6 all-gather.28
  360.6 63.6 all-gather.30
  425.9 63.5 all-gather.32
  491.1 63.6 all-gather.34

commit v2 on v1

v2 whole, which is shorter than its diff:
```python
import functools
import math
import jax
import jax.numpy as jnp
from jax import lax
from jax.experimental import pallas as pl
from jax.experimental.pallas import tpu as pltpu
from jax.sharding import PartitionSpec as P

NORM_EPS = 1e-5
ROPE_BASE = 10000.0
ROPE_SCALE = math.sqrt(1.0 + math.log(32.0) / math.log(4096.0))
F32 = jnp.float32
BF16 = jnp.bfloat16
MESH = pl.DeviceIdType.MESH
VMEM_LIMIT = 62 * 1024 * 1024
QB = 128
ANY = pl.BlockSpec(memory_space=pl.ANY)


def dot_nn(a, b):
    return lax.dot_general(a, b, (((1,), (0,)), ((), ())), preferred_element_type=F32)


def dot_nt(a, b):
    return lax.dot_general(a, b, (((1,), (1,)), ((), ())), preferred_element_type=F32)


def dot_tn(a, b):
    return lax.dot_general(a, b, (((0,), (0,)), ((), ())), preferred_element_type=F32)


def lane(index, width):
    return pl.ds(pl.multiple_of(index * width, 128), width)


def my_core():
    return lax.rem(lax.axis_index('sp'), 2)


def half_tables(positions, long_factor):
    half = long_factor.shape[0]
    exponents = jnp.arange(0, 2 * half, 2).astype(F32) / (2 * half)
    inv_freq = 1.0 / (long_factor * ROPE_BASE ** exponents)
    angles = positions.astype(F32)[:, None] * inv_freq
    return jnp.concatenate([jnp.cos(angles) * ROPE_SCALE, jnp.sin(angles) * ROPE_SCALE], axis=-1)


def attend_kernel(ranks, slots, group, hd, nb, rn_ref, dy_ref, wqkv_ref, wout_ref, tab_ref, gath_ref, o_ref, dqkv_ref,
                  wq_s, wo_s, rbuf, dbuf, tabs, cos_s, sin_s, qkv_s, do_s, qs, dos, ks, ps, dss,
                  ssem, rsem, tsend, trecv, wsem, lsem, gsem):
    b = pl.program_id(0)
    tl, dim = rn_ref.shape[1], rn_ref.shape[2]
    seq = ranks * tl
    q_cols, k_cols = slots * group * hd, slots * hd
    q_dim, kv_dim = 2 * q_cols, 2 * k_cols
    me = lax.axis_index('sp')
    core = lax.rem(me, 2)
    peer = me + 1 - 2 * core
    left, right = lax.rem(me + ranks - 2, ranks), lax.rem(me + 2, ranks)
    far = lax.rem(me + 4, ranks)
    cross = 1 - 2 * core

    def rcopy(src, dst, kind, at, target):
        return pltpu.make_async_remote_copy(src_ref=src, dst_ref=dst, send_sem=ssem.at[kind, at],
                                            recv_sem=rsem.at[kind, at], device_id={'sp': target}, device_id_type=MESH)

    def both(rank, at):
        return gath_ref.at[:, rank, at]

    def direct(at):
        for kind, target in ((0, right), (1, left), (4, peer)):
            rcopy(rn_ref.at[at], gath_ref.at[0, me, at], kind, at, target).start()
            rcopy(dy_ref.at[at], gath_ref.at[1, me, at], kind, at, target).start()

    def relay_near(at):
        rcopy(both(left, at), both(left, at), 0, at, me).wait_recv()
        rcopy(both(right, at), both(right, at), 1, at, me).wait_recv()
        rcopy(gath_ref.at[0, left, at], gath_ref.at[0, left, at], 2, at, right).start()
        rcopy(gath_ref.at[1, right, at], gath_ref.at[1, right, at], 3, at, left).start()

    def share_near(at):
        rcopy(both(left, at), both(left, at), 5, at, peer).start()
        rcopy(both(right, at), both(right, at), 6, at, peer).start()

    def relay_far(at):
        rcopy(gath_ref.at[0, far, at], gath_ref.at[0, far, at], 2, at, me).wait_recv()
        rcopy(gath_ref.at[1, far, at], gath_ref.at[1, far, at], 3, at, me).wait_recv()
        rcopy(both(far, at), both(far, at), 7, at, peer).start()

    def wait_shared(at):
        for kind, rank in ((4, peer), (5, left + cross), (6, right + cross), (7, far + cross)):
            rcopy(both(rank, at), both(rank, at), kind, at, me).wait_recv()

    def load(at):
        pltpu.make_async_copy(rn_ref.at[at], rbuf.at[me], lsem.at[0]).start()
        pltpu.make_async_copy(dy_ref.at[at], dbuf.at[me], lsem.at[1]).start()
        for step in range(1, ranks):
            rank = lax.rem(me + step, ranks)
            pltpu.make_async_copy(gath_ref.at[0, rank, at], rbuf.at[rank], lsem.at[0]).start()
            pltpu.make_async_copy(gath_ref.at[1, rank, at], dbuf.at[rank], lsem.at[1]).start()

    def keep_own(at):
        return (pltpu.make_async_copy(rbuf.at[me], gath_ref.at[0, me, at], gsem.at[0]),
                pltpu.make_async_copy(dbuf.at[me], gath_ref.at[1, me, at], gsem.at[1]))

    def table_copy(target):
        return pltpu.make_async_remote_copy(src_ref=tab_ref, dst_ref=tabs.at[me], send_sem=tsend.at[target],
                                            recv_sem=trecv.at[me], device_id={'sp': target}, device_id_type=MESH)

    def weight_copies():
        return (pltpu.make_async_copy(wqkv_ref.at[:, lane(core, q_cols)], wq_s.at[:, pl.ds(0, q_cols)], wsem.at[0]),
                pltpu.make_async_copy(wqkv_ref.at[:, pl.ds(pl.multiple_of(q_dim + core * k_cols, 128), k_cols)],
                                      wq_s.at[:, pl.ds(q_cols, k_cols)], wsem.at[1]),
                pltpu.make_async_copy(wqkv_ref.at[:, pl.ds(pl.multiple_of(q_dim + kv_dim + core * k_cols, 128), k_cols)],
                                      wq_s.at[:, pl.ds(q_cols + k_cols, k_cols)], wsem.at[2]),
                pltpu.make_async_copy(wout_ref.at[pl.ds(pl.multiple_of(core * q_cols, 128), q_cols)], wo_s, wsem.at[3]))

    @pl.when(b == 0)
    def _():
        for copy in weight_copies():
            copy.start()
        own_table = pltpu.make_async_copy(tab_ref, tabs.at[me], wsem.at[4])
        own_table.start()
        barrier = pltpu.get_barrier_semaphore()
        for step in range(1, ranks):
            pl.semaphore_signal(barrier, inc=1, device_id={'sp': lax.rem(me + step, ranks)}, device_id_type=MESH)
        pl.semaphore_wait(barrier, ranks - 1)
        direct(0)
        for step in range(1, ranks):
            table_copy(lax.rem(me + step, ranks)).start()
        relay_near(0)
        direct(1)
        share_near(0)
        own_table.wait()
        for step in range(1, ranks):
            rank = lax.rem(me + step, ranks)
            pltpu.make_async_remote_copy(src_ref=tab_ref, dst_ref=tabs.at[rank], send_sem=tsend.at[rank],
                                         recv_sem=trecv.at[rank], device_id={'sp': rank}, device_id_type=MESH).wait()
        tab = tabs[...].reshape(seq, hd)
        turned = pltpu.roll(tab, hd // 2, 1)
        low = lax.broadcasted_iota(jnp.int32, (seq, hd), 1) < hd // 2
        cos_s[...] = jnp.where(low, tab, turned)
        sin_s[...] = jnp.where(low, -turned, tab)
        relay_far(0)
        wait_shared(0)
        load(0)
        for copy in weight_copies():
            copy.wait()

    @pl.when(b + 1 < nb)
    def _():
        relay_near(b + 1)

    @pl.when(b + 2 < nb)
    def _():
        direct(b + 2)

    @pl.when(b + 1 < nb)
    def _():
        share_near(b + 1)

    pltpu.make_async_copy(rbuf, rbuf, lsem.at[0]).wait()
    pltpu.make_async_copy(dbuf, dbuf, lsem.at[1]).wait()
    for copy in keep_own(b):
        copy.start()
    qkv_s[...] = dot_nn(rbuf[...].reshape(seq, dim), wq_s[...]).astype(BF16)
    do_s[...] = dot_nt(dbuf[...].reshape(seq, dim), wo_s[...]).astype(BF16)

    nblk = seq // QB
    rpb = QB // tl
    rows_blk = group * QB
    score_scale = hd ** -0.5
    exp_scale = score_scale * math.log2(math.e)
    row_ids = lax.broadcasted_iota(jnp.int32, (rows_blk, QB), 0) % QB
    col_ids = lax.broadcasted_iota(jnp.int32, (rows_blk, QB), 1)
    causal = row_ids >= col_ids

    def rope(vals, rows):
        wide = vals.astype(F32)
        return (wide * cos_s[rows] + pltpu.roll(wide, hd // 2, 1) * sin_s[rows]).astype(BF16)

    def rope_back(vals, rows):
        wide = vals.astype(BF16).astype(F32)
        return (wide * cos_s[rows] - pltpu.roll(wide, hd // 2, 1) * sin_s[rows]).astype(BF16)

    def one_slot(slot, carry):
        q_at = [lane(slot * group + g, hd) for g in range(group)]
        k_at = pl.ds(pl.multiple_of(q_cols + slot * hd, hd), hd)
        v_at = pl.ds(pl.multiple_of(q_cols + k_cols + slot * hd, hd), hd)
        ks[...] = rope(qkv_s[:, k_at], pl.ds(0, seq))
        for g in range(group):
            for blk in range(nblk):
                rows = pl.ds(blk * QB, QB)
                dst = pl.ds(blk * rows_blk + g * QB, QB)
                qs[dst] = rope(qkv_s[rows, q_at[g]], rows)
                dos[dst] = do_s[rows, q_at[g]]
        for blk in range(nblk):
            span = (blk + 1) * QB
            rows = pl.ds(blk * rows_blk, rows_blk)
            keys = ks[:span]
            vals = qkv_s[:span, v_at]
            scores = dot_nt(qs[rows], keys)
            diag = jnp.where(causal, scores[:, span - QB:], -jnp.inf)
            scores = diag if blk == 0 else jnp.concatenate([scores[:, :span - QB], diag], axis=1)
            top = jnp.max(scores, axis=1, keepdims=True)
            ex = jnp.exp2((scores - top) * exp_scale)
            probs = ex * (1.0 / jnp.sum(ex, axis=1, keepdims=True))
            low = probs.astype(BF16)
            ps[rows, :span] = low
            outs = dot_nn(low, vals).astype(BF16)
            gp = dot_nt(dos[rows], vals).astype(BF16).astype(F32)
            rdot = jnp.sum(gp * probs, axis=1, keepdims=True)
            gs = (probs * (gp - rdot) * score_scale).astype(BF16)
            dss[rows, :span] = gs
            gq = dot_nn(gs, keys)
            for g in range(group):
                part = outs[g * QB:(g + 1) * QB].reshape(rpb, tl, hd)
                o_ref[blk * rpb:(blk + 1) * rpb, 0, :, q_at[g]] = part
                back = rope_back(gq[g * QB:(g + 1) * QB], pl.ds(blk * QB, QB)).reshape(rpb, tl, hd)
                dqkv_ref[blk * rpb:(blk + 1) * rpb, 0, :, q_at[g]] = back
        for blk in range(nblk):
            rows = pl.ds(blk * rows_blk, (nblk - blk) * rows_blk)
            cols = slice(blk * QB, (blk + 1) * QB)
            gv = dot_tn(ps[rows, cols], dos[rows]).astype(BF16).reshape(rpb, tl, hd)
            gk = rope_back(dot_tn(dss[rows, cols], qs[rows]), pl.ds(blk * QB, QB)).reshape(rpb, tl, hd)
            dqkv_ref[blk * rpb:(blk + 1) * rpb, 0, :, v_at] = gv
            dqkv_ref[blk * rpb:(blk + 1) * rpb, 0, :, k_at] = gk

        @pl.when((slot == 0) & (b + 1 < nb))
        def _():
            relay_far(b + 1)

        @pl.when((slot == 1) & (b + 1 < nb))
        def _():
            for copy in keep_own(b):
                copy.wait()
            wait_shared(b + 1)
            load(b + 1)
        return carry

    lax.fori_loop(0, slots, one_slot, 0)

    @pl.when(b == nb - 1)
    def _():
        for copy in keep_own(b):
            copy.wait()

        def drain(at, carry):
            for kind, rank in ((0, me), (1, me), (4, me), (5, left), (6, right), (7, far)):
                rcopy(both(rank, at), both(rank, at), kind, at, me).wait_send()
            for kind in (2, 3):
                rcopy(gath_ref.at[0, me, at], gath_ref.at[0, me, at], kind, at, me).wait_send()
            return carry
        lax.fori_loop(0, nb, drain, 0)


def attend(normed, grad_out, w_qkv, w_out, table, ranks):
    nb, tl, dim = normed.shape
    hd = table.shape[1]
    seq = ranks * tl
    q_cols, k_cols = w_out.shape[0] // 2, (w_qkv.shape[1] - w_out.shape[0]) // 4
    slots = k_cols // hd
    group = q_cols // k_cols
    cols = q_cols + 2 * k_cols
    flops = 2 * nb * seq * dim * (cols + q_cols) + 2 * 6 * nb * slots * group * seq * seq * hd
    return pl.pallas_call(
        functools.partial(attend_kernel, ranks, slots, group, hd, nb),
        grid=(nb,),
        in_specs=[ANY] * 5,
        out_specs=[ANY, pl.BlockSpec((ranks, 1, tl, q_cols), lambda b: (0, b, 0, 0)),
                   pl.BlockSpec((ranks, 1, tl, cols), lambda b: (0, b, 0, 0))],
        out_shape=[jax.ShapeDtypeStruct((2, ranks, nb, tl, dim), BF16),
                   jax.ShapeDtypeStruct((ranks, nb, tl, q_cols), BF16),
                   jax.ShapeDtypeStruct((ranks, nb, tl, cols), BF16)],
        scratch_shapes=[pltpu.VMEM((dim, cols), BF16), pltpu.VMEM((q_cols, dim), BF16),
                        pltpu.VMEM((ranks, tl, dim), BF16), pltpu.VMEM((ranks, tl, dim), BF16),
                        pltpu.VMEM((ranks, tl, hd), F32), pltpu.VMEM((seq, hd), F32), pltpu.VMEM((seq, hd), F32),
                        pltpu.VMEM((seq, cols), BF16), pltpu.VMEM((seq, q_cols), BF16),
                        pltpu.VMEM((group * seq, hd), BF16), pltpu.VMEM((group * seq, hd), BF16),
                        pltpu.VMEM((seq, hd), BF16),
                        pltpu.VMEM((group * seq, seq), BF16), pltpu.VMEM((group * seq, seq), BF16),
                        pltpu.SemaphoreType.DMA((8, nb)), pltpu.SemaphoreType.DMA((8, nb)),
                        pltpu.SemaphoreType.DMA((ranks,)), pltpu.SemaphoreType.DMA((ranks,)),
                        pltpu.SemaphoreType.DMA((5,)), pltpu.SemaphoreType.DMA((2,)), pltpu.SemaphoreType.DMA((2,))],
        compiler_params=pltpu.CompilerParams(dimension_semantics=("arbitrary",), vmem_limit_bytes=VMEM_LIMIT,
                                             collective_id=0, has_side_effects=True),
        cost_estimate=pl.CostEstimate(flops=flops, bytes_accessed=2 * nb * seq * (4 * dim + cols + q_cols),
                                      transcendentals=nb * slots * group * seq * seq),
        name="attend",
    )(normed, grad_out, w_qkv, w_out, table)


class Placer:
    def __init__(self, recv, full, buf, sems, steps, pieces):
        self.recv, self.full, self.buf, self.sems, self.steps, self.pieces = recv, full, buf, sems, steps, pieces
        self.rows = recv.shape[0] // steps

    def take(self, step):
        at = pl.ds(pl.multiple_of(step * self.rows, 8), self.rows)
        return pltpu.make_async_copy(self.recv.at[at], self.buf.at[lax.rem(step, 2)], self.sems.at[0, lax.rem(step, 2)])

    def put(self, step):
        out = []
        slot = lax.rem(step, 2)
        for n, (src_col, width, dst) in enumerate(self.pieces):
            out.append(pltpu.make_async_copy(self.buf.at[slot, :, pl.ds(src_col, width)], self.full.at[dst(step * self.rows, self.rows, width)],
                                             self.sems.at[1 + n, slot]))
        return out

    def first(self):
        self.take(0).start()

    def step(self, step):
        self.take(step).wait()
        for copy in self.put(step):
            copy.start()

        @pl.when(step >= 1)
        def _():
            for copy in self.put(step - 1):
                copy.wait()

        @pl.when(step + 1 < self.steps)
        def _():
            self.take(step + 1).start()

    def last(self):
        for copy in self.put(self.steps - 1):
            copy.wait()


def peer_cols(base, stride):
    def where(row, rows, width):
        return (pl.ds(pl.multiple_of(row, 8), rows), pl.ds(pl.multiple_of(base + (1 - my_core()) * stride, 128), width))
    return where


def peer_rows(stride):
    def where(row, rows, width):
        return (pl.ds(pl.multiple_of((1 - my_core()) * stride + row, 8), rows), pl.ds(0, width))
    return where


def weight_grad_kernel(total, left_at, right_at, chunks, pieces, place_pieces, n_extra, *refs):
    left_ref, right_ref = refs[0], refs[1]
    n_in = 2 + n_extra
    placing = place_pieces is not None
    n_out = 3 if placing else 2
    outs = refs[n_in:n_in + n_out]
    lbuf, rbuf, acc, sems = refs[n_in + n_out:n_in + n_out + 4]
    placer = None
    if placing:
        placer = Placer(refs[2], outs[2], refs[-2], refs[-1], total, place_pieces)
        placer.first()

    def fetch(step, slot):
        return (pltpu.make_async_copy(left_ref.at[left_at(step)], lbuf.at[slot], sems.at[0, slot]),
                pltpu.make_async_copy(right_ref.at[right_at(step)], rbuf.at[slot], sems.at[1, slot]))

    def flat(buf, slot):
        val = buf[slot]
        return val.reshape(-1, val.shape[-1])

    for copy in fetch(0, 0):
        copy.start()
    acc[...] = jnp.zeros_like(acc)

    def body(step, carry):
        slot = lax.rem(step, 2)
        for copy in fetch(step + 1, 1 - slot):
            copy.start()
        for copy in fetch(step, slot):
            copy.wait()
        if placing:
            placer.step(step)
        acc[...] += dot_tn(flat(lbuf, slot), flat(rbuf, slot))
        return carry

    lax.fori_loop(0, total - 1, body, 0)
    for copy in fetch(total - 1, (total - 1) % 2):
        copy.wait()
    if placing:
        placer.step(jnp.int32(total - 1))
    copies = []
    last = (total - 1) % 2
    part = acc.shape[0] // chunks
    for n in range(chunks):
        rows = pl.ds(n * part, part)
        val = lbuf[last, :, :, n * part:(n + 1) * part]
        acc[rows] += dot_tn(val.reshape(-1, part), flat(rbuf, last))
        for m, (out, src_col, width, dst) in enumerate(pieces):
            copy = pltpu.make_async_copy(acc.at[rows, pl.ds(src_col, width)], outs[out].at[dst(n * part, part, width)],
                                         sems.at[2 + m, n])
            copy.start()
            copies.append(copy)
    for copy in copies:
        copy.wait()
    if placing:
        placer.last()


def weight_grad(left, right, left_sel, right_sel, acc_shape, chunks, pieces, full_struct, carried, place, order, name):
    ranks, nb, tl = right.shape[-4], right.shape[-3], right.shape[-2]

    def at(sel, ref):
        if sel[0] == "plane":
            return (lambda step: (sel[1], slice(None), step)), ref.shape[-1]
        return (lambda step: (slice(None), step, slice(None), pl.ds(sel[1], sel[2]))), sel[2]
    left_at, left_width = at(left_sel, left)
    right_at, right_width = at(right_sel, right)
    operands, aliases = [left, right], {}
    out_shape = [full_struct, jax.ShapeDtypeStruct(acc_shape, F32)]
    scratch = [pltpu.VMEM((2, ranks, tl, left_width), BF16), pltpu.VMEM((2, ranks, tl, right_width), BF16),
               pltpu.VMEM(acc_shape, F32), pltpu.SemaphoreType.DMA((2 + len(pieces), max(2, chunks)))]
    place_pieces = None
    if place is not None:
        recv, full, place_pieces = place
        operands += [recv, full]
        aliases[3] = 2
        out_shape.append(jax.ShapeDtypeStruct(full.shape, F32))
        scratch += [pltpu.VMEM((2, recv.shape[0] // nb, recv.shape[1]), F32),
                    pltpu.SemaphoreType.DMA((1 + len(place_pieces), 2))]
    if carried is not None:
        aliases[len(operands)] = 0
        operands.append(carried)
    operands += order
    rows = ranks * nb * tl
    return pl.pallas_call(
        functools.partial(weight_grad_kernel, nb, left_at, right_at, chunks, pieces, place_pieces, len(operands) - 2),
        in_specs=[ANY] * len(operands),
        out_specs=[ANY] * len(out_shape),
        out_shape=out_shape,
        scratch_shapes=scratch,
        input_output_aliases=aliases,
        compiler_params=pltpu.CompilerParams(vmem_limit_bytes=VMEM_LIMIT),
        cost_estimate=pl.CostEstimate(flops=2 * rows * acc_shape[0] * acc_shape[1],
                                      bytes_accessed=2 * rows * (left_width + right_width) + 8 * acc_shape[0] * acc_shape[1],
                                      transcendentals=0),
        name=name,
    )(*operands)


def canonical_copies(mine_ref, pair_ref, full, sems, parts):
    core, me = my_core(), lax.axis_index('sp')
    out, src, base = [], 0, 0
    for n, width in enumerate(parts):
        for side, ref in enumerate((mine_ref.at[me], pair_ref)):
            owner = core if side == 0 else 1 - core
            dst = pl.ds(pl.multiple_of(base + owner * width, 128), width)
            out.append(pltpu.make_async_copy(ref.at[:, :, pl.ds(src, width)], full.at[:, :, dst], sems.at[n, side]))
        src += width
        base += 2 * width
    return out


def hidden_grad_kernel(parts, place_pieces, w_ref, x_ref, inv_ref, gain_ref, gm_ref, gp_ref, dy_ref, recv_ref, full_in,
                       dx_ref, dg_ref, full_ref, gfull, dn_s, dys, mean_s, bounce, csem, psem, dsem):
    del full_in
    step = pl.program_id(0)
    steps = pl.num_programs(0)
    nb, tl, dim = dys.shape
    rows = nb * tl
    width = w_ref.shape[0]
    placer = Placer(recv_ref, full_ref, bounce, psem, recv_ref.shape[0] // bounce.shape[1], place_pieces)

    @pl.when(step == 0)
    def _():
        for copy in canonical_copies(gm_ref, gp_ref, gfull, csem, parts):
            copy.start()
        placer.first()
        pltpu.make_async_copy(dy_ref, dys, dsem.at[0]).start()
        mean_s[...] = jnp.zeros_like(mean_s)
        for copy in canonical_copies(gm_ref, gp_ref, gfull, csem, parts):
            copy.wait()

    placer.step(step)
    low = dot_nt(gfull[...].reshape(rows, gfull.shape[-1]), w_ref[...]).astype(BF16)
    at = lane(step, width)
    dn_s[:, at] = low
    grad = low.astype(F32)
    unit = x_ref[:, :, at].reshape(rows, width).astype(F32) * inv_ref[...]
    mean_s[...] += jnp.sum(grad * gain_ref[:, at] * unit, axis=1, keepdims=True)
    dg_ref[:, at] = jnp.sum(grad * unit, axis=0, keepdims=True)

    @pl.when(step == steps - 1)
    def _():
        pltpu.make_async_copy(dy_ref, dys, dsem.at[0]).wait()

        def finish(i, carry):
            span = pl.ds(pl.multiple_of(i * tl, tl), tl)
            inv = inv_ref[span]
            unit_rows = x_ref[i].astype(F32) * inv
            inner = inv * (dn_s[span].astype(F32) * gain_ref[...] - unit_rows * (mean_s[span] * (1.0 / dim)))
            dys[i] = (dys[i].astype(F32) + inner).astype(BF16)
            pltpu.make_async_copy(dys.at[i], dx_ref.at[i], dsem.at[1]).start()
            return carry
        lax.fori_loop(0, nb, finish, 0)
        placer.last()
        pltpu.make_async_copy(dys, dx_ref, dsem.at[1]).wait()


def hidden_grad(hidden, grad_out, inv_rms, norm_weight, w_qkv, g_all, g_pair, recv, full, parts, place_pieces):
    nb, tl, dim = hidden.shape
    cols = w_qkv.shape[1]
    width = 512
    steps = dim // width
    const = lambda *shape: pl.BlockSpec(shape, lambda n: (0,) * len(shape), pipeline_mode=pl.Buffered(1))
    return pl.pallas_call(
        functools.partial(hidden_grad_kernel, parts, place_pieces),
        grid=(steps,),
        in_specs=[pl.BlockSpec((width, cols), lambda n: (n, 0)), const(nb, tl, dim), const(nb * tl, 1), const(1, dim),
                  ANY, ANY, ANY, ANY, ANY],
        out_specs=[ANY, const(1, dim), ANY],
        out_shape=[jax.ShapeDtypeStruct((nb, tl, dim), BF16), jax.ShapeDtypeStruct((1, dim), F32),
                   jax.ShapeDtypeStruct(full.shape, F32)],
        scratch_shapes=[pltpu.VMEM((nb, tl, cols), BF16), pltpu.VMEM((nb * tl, dim), BF16), pltpu.VMEM((nb, tl, dim), BF16),
                        pltpu.VMEM((nb * tl, 1), F32), pltpu.VMEM((2, recv.shape[0] // steps, recv.shape[1]), F32),
                        pltpu.SemaphoreType.DMA((len(parts), 2)), pltpu.SemaphoreType.DMA((1 + len(place_pieces), 2)),
                        pltpu.SemaphoreType.DMA((2,))],
        input_output_aliases={8: 2},
        compiler_params=pltpu.CompilerParams(dimension_semantics=("arbitrary",), vmem_limit_bytes=VMEM_LIMIT),
        cost_estimate=pl.CostEstimate(flops=2 * nb * tl * dim * cols, bytes_accessed=2 * dim * cols + 8 * recv.size,
                                      transcendentals=0),
        name="hidden_grad",
    )(w_qkv, hidden, inv_rms, norm_weight, g_all, g_pair, grad_out, recv, full)


def project_out_kernel(parts, place_pieces, w_ref, x_ref, om_ref, op_ref, recv_ref, full_in, y_ref, full_ref,
                       ofull, bounce, csem, psem):
    del full_in
    step = pl.program_id(0)
    steps = pl.num_programs(0)
    nb, tl, q_dim = ofull.shape
    placer = Placer(recv_ref, full_ref, bounce, psem, recv_ref.shape[0] // bounce.shape[1], place_pieces)

    @pl.when(step == 0)
    def _():
        for copy in canonical_copies(om_ref, op_ref, ofull, csem, parts):
            copy.start()
        placer.first()
        for copy in canonical_copies(om_ref, op_ref, ofull, csem, parts):
            copy.wait()

    placer.step(step)
    mixed = dot_nn(ofull[...].reshape(nb * tl, q_dim), w_ref[...])
    y_ref[...] = (x_ref[...].astype(F32) + mixed.reshape(y_ref.shape)).astype(BF16)

    @pl.when(step == steps - 1)
    def _():
        placer.last()


def project_out(hidden, w_out, o_all, o_pair, recv, full, parts, place_pieces):
    nb, tl, dim = hidden.shape
    q_dim = w_out.shape[0]
    width = 512
    steps = dim // width
    tile = pl.BlockSpec((nb, tl, width), lambda n: (0, 0, n))
    return pl.pallas_call(
        functools.partial(project_out_kernel, parts, place_pieces),
        grid=(steps,),
        in_specs=[pl.BlockSpec((q_dim, width), lambda n: (0, n)), tile, ANY, ANY, ANY, ANY],
        out_specs=[tile, ANY],
        out_shape=[jax.ShapeDtypeStruct((nb, tl, dim), BF16), jax.ShapeDtypeStruct(full.shape, F32)],
        scratch_shapes=[pltpu.VMEM((nb, tl, q_dim), BF16), pltpu.VMEM((2, recv.shape[0] // steps, recv.shape[1]), F32),
                        pltpu.SemaphoreType.DMA((len(parts), 2)), pltpu.SemaphoreType.DMA((1 + len(place_pieces), 2))],
        input_output_aliases={5: 1},
        compiler_params=pltpu.CompilerParams(dimension_semantics=("arbitrary",), vmem_limit_bytes=VMEM_LIMIT),
        cost_estimate=pl.CostEstimate(flops=2 * nb * tl * dim * q_dim, bytes_accessed=2 * dim * q_dim + 8 * recv.size,
                                      transcendentals=0),
        name="project_out",
    )(w_out, hidden, o_all, o_pair, recv, full)


def group_sum_kernel(ranks, part_ref, sum_ref, parts, ssem, rsem):
    me = lax.axis_index('sp')
    barrier = pltpu.get_barrier_semaphore()
    for step in range(1, ranks):
        pl.semaphore_signal(barrier, inc=1, device_id={'sp': lax.rem(me + step, ranks)}, device_id_type=MESH)
    pl.semaphore_wait(barrier, ranks - 1)

    def copy(slot, target):
        return pltpu.make_async_remote_copy(src_ref=part_ref, dst_ref=parts.at[slot], send_sem=ssem.at[target],
                                            recv_sem=rsem.at[slot], device_id={'sp': target}, device_id_type=MESH)
    own = pltpu.make_async_copy(part_ref, parts.at[me], ssem.at[me])
    own.start()
    for step in range(1, ranks):
        copy(me, lax.rem(me + step, ranks)).start()
    own.wait()
    for step in range(1, ranks):
        rank = lax.rem(me + step, ranks)
        copy(rank, rank).wait()
    total = parts[0]
    for rank in range(1, ranks):
        total = total + parts[rank]
    sum_ref[...] = total


def group_sum(part, ranks):
    return pl.pallas_call(
        functools.partial(group_sum_kernel, ranks),
        in_specs=[ANY],
        out_specs=pl.BlockSpec(memory_space=pltpu.VMEM),
        out_shape=jax.ShapeDtypeStruct(part.shape, F32),
        scratch_shapes=[pltpu.VMEM((ranks,) + part.shape, F32), pltpu.SemaphoreType.DMA((ranks,)),
                        pltpu.SemaphoreType.DMA((ranks,))],
        compiler_params=pltpu.CompilerParams(collective_id=1, has_side_effects=True),
        cost_estimate=pl.CostEstimate(flops=ranks * part.size, bytes_accessed=8 * ranks * part.size, transcendentals=0),
        name="group_sum",
    )(part)


def block_body(ranks, hidden, positions, long_factor, norm_weight, w_qkv, w_out, grad_out):
    nb, tl, dim = hidden.shape
    hd = 2 * long_factor.shape[0]
    q_dim = w_out.shape[0]
    kv_dim = (w_qkv.shape[1] - q_dim) // 2
    me = lax.axis_index('sp')
    other = me + 1 - 2 * lax.rem(me, 2)
    pair = [(i, i ^ 1) for i in range(ranks)]
    qh, kh = q_dim // 2, kv_dim // 2

    hidden_wide = hidden.astype(F32)
    inv_rms = lax.rsqrt(jnp.mean(hidden_wide * hidden_wide, axis=-1, keepdims=True) + NORM_EPS)
    normed = (hidden_wide * inv_rms * norm_weight).astype(BF16)
    gathered, o_all, g_all = attend(normed, grad_out, w_qkv, w_out, half_tables(positions, long_factor), ranks)
    o_pair = lax.ppermute(lax.dynamic_index_in_dim(o_all, other, 0, keepdims=False), 'sp', pair)
    g_pair = lax.ppermute(lax.dynamic_index_in_dim(g_all, other, 0, keepdims=False), 'sp', pair)

    half = (qh + 2 * kh) // 2
    q_left = qh - half
    dwq_struct = jax.ShapeDtypeStruct(w_qkv.shape, F32)
    dwo_struct = jax.ShapeDtypeStruct(w_out.shape, F32)

    def own_cols(base, stride):
        def where(row, rows, width):
            return (pl.ds(row, rows), pl.ds(pl.multiple_of(base + my_core() * stride, 128), width))
        return where

    def own_rows(stride):
        def where(row, rows, width):
            return (pl.ds(pl.multiple_of(my_core() * stride + row, 8), rows), pl.ds(0, width))
        return where

    def same(row, rows, width):
        return (pl.ds(row, rows), pl.ds(0, width))

    dwo, send_o = weight_grad(o_all, gathered, ("cols", 0, qh), ("plane", 1), (qh, dim), 4,
                              [(0, 0, dim, own_rows(qh)), (1, 0, dim, same)], dwo_struct, None, None, [], "wgrad_out")
    recv_o = lax.ppermute(send_o, 'sp', pair)
    dwq, send_a = weight_grad(gathered, g_all, ("plane", 0), ("cols", 0, half), (dim, half), 4,
                              [(0, 0, half, own_cols(0, qh)), (1, 0, half, same)], dwq_struct, None, None, [dwo],
                              "wgrad_qkv_a")
    recv_a = lax.ppermute(send_a, 'sp', pair)
    dwq, send_b, dwo = weight_grad(gathered, g_all, ("plane", 0), ("cols", half, half), (dim, half), 4,
                                   [(0, 0, q_left, own_cols(half, qh)), (0, q_left, kh, own_cols(q_dim, kh)),
                                    (0, q_left + kh, kh, own_cols(q_dim + kv_dim, kh)), (1, 0, half, same)],
                                   dwq_struct, dwq, (recv_o, dwo, [(0, dim, peer_rows(qh))]), [o_pair, g_pair], "wgrad_qkv_b")
    recv_b = lax.ppermute(send_b, 'sp', pair)
    grad_hidden, grad_norm, dwq = hidden_grad(
        hidden, grad_out, inv_rms.reshape(nb * tl, 1), norm_weight[None], w_qkv, g_all, g_pair, recv_a, dwq,
        [qh, kh, kh], [(0, half, peer_cols(0, qh))])
    out_hidden, dwq = project_out(
        hidden, w_out, o_all, o_pair, recv_b, dwq, [qh],
        [(0, q_left, peer_cols(half, qh)), (q_left, kh, peer_cols(q_dim, kh)), (q_left + kh, kh, peer_cols(q_dim + kv_dim, kh))])
    grad_norm = group_sum(grad_norm.reshape(-1, 128), ranks).reshape(-1)
    return out_hidden, grad_hidden, grad_norm, dwq, dwo


def solution(mesh):
    token_spec = P('dp', 'sp', None)
    return jax.shard_map(functools.partial(block_body, mesh.shape['sp']), mesh=mesh,
                         in_specs=(token_spec, P(('dp', 'sp')), P(), P(), P(), P(), token_spec),
                         out_specs=(token_spec, token_spec, P('dp'), P('dp', None), P('dp', None)),
                         check_vma=False)
```

time: 1110 us -> 890 us (0.80)
  local copies, waits for them, and re-layouts: 88.5 us -> 11 us
  matrix products: 68.1 us -> 0 us
  other arithmetic: 55.4 us -> 14.3 us
  between operations: 15.2 us -> 0.93 us
    dot_general x2 -> x0, matrix products: 68.1 us -> none  [the longest x1 42.4 us: block_body(): jnp.einsum('bse,de->bsd', grad_qkv, w_qkv, preferred_element_type=F32)]
    unnamed x61 -> x7, local copies, waits for them, and re-layouts: 61.4 us -> 0.62 us
    dynamic_slice x3 -> x0, local copies, waits for them, and re-layouts: 21.4 us -> none  [the longest x1 8.27 us: block_body(): wo_own_t = lax.dynamic_slice_in_dim(w_out, core * qh, qh, 0).T]
    select_n x2 -> x0, other arithmetic: 14.7 us -> none  [the longest x1 8.82 us: in_order(): hi = jnp.where(core == 0, peer, mine)]
    another operation x2 -> x0, other arithmetic: 13.1 us -> none  [block_body(): both = jnp.stack([normed, grad_out])]
    concatenate x2 -> x1, other arithmetic: 12.9 us -> 0.7 us  [half_tables(): jnp.concatenate([jnp.cos(angles) * ROPE_SCALE, jnp.sin(angles) * ROPE_SCA...]
    pallas_call x15 -> x7, Pallas kernels: 856 us -> 857 us  [the longest x1 498 us: attend(): pl.pallas_call(functools.partial(attend_kernel, ranks, slots, group, hd,...]
  transfers between devices with their start and end apart: 17 -> 5, of which waited for: 1 -> 0; matrix products, arithmetic and copies ran while one was open for 17% -> 1% of each run, Pallas kernels for 61% -> 26%
where the time goes in v2:
time: 890 us; the launch traced here: 886 us
  Pallas kernels  857 us (96%)
  other arithmetic  14.3 us (2%)
  local copies, waits for them, and re-layouts  11 us (1%)
    pallas_call x1, Pallas kernels, attend(): pl.pallas_call(functools.partial(attend_kernel, ranks, slots, group, hd,...  498 us
    pallas_call x3, Pallas kernels, weight_grad(): pl.pallas_call(functools.partial(weight_grad_kernel, nb, left_at, right_a...  259 us
    pallas_call x1, Pallas kernels, hidden_grad(): pl.pallas_call(functools.partial(hidden_grad_kernel, parts, place_pieces)...  59.4 us
    pallas_call x1, Pallas kernels, project_out(): pl.pallas_call(functools.partial(project_out_kernel, parts, place_pieces)...  35.8 us
  transfers between devices with their start and end apart: 5, of which 0 were waited for; matrix products, arithmetic and copies ran while one was open for 1% of the time, Pallas kernels for 26%

profile of v2, /device:TPU:113, one launch (start us, length us, event | category | flops | bytes accessed | tf_op | source)
XLA Modules:
  0.0 886.1 jit_solution(8245946946817857974)
XLA Ops:
  0.6 0.7 convert_element_type.14
  1.3 0.7 multiply_divide_fusion
  2.0 4.1 fusion
  6.1 0.0 copy-start
  6.1 0.2 fusion.3
  6.3 0.7 pad_maximum_fusion.tab_ref
  7.0 0.0 copy-done
  7.0 8.0 fusion.2.rn_ref
  15.0 497.6 %attend.1 = (bf16[2,8,16,64,3072]{4,3,2,1,0:T(8,128)(2,1)}, bf16[8,16,64,1536]{3,2,1,0:T(8,128)(2,1)}, bf16[8,16,64,2560]{3,2,1,0:T(8,128)(2,1)}) custom-call(bf16[16,64,3072]{2,1,0:T(8,128)(2,1)} %fusion.2.rn_ref, bf16[16,64,3072]{2,1,0:T(8,128)(2,1)} %dy_ref.3, bf16[3072,5120]{1,0:T(8,128)(2,1)} %w_ref.2, bf16[3072,3072]{1,0:T(8,128)(2,1)} %w_ref.3, ...), custom_call_target="tpu_custom_call" | custom-call | flops 283467841536 | bytes 268435456 | tf_op jit(solution)/shard_map/attend/pallas_call | solution.py:267
  512.6 92.8 %wgrad_out.1 = (f32[3072,3072]{1,0:T(8,128)}, f32[1536,3072]{1,0:T(8,128)}) custom-call(bf16[8,16,64,1536]{3,2,1,0:T(8,128)(2,1)} %get-tuple-element.20.refs_0_.om_ref, bf16[2,8,16,64,3072]{4,3,2,1,0:T(8,128)(2,1)} %get-tuple-element.21.refs_1_.refs_0_), custom_call_target="tpu_custom_call" | custom-call | flops 77309411328 | bytes 113246208 | tf_op jit(solution)/shard_map/wgrad_out/pallas_call | solution.py:429
  605.3 1.4 collective-permute-start.1
  606.7 5.3 dynamic-slice_bitcast_fusion
  612.0 0.0 collective-permute-start.2
  612.1 3.8 dynamic-slice_bitcast_fusion.1
  615.9 0.5 collective-permute-start
  616.4 81.0 %wgrad_qkv_a.1 = (f32[3072,5120]{1,0:T(8,128)}, f32[3072,1280]{1,0:T(8,128)}) custom-call(bf16[2,8,16,64,3072]{4,3,2,1,0:T(8,128)(2,1)} %get-tuple-element.21.refs_1_.refs_0_, bf16[8,16,64,2560]{3,2,1,0:T(8,128)(2,1)} %get-tuple-element.22.refs_1_.gm_ref, f32[3072,3072]{1,0:T(8,128)} %get-tuple-element.24.refs_2_.refs_3_), custom_call_target="tpu_custom_call" | custom-call | flops 64424509440 | bytes 102760448 | tf_op jit(solution)/shard_map/wgrad_qkv_a/pallas_call | solution.py:429
  697.4 0.2 collective-permute-start.4
  697.5 0.0 collective-permute-done.refs_5_.op_ref
  697.5 0.0 collective-permute-done.2.refs_6_.gp_ref
  697.5 0.0 collective-permute-done.1.refs_2_
  697.5 0.0 copy-start.1
  697.5 84.8 %wgrad_qkv_b.1 = (f32[3072,5120]{1,0:T(8,128)}, f32[3072,1280]{1,0:T(8,128)}, f32[3072,3072]{1,0:T(8,128)}) custom-call(bf16[2,8,16,64,3072]{4,3,2,1,0:T(8,128)(2,1)} %get-tuple-element.21.refs_1_.refs_0_, bf16[8,16,64,2560]{3,2,1,0:T(8,128)(2,1)} %get-tuple-element.22.refs_1_.gm_ref, ...), custom_call_target="tpu_custom_call", output_to_operand_aliasing={{2}: (3, {}), {0}: (4, {})} | custom-call | flops 64424509440 | bytes 102760448 | tf_op jit(solution)/shard_map/wgrad_qkv_b/pallas_call | solution.py:429
  782.4 0.5 collective-permute-start.3
  782.8 0.0 copy-done.1
  782.8 1.3 rsqrt.20.inv_ref
  784.1 0.0 collective-permute-done.4.recv_ref
  784.1 59.4 %hidden_grad.1 = (bf16[16,64,3072]{2,1,0:T(8,128)(2,1)}, f32[1,3072]{1,0:T(1,128)}, f32[3072,5120]{1,0:T(8,128)}) custom-call(bf16[3072,5120]{1,0:T(8,128)(2,1)} %w_ref.2, bf16[16,64,3072]{2,1,0:T(8,128)(2,1)} %x_ref.3, f32[1024,1]{1,0:T(8,128)} %rsqrt.20.inv_ref, f32[1,3072]{1,0:T(1,128)} %bitcast.7, ...), custom_call_target="tpu_custom_call", output_to_operand_aliasing={{2}: (8, {})} | custom-call | flops 32212254720 | bytes 62914560 | tf_op jit(solution)/shard_map/hidden_grad/pallas_call | solution.py:509
  843.5 6.0 group_sum.1
  849.5 0.0 collective-permute-done.3.recv_ref
  849.5 0.0 copy-start.2
  849.5 35.8 %project_out.1 = (bf16[16,64,3072]{2,1,0:T(8,128)(2,1)}, f32[3072,5120]{1,0:T(8,128)}) custom-call(bf16[3072,3072]{1,0:T(8,128)(2,1)} %w_ref.3, bf16[16,64,3072]{2,1,0:T(8,128)(2,1)} %x_ref.3, bf16[8,16,64,1536]{3,2,1,0:T(8,128)(2,1)} %get-tuple-element.20.refs_0_.om_ref, ...), custom_call_target="tpu_custom_call", output_to_operand_aliasing={{1}: (5, {})} | custom-call | flops 19327352832 | bytes 50331648 | tf_op jit(solution)/shard_map/project_out/pallas_call | solution.py:560
  885.3 0.0 copy-done.2
  885.3 0.6 copy.22
  (1 shorter events, 0.0 us)
Async XLA Ops:
  6.1 0.9 copy-start
  605.3 92.2 %collective-permute-start.1 = (f32[1536,3072]{1,0:T(8,128)}, f32[1536,3072]{1,0:T(8,128)}, u32[]{:S(2)}, u32[]{:S(2)}) collective-permute-start(f32[1536,3072]{1,0:T(8,128)} %get-tuple-element.23), channel_id=1, source_target_pairs={{0,1},{1,0},{2,3},{3,2},{4,5},{5,4},{6,7},{7,6},{8,9},{9,8},{10,11... | collective-permute-start | bytes 56623112 | tf_op jit(solution)/shard_map/ppermute | solution.py:651
  612.0 85.5 %collective-permute-start.2 = (bf16[16,64,2560]{2,1,0:T(8,128)(2,1)}, bf16[16,64,2560]{2,1,0:T(8,128)(2,1)}, u32[]{:S(2)}, u32[]{:S(2)}) collective-permute-start(bf16[16,64,2560]{2,1,0:T(8,128)(2,1)} %dynamic-slice_bitcast_fusion), channel_id=1, source_target_pairs={{0,1},{1,0},{2,3},{3,2},{4,5},{5,4},{6,7},{7,6},{8,9},{9,8},{10,11... | collective-permute-start | bytes 15728648 | tf_op jit(solution)/shard_map/ppermute | solution.py:629
  615.9 81.6 %collective-permute-start = (bf16[16,64,1536]{2,1,0:T(8,128)(2,1)}, bf16[16,64,1536]{2,1,0:T(8,128)(2,1)}, u32[]{:S(2)}, u32[]{:S(2)}) collective-permute-start(bf16[16,64,1536]{2,1,0:T(8,128)(2,1)} %dynamic-slice_bitcast_fusion.1), channel_id=1, source_target_pairs={{0,1},{1,0},{2,3},{3,2},{4,5},{5,4},{6,7},{7,6},{8,9},{9,8},{10,11... | collective-permute-start | bytes 9437192 | tf_op jit(solution)/shard_map/ppermute | solution.py:628
  697.4 86.7 %collective-permute-start.4 = (f32[3072,1280]{1,0:T(8,128)}, f32[3072,1280]{1,0:T(8,128)}, u32[]{:S(2)}, u32[]{:S(2)}) collective-permute-start(f32[3072,1280]{1,0:T(8,128)} %get-tuple-element.27), channel_id=1, source_target_pairs={{0,1},{1,0},{2,3},{3,2},{4,5},{5,4},{6,7},{7,6},{8,9},{9,8},{10,11... | collective-permute-start | bytes 47185928 | tf_op jit(solution)/shard_map/ppermute | solution.py:655
  697.5 85.3 %copy-start.1 = (f32[16,64]{1,0:T(8,128)S(1)}, f32[16,64]{1,0:T(8,128)}, u32[]{:S(2)}) copy-start(f32[16,64]{1,0:T(8,128)} %copy-done) | copy-start | bytes 12292
  782.4 67.2 %collective-permute-start.3 = (f32[3072,1280]{1,0:T(8,128)}, f32[3072,1280]{1,0:T(8,128)}, u32[]{:S(2)}, u32[]{:S(2)}) collective-permute-start(f32[3072,1280]{1,0:T(8,128)} %get-tuple-element.26), channel_id=1, source_target_pairs={{0,1},{1,0},{2,3},{3,2},{4,5},{5,4},{6,7},{7,6},{8,9},{9,8},{10,11... | collective-permute-start | bytes 47185928 | tf_op jit(solution)/shard_map/ppermute | solution.py:660
  849.5 35.8 %copy-start.2 = (f32[24,128]{1,0:T(8,128)S(1)}, f32[24,128]{1,0:T(8,128)}, u32[]{:S(2)}) copy-start(f32[24,128]{1,0:T(8,128)} %group_sum.1) | copy-start | bytes 36868

commit v3 on v2

--- a/solution.py
+++ b/solution.py
@@ -13,7 +13,7 @@
 F32 = jnp.float32
 BF16 = jnp.bfloat16
 MESH = pl.DeviceIdType.MESH
-VMEM_LIMIT = 62 * 1024 * 1024
+VMEM_LIMIT = 67000000
 QB = 128
 ANY = pl.BlockSpec(memory_space=pl.ANY)
 
@@ -46,8 +46,8 @@
     return jnp.concatenate([jnp.cos(angles) * ROPE_SCALE, jnp.sin(angles) * ROPE_SCALE], axis=-1)
 
 
-def attend_kernel(ranks, slots, group, hd, nb, rn_ref, dy_ref, wqkv_ref, wout_ref, tab_ref, gath_ref, o_ref, dqkv_ref,
-                  wq_s, wo_s, rbuf, dbuf, tabs, cos_s, sin_s, qkv_s, do_s, qs, dos, ks, ps, dss,
+def attend_kernel(ranks, slots, group, hd, nb, rn_ref, dy_ref, wqkv_ref, wout_ref, tab_ref, gath_ref, o_ref, dqkv_ref, osend_ref, gsend_ref,
+                  wq_s, wo_s, rbuf, dbuf, tabs, cos_s, sin_s, qkv_s, do_s, qs, dos, ks, ps, dss, sc, gps,
                   ssem, rsem, tsend, trecv, wsem, lsem, gsem):
     b = pl.program_id(0)
     tl, dim = rn_ref.shape[1], rn_ref.shape[2]
@@ -131,6 +131,7 @@
             table_copy(lax.rem(me + step, ranks)).start()
         relay_near(0)
         direct(1)
+        direct(2)
         share_near(0)
         own_table.wait()
         for step in range(1, ranks):
@@ -152,9 +153,9 @@
     def _():
         relay_near(b + 1)
 
-    @pl.when(b + 2 < nb)
-    def _():
-        direct(b + 2)
+    @pl.when(b + 3 < nb)
+    def _():
+        direct(b + 3)
 
     @pl.when(b + 1 < nb)
     def _():
@@ -172,9 +173,10 @@
     rows_blk = group * QB
     score_scale = hd ** -0.5
     exp_scale = score_scale * math.log2(math.e)
-    row_ids = lax.broadcasted_iota(jnp.int32, (rows_blk, QB), 0) % QB
-    col_ids = lax.broadcasted_iota(jnp.int32, (rows_blk, QB), 1)
+    row_ids = lax.broadcasted_iota(jnp.int32, (QB, QB), 0)
+    col_ids = lax.broadcasted_iota(jnp.int32, (QB, QB), 1)
     causal = row_ids >= col_ids
+    lanes = ks.shape[0]
 
     def rope(vals, rows):
         wide = vals.astype(F32)
@@ -184,54 +186,71 @@
         wide = vals.astype(BF16).astype(F32)
         return (wide * cos_s[rows] - pltpu.roll(wide, hd // 2, 1) * sin_s[rows]).astype(BF16)
 
-    def one_slot(slot, carry):
-        q_at = [lane(slot * group + g, hd) for g in range(group)]
-        k_at = pl.ds(pl.multiple_of(q_cols + slot * hd, hd), hd)
-        v_at = pl.ds(pl.multiple_of(q_cols + k_cols + slot * hd, hd), hd)
-        ks[...] = rope(qkv_s[:, k_at], pl.ds(0, seq))
-        for g in range(group):
-            for blk in range(nblk):
-                rows = pl.ds(blk * QB, QB)
-                dst = pl.ds(blk * rows_blk + g * QB, QB)
-                qs[dst] = rope(qkv_s[rows, q_at[g]], rows)
-                dos[dst] = do_s[rows, q_at[g]]
-        for blk in range(nblk):
+    def one_pair(pair, carry):
+        def q_at(s, g):
+            return lane((pair * lanes + s) * group + g, hd)
+
+        def k_at(s):
+            return pl.ds(pl.multiple_of(q_cols + (pair * lanes + s) * hd, hd), hd)
+
+        def v_at(s):
+            return pl.ds(pl.multiple_of(q_cols + k_cols + (pair * lanes + s) * hd, hd), hd)
+
+        def prepare(s):
+            ks[s] = rope(qkv_s[:, k_at(s)], pl.ds(0, seq))
+            for g in range(group):
+                for blk in range(nblk):
+                    rows = pl.ds(blk * QB, QB)
+                    dst = pl.ds(blk * rows_blk + g * QB, QB)
+                    qs[s, dst] = rope(qkv_s[rows, q_at(s, g)], rows)
+                    dos[s, dst] = do_s[rows, q_at(s, g)]
+
+        def softmax(s, blk):
             span = (blk + 1) * QB
             rows = pl.ds(blk * rows_blk, rows_blk)
-            keys = ks[:span]
-            vals = qkv_s[:span, v_at]
-            scores = dot_nt(qs[rows], keys)
-            diag = jnp.where(causal, scores[:, span - QB:], -jnp.inf)
-            scores = diag if blk == 0 else jnp.concatenate([scores[:, :span - QB], diag], axis=1)
-            top = jnp.max(scores, axis=1, keepdims=True)
-            ex = jnp.exp2((scores - top) * exp_scale)
-            probs = ex * (1.0 / jnp.sum(ex, axis=1, keepdims=True))
-            low = probs.astype(BF16)
-            ps[rows, :span] = low
-            outs = dot_nn(low, vals).astype(BF16)
-            gp = dot_nt(dos[rows], vals).astype(BF16).astype(F32)
-            rdot = jnp.sum(gp * probs, axis=1, keepdims=True)
-            gs = (probs * (gp - rdot) * score_scale).astype(BF16)
-            dss[rows, :span] = gs
-            gq = dot_nn(gs, keys)
+            sc[s, :, :span] = dot_nt(qs[s, rows], ks[s, :span])
+            gps[s, :, :span] = dot_nt(dos[s, rows], qkv_s[:span, v_at(s)]).astype(BF16)
             for g in range(group):
-                part = outs[g * QB:(g + 1) * QB].reshape(rpb, tl, hd)
-                o_ref[blk * rpb:(blk + 1) * rpb, 0, :, q_at[g]] = part
-                back = rope_back(gq[g * QB:(g + 1) * QB], pl.ds(blk * QB, QB)).reshape(rpb, tl, hd)
-                dqkv_ref[blk * rpb:(blk + 1) * rpb, 0, :, q_at[g]] = back
-        for blk in range(nblk):
+                part = slice(g * QB, (g + 1) * QB)
+                dst = pl.ds(blk * rows_blk + g * QB, QB)
+                scores = sc[s, part, :span]
+                diag = jnp.where(causal, scores[:, span - QB:], -jnp.inf)
+                scores = diag if blk == 0 else jnp.concatenate([scores[:, :span - QB], diag], axis=1)
+                top = jnp.max(scores, axis=1, keepdims=True)
+                ex = jnp.exp2((scores - top) * exp_scale)
+                probs = ex * (1.0 / jnp.sum(ex, axis=1, keepdims=True))
+                ps[s, dst, :span] = probs.astype(BF16)
+                gp = gps[s, part, :span].astype(F32)
+                rdot = jnp.sum(gp * probs, axis=1, keepdims=True)
+                dss[s, dst, :span] = (probs * (gp - rdot) * score_scale).astype(BF16)
+
+        def by_query(s, blk):
+            span = (blk + 1) * QB
+            rows = pl.ds(blk * rows_blk, rows_blk)
+            outs = dot_nn(ps[s, rows, :span], qkv_s[:span, v_at(s)]).astype(BF16)
+            gq = dot_nn(dss[s, rows, :span], ks[s, :span])
+            for g in range(group):
+                part = slice(g * QB, (g + 1) * QB)
+                o_ref[blk * rpb:(blk + 1) * rpb, 0, :, q_at(s, g)] = outs[part].reshape(rpb, tl, hd)
+                back = rope_back(gq[part], pl.ds(blk * QB, QB)).reshape(rpb, tl, hd)
+                dqkv_ref[blk * rpb:(blk + 1) * rpb, 0, :, q_at(s, g)] = back
+
+        def by_key(s, blk):
             rows = pl.ds(blk * rows_blk, (nblk - blk) * rows_blk)
             cols = slice(blk * QB, (blk + 1) * QB)
-            gv = dot_tn(ps[rows, cols], dos[rows]).astype(BF16).reshape(rpb, tl, hd)
-            gk = rope_back(dot_tn(dss[rows, cols], qs[rows]), pl.ds(blk * QB, QB)).reshape(rpb, tl, hd)
-            dqkv_ref[blk * rpb:(blk + 1) * rpb, 0, :, v_at] = gv
-            dqkv_ref[blk * rpb:(blk + 1) * rpb, 0, :, k_at] = gk
-
-        @pl.when((slot == 0) & (b + 1 < nb))
-        def _():
-            relay_far(b + 1)
-
-        @pl.when((slot == 1) & (b + 1 < nb))
+            gv = dot_tn(ps[s, rows, cols], dos[s, rows]).astype(BF16).reshape(rpb, tl, hd)
+            gk = rope_back(dot_tn(dss[s, rows, cols], qs[s, rows]), pl.ds(blk * QB, QB)).reshape(rpb, tl, hd)
+            dqkv_ref[blk * rpb:(blk + 1) * rpb, 0, :, v_at(s)] = gv
+            dqkv_ref[blk * rpb:(blk + 1) * rpb, 0, :, k_at(s)] = gk
+
+        for s in range(lanes):
+            prepare(s)
+        for blk in range(nblk - 1, -1, -1):
+            for work in (softmax, by_query, by_key):
+                for s in range(lanes):
+                    work(s, blk)
+
+        @pl.when((pair == 0) & (b + 1 < nb))
         def _():
             for copy in keep_own(b):
                 copy.wait()
@@ -239,7 +258,13 @@
             load(b + 1)
         return carry
 
-    lax.fori_loop(0, slots, one_slot, 0)
+    @pl.when(b + 1 < nb)
+    def _():
+        relay_far(b + 1)
+
+    lax.fori_loop(0, slots // lanes, one_pair, 0)
+    osend_ref[0] = o_ref[peer, 0]
+    gsend_ref[0] = dqkv_ref[peer, 0]
 
     @pl.when(b == nb - 1)
     def _():
@@ -263,23 +288,27 @@
     slots = k_cols // hd
     group = q_cols // k_cols
     cols = q_cols + 2 * k_cols
+    lanes = math.gcd(2, slots)
     flops = 2 * nb * seq * dim * (cols + q_cols) + 2 * 6 * nb * slots * group * seq * seq * hd
     return pl.pallas_call(
         functools.partial(attend_kernel, ranks, slots, group, hd, nb),
         grid=(nb,),
         in_specs=[ANY] * 5,
         out_specs=[ANY, pl.BlockSpec((ranks, 1, tl, q_cols), lambda b: (0, b, 0, 0)),
-                   pl.BlockSpec((ranks, 1, tl, cols), lambda b: (0, b, 0, 0))],
+                   pl.BlockSpec((ranks, 1, tl, cols), lambda b: (0, b, 0, 0)),
+                   pl.BlockSpec((1, tl, q_cols), lambda b: (b, 0, 0)), pl.BlockSpec((1, tl, cols), lambda b: (b, 0, 0))],
         out_shape=[jax.ShapeDtypeStruct((2, ranks, nb, tl, dim), BF16),
                    jax.ShapeDtypeStruct((ranks, nb, tl, q_cols), BF16),
-                   jax.ShapeDtypeStruct((ranks, nb, tl, cols), BF16)],
+                   jax.ShapeDtypeStruct((ranks, nb, tl, cols), BF16),
+                   jax.ShapeDtypeStruct((nb, tl, q_cols), BF16), jax.ShapeDtypeStruct((nb, tl, cols), BF16)],
         scratch_shapes=[pltpu.VMEM((dim, cols), BF16), pltpu.VMEM((q_cols, dim), BF16),
                         pltpu.VMEM((ranks, tl, dim), BF16), pltpu.VMEM((ranks, tl, dim), BF16),
                         pltpu.VMEM((ranks, tl, hd), F32), pltpu.VMEM((seq, hd), F32), pltpu.VMEM((seq, hd), F32),
                         pltpu.VMEM((seq, cols), BF16), pltpu.VMEM((seq, q_cols), BF16),
-                        pltpu.VMEM((group * seq, hd), BF16), pltpu.VMEM((group * seq, hd), BF16),
-                        pltpu.VMEM((seq, hd), BF16),
-                        pltpu.VMEM((group * seq, seq), BF16), pltpu.VMEM((group * seq, seq), BF16),
+                        pltpu.VMEM((lanes, group * seq, hd), BF16), pltpu.VMEM((lanes, group * seq, hd), BF16),
+                        pltpu.VMEM((lanes, seq, hd), BF16),
+                        pltpu.VMEM((lanes, group * seq, seq), BF16), pltpu.VMEM((lanes, group * seq, seq), BF16),
+                        pltpu.VMEM((lanes, group * QB, seq), F32), pltpu.VMEM((lanes, group * QB, seq), BF16),
                         pltpu.SemaphoreType.DMA((8, nb)), pltpu.SemaphoreType.DMA((8, nb)),
                         pltpu.SemaphoreType.DMA((ranks,)), pltpu.SemaphoreType.DMA((ranks,)),
                         pltpu.SemaphoreType.DMA((5,)), pltpu.SemaphoreType.DMA((2,)), pltpu.SemaphoreType.DMA((2,))],
@@ -342,17 +371,13 @@
     return where
 
 
-def weight_grad_kernel(total, left_at, right_at, chunks, pieces, place_pieces, n_extra, *refs):
+def weight_grad_kernel(total, left_at, right_at, chunks, pieces, placing, n_in, n_out, *refs):
     left_ref, right_ref = refs[0], refs[1]
-    n_in = 2 + n_extra
-    placing = place_pieces is not None
-    n_out = 3 if placing else 2
     outs = refs[n_in:n_in + n_out]
     lbuf, rbuf, acc, sems = refs[n_in + n_out:n_in + n_out + 4]
-    placer = None
-    if placing:
-        placer = Placer(refs[2], outs[2], refs[-2], refs[-1], total, place_pieces)
-        placer.first()
+    extra = refs[n_in + n_out + 4:]
+    placers = [Placer(refs[src], outs[dst], extra[2 * n], extra[2 * n + 1], total, place_pieces)
+               for n, (src, dst, place_pieces) in enumerate(placing)]
 
     def fetch(step, slot):
         return (pltpu.make_async_copy(left_ref.at[left_at(step)], lbuf.at[slot], sems.at[0, slot]),
@@ -364,6 +389,8 @@
 
     for copy in fetch(0, 0):
         copy.start()
+    for placer in placers:
+        placer.first()
     acc[...] = jnp.zeros_like(acc)
 
     def body(step, carry):
@@ -372,23 +399,27 @@
             copy.start()
         for copy in fetch(step, slot):
             copy.wait()
-        if placing:
+        for placer in placers:
             placer.step(step)
         acc[...] += dot_tn(flat(lbuf, slot), flat(rbuf, slot))
         return carry
 
-    lax.fori_loop(0, total - 1, body, 0)
-    for copy in fetch(total - 1, (total - 1) % 2):
-        copy.wait()
-    if placing:
-        placer.step(jnp.int32(total - 1))
+    lax.fori_loop(0, total - 2, body, 0)
+    ends = ((total - 2) % 2, (total - 1) % 2)
+    for copy in fetch(total - 1, ends[1]):
+        copy.start()
+    for n, slot in enumerate(ends):
+        for copy in fetch(total - 2 + n, slot):
+            copy.wait()
+        for placer in placers:
+            placer.step(jnp.int32(total - 2 + n))
     copies = []
-    last = (total - 1) % 2
     part = acc.shape[0] // chunks
     for n in range(chunks):
         rows = pl.ds(n * part, part)
-        val = lbuf[last, :, :, n * part:(n + 1) * part]
-        acc[rows] += dot_tn(val.reshape(-1, part), flat(rbuf, last))
+        for slot in ends:
+            val = lbuf[slot, :, :, n * part:(n + 1) * part]
+            acc[rows] += dot_tn(val.reshape(-1, part), flat(rbuf, slot))
         for m, (out, src_col, width, dst) in enumerate(pieces):
             copy = pltpu.make_async_copy(acc.at[rows, pl.ds(src_col, width)], outs[out].at[dst(n * part, part, width)],
                                          sems.at[2 + m, n])
@@ -396,11 +427,11 @@
             copies.append(copy)
     for copy in copies:
         copy.wait()
-    if placing:
+    for placer in placers:
         placer.last()
 
 
-def weight_grad(left, right, left_sel, right_sel, acc_shape, chunks, pieces, full_struct, carried, place, order, name):
+def weight_grad(left, right, left_sel, right_sel, acc_shape, chunks, pieces, full_struct, carried, places, order, name):
     ranks, nb, tl = right.shape[-4], right.shape[-3], right.shape[-2]
 
     def at(sel, ref):
@@ -413,12 +444,16 @@
     out_shape = [full_struct, jax.ShapeDtypeStruct(acc_shape, F32)]
     scratch = [pltpu.VMEM((2, ranks, tl, left_width), BF16), pltpu.VMEM((2, ranks, tl, right_width), BF16),
                pltpu.VMEM(acc_shape, F32), pltpu.SemaphoreType.DMA((2 + len(pieces), max(2, chunks)))]
-    place_pieces = None
-    if place is not None:
-        recv, full, place_pieces = place
-        operands += [recv, full]
-        aliases[3] = 2
-        out_shape.append(jax.ShapeDtypeStruct(full.shape, F32))
+    placing = []
+    for recv, full, place_pieces in places:
+        src, dst = len(operands), 0
+        operands.append(recv)
+        if full is not None:
+            dst = len(out_shape)
+            aliases[len(operands)] = dst
+            operands.append(full)
+            out_shape.append(jax.ShapeDtypeStruct(full.shape, F32))
+        placing.append((src, dst, place_pieces))
         scratch += [pltpu.VMEM((2, recv.shape[0] // nb, recv.shape[1]), F32),
                     pltpu.SemaphoreType.DMA((1 + len(place_pieces), 2))]
     if carried is not None:
@@ -427,7 +462,7 @@
     operands += order
     rows = ranks * nb * tl
     return pl.pallas_call(
-        functools.partial(weight_grad_kernel, nb, left_at, right_at, chunks, pieces, place_pieces, len(operands) - 2),
+        functools.partial(weight_grad_kernel, nb, left_at, right_at, chunks, pieces, placing, len(operands), len(out_shape)),
         in_specs=[ANY] * len(operands),
         out_specs=[ANY] * len(out_shape),
         out_shape=out_shape,
@@ -454,123 +489,135 @@
     return out
 
 
-def hidden_grad_kernel(parts, place_pieces, w_ref, x_ref, inv_ref, gain_ref, gm_ref, gp_ref, dy_ref, recv_ref, full_in,
-                       dx_ref, dg_ref, full_ref, gfull, dn_s, dys, mean_s, bounce, csem, psem, dsem):
-    del full_in
+def hidden_grad_kernel(parts, w_ref, x_ref, inv_ref, gain_ref, gm_ref, gp_ref, dy_ref, order_ref,
+                       dx_ref, dg_ref, gfull, dn_s, xs, dys, mean_s, csem, dsem):
+    del order_ref
     step = pl.program_id(0)
     steps = pl.num_programs(0)
     nb, tl, dim = dys.shape
     rows = nb * tl
     width = w_ref.shape[0]
-    placer = Placer(recv_ref, full_ref, bounce, psem, recv_ref.shape[0] // bounce.shape[1], place_pieces)
 
     @pl.when(step == 0)
     def _():
         for copy in canonical_copies(gm_ref, gp_ref, gfull, csem, parts):
             copy.start()
-        placer.first()
-        pltpu.make_async_copy(dy_ref, dys, dsem.at[0]).start()
+        pltpu.make_async_copy(x_ref, xs, dsem.at[0]).start()
+        pltpu.make_async_copy(dy_ref, dys, dsem.at[1]).start()
         mean_s[...] = jnp.zeros_like(mean_s)
         for copy in canonical_copies(gm_ref, gp_ref, gfull, csem, parts):
             copy.wait()
 
-    placer.step(step)
-    low = dot_nt(gfull[...].reshape(rows, gfull.shape[-1]), w_ref[...]).astype(BF16)
     at = lane(step, width)
-    dn_s[:, at] = low
-    grad = low.astype(F32)
-    unit = x_ref[:, :, at].reshape(rows, width).astype(F32) * inv_ref[...]
-    mean_s[...] += jnp.sum(grad * gain_ref[:, at] * unit, axis=1, keepdims=True)
-    dg_ref[:, at] = jnp.sum(grad * unit, axis=0, keepdims=True)
+    dn_s[:, at] = dot_nt(gfull[...].reshape(rows, gfull.shape[-1]), w_ref[...]).astype(BF16)
+
+    @pl.when(step == 0)
+    def _():
+        pltpu.make_async_copy(x_ref, xs, dsem.at[0]).wait()
+
+    grad = dn_s[:, at].astype(F32)
+    unit = xs[:, :, at].reshape(rows, width).astype(F32) * inv_ref[...]
+    prod = grad * unit
+    mean_s[...] += jnp.sum(prod * gain_ref[:, at], axis=1, keepdims=True)
+    dg_ref[:, at] = jnp.sum(prod, axis=0, keepdims=True)
 
     @pl.when(step == steps - 1)
     def _():
-        pltpu.make_async_copy(dy_ref, dys, dsem.at[0]).wait()
+        pltpu.make_async_copy(dy_ref, dys, dsem.at[1]).wait()
 
         def finish(i, carry):
-            span = pl.ds(pl.multiple_of(i * tl, tl), tl)
-            inv = inv_ref[span]
-            unit_rows = x_ref[i].astype(F32) * inv
-            inner = inv * (dn_s[span].astype(F32) * gain_ref[...] - unit_rows * (mean_s[span] * (1.0 / dim)))
-            dys[i] = (dys[i].astype(F32) + inner).astype(BF16)
-            pltpu.make_async_copy(dys.at[i], dx_ref.at[i], dsem.at[1]).start()
+            for sub in range(tl // 16):
+                here = pl.ds(sub * 16, 16)
+                span = pl.ds(pl.multiple_of(i * tl + sub * 16, 16), 16)
+                inv = inv_ref[span]
+                unit_rows = xs[i, here].astype(F32) * inv
+                inner = inv * (dn_s[span].astype(F32) * gain_ref[...] - unit_rows * (mean_s[span] * (1.0 / dim)))
+                dys[i, here] = (dys[i, here].astype(F32) + inner).astype(BF16)
+            pltpu.make_async_copy(dys.at[i], dx_ref.at[i], dsem.at[2]).start()
             return carry
         lax.fori_loop(0, nb, finish, 0)
-        placer.last()
-        pltpu.make_async_copy(dys, dx_ref, dsem.at[1]).wait()
-
-
-def hidden_grad(hidden, grad_out, inv_rms, norm_weight, w_qkv, g_all, g_pair, recv, full, parts, place_pieces):
+        pltpu.make_async_copy(dys, dx_ref, dsem.at[2]).wait()
+
+
+def hidden_grad(hidden, grad_out, inv_rms, norm_weight, w_qkv, g_all, g_pair, parts, order):
     nb, tl, dim = hidden.shape
     cols = w_qkv.shape[1]
     width = 512
-    steps = dim // width
     const = lambda *shape: pl.BlockSpec(shape, lambda n: (0,) * len(shape), pipeline_mode=pl.Buffered(1))
     return pl.pallas_call(
-        functools.partial(hidden_grad_kernel, parts, place_pieces),
-        grid=(steps,),
-        in_specs=[pl.BlockSpec((width, cols), lambda n: (n, 0)), const(nb, tl, dim), const(nb * tl, 1), const(1, dim),
-                  ANY, ANY, ANY, ANY, ANY],
-        out_specs=[ANY, const(1, dim), ANY],
-        out_shape=[jax.ShapeDtypeStruct((nb, tl, dim), BF16), jax.ShapeDtypeStruct((1, dim), F32),
-                   jax.ShapeDtypeStruct(full.shape, F32)],
+        functools.partial(hidden_grad_kernel, parts),
+        grid=(dim // width,),
+        in_specs=[pl.BlockSpec((width, cols), lambda n: (n, 0)), ANY, const(nb * tl, 1), const(1, dim),
+                  ANY, ANY, ANY, ANY],
+        out_specs=[ANY, const(1, dim)],
+        out_shape=[jax.ShapeDtypeStruct((nb, tl, dim), BF16), jax.ShapeDtypeStruct((1, dim), F32)],
         scratch_shapes=[pltpu.VMEM((nb, tl, cols), BF16), pltpu.VMEM((nb * tl, dim), BF16), pltpu.VMEM((nb, tl, dim), BF16),
-                        pltpu.VMEM((nb * tl, 1), F32), pltpu.VMEM((2, recv.shape[0] // steps, recv.shape[1]), F32),
-                        pltpu.SemaphoreType.DMA((len(parts), 2)), pltpu.SemaphoreType.DMA((1 + len(place_pieces), 2)),
-                        pltpu.SemaphoreType.DMA((2,))],
-        input_output_aliases={8: 2},
+                        pltpu.VMEM((nb, tl, dim), BF16), pltpu.VMEM((nb * tl, 1), F32),
+                        pltpu.SemaphoreType.DMA((len(parts), 2)), pltpu.SemaphoreType.DMA((3,))],
         compiler_params=pltpu.CompilerParams(dimension_semantics=("arbitrary",), vmem_limit_bytes=VMEM_LIMIT),
-        cost_estimate=pl.CostEstimate(flops=2 * nb * tl * dim * cols, bytes_accessed=2 * dim * cols + 8 * recv.size,
-                                      transcendentals=0),
+        cost_estimate=pl.CostEstimate(flops=2 * nb * tl * dim * cols, bytes_accessed=2 * dim * cols, transcendentals=0),
         name="hidden_grad",
-    )(w_qkv, hidden, inv_rms, norm_weight, g_all, g_pair, grad_out, recv, full)
-
-
-def project_out_kernel(parts, place_pieces, w_ref, x_ref, om_ref, op_ref, recv_ref, full_in, y_ref, full_ref,
-                       ofull, bounce, csem, psem):
-    del full_in
-    step = pl.program_id(0)
-    steps = pl.num_programs(0)
+    )(w_qkv, hidden, inv_rms, norm_weight, g_all, g_pair, grad_out, order)
+
+
+def project_out_kernel(parts, w_ref, x_ref, om_ref, op_ref, order_ref, y_ref, ofull, csem):
+    del order_ref
     nb, tl, q_dim = ofull.shape
-    placer = Placer(recv_ref, full_ref, bounce, psem, recv_ref.shape[0] // bounce.shape[1], place_pieces)
-
-    @pl.when(step == 0)
+
+    @pl.when(pl.program_id(0) == 0)
     def _():
         for copy in canonical_copies(om_ref, op_ref, ofull, csem, parts):
             copy.start()
-        placer.first()
         for copy in canonical_copies(om_ref, op_ref, ofull, csem, parts):
             copy.wait()
 
-    placer.step(step)
     mixed = dot_nn(ofull[...].reshape(nb * tl, q_dim), w_ref[...])
     y_ref[...] = (x_ref[...].astype(F32) + mixed.reshape(y_ref.shape)).astype(BF16)
 
-    @pl.when(step == steps - 1)
-    def _():
-        placer.last()
-
-
-def project_out(hidden, w_out, o_all, o_pair, recv, full, parts, place_pieces):
+
+def project_out(hidden, w_out, o_all, o_pair, parts, order):
     nb, tl, dim = hidden.shape
     q_dim = w_out.shape[0]
     width = 512
-    steps = dim // width
     tile = pl.BlockSpec((nb, tl, width), lambda n: (0, 0, n))
     return pl.pallas_call(
-        functools.partial(project_out_kernel, parts, place_pieces),
-        grid=(steps,),
-        in_specs=[pl.BlockSpec((q_dim, width), lambda n: (0, n)), tile, ANY, ANY, ANY, ANY],
-        out_specs=[tile, ANY],
-        out_shape=[jax.ShapeDtypeStruct((nb, tl, dim), BF16), jax.ShapeDtypeStruct(full.shape, F32)],
-        scratch_shapes=[pltpu.VMEM((nb, tl, q_dim), BF16), pltpu.VMEM((2, recv.shape[0] // steps, recv.shape[1]), F32),
-                        pltpu.SemaphoreType.DMA((len(parts), 2)), pltpu.SemaphoreType.DMA((1 + len(place_pieces), 2))],
-        input_output_aliases={5: 1},
+        functools.partial(project_out_kernel, parts),
+        grid=(dim // width,),
+        in_specs=[pl.BlockSpec((q_dim, width), lambda n: (0, n)), tile, ANY, ANY, ANY],
+        out_specs=tile,
+        out_shape=jax.ShapeDtypeStruct((nb, tl, dim), BF16),
+        scratch_shapes=[pltpu.VMEM((nb, tl, q_dim), BF16), pltpu.SemaphoreType.DMA((len(parts), 2))],
         compiler_params=pltpu.CompilerParams(dimension_semantics=("arbitrary",), vmem_limit_bytes=VMEM_LIMIT),
-        cost_estimate=pl.CostEstimate(flops=2 * nb * tl * dim * q_dim, bytes_accessed=2 * dim * q_dim + 8 * recv.size,
-                                      transcendentals=0),
+        cost_estimate=pl.CostEstimate(flops=2 * nb * tl * dim * q_dim, bytes_accessed=2 * dim * q_dim, transcendentals=0),
         name="project_out",
-    )(w_out, hidden, o_all, o_pair, recv, full)
+    )(w_out, hidden, o_all, o_pair, order)
+
+
+def place_kernel(steps, place_pieces, recv_ref, full_in, full_ref, bounce, sems):
+    del full_in
+    placer = Placer(recv_ref, full_ref, bounce, sems, steps, place_pieces)
+    placer.first()
+
+    def body(step, carry):
+        placer.step(step)
+        return carry
+    lax.fori_loop(0, steps, body, 0)
+    placer.last()
+
+
+def place(recv, full, place_pieces, steps):
+    return pl.pallas_call(
+        functools.partial(place_kernel, steps, place_pieces),
+        in_specs=[ANY, ANY],
+        out_specs=ANY,
+        out_shape=jax.ShapeDtypeStruct(full.shape, F32),
+        scratch_shapes=[pltpu.VMEM((2, recv.shape[0] // steps, recv.shape[1]), F32),
+                        pltpu.SemaphoreType.DMA((1 + len(place_pieces), 2))],
+        input_output_aliases={1: 0},
+        compiler_params=pltpu.CompilerParams(vmem_limit_bytes=VMEM_LIMIT),
+        cost_estimate=pl.CostEstimate(flops=recv.size, bytes_accessed=8 * recv.size, transcendentals=0),
+        name="place",
+    )(recv, full)
 
 
 def group_sum_kernel(ranks, part_ref, sum_ref, parts, ssem, rsem):
@@ -616,22 +663,16 @@
     hd = 2 * long_factor.shape[0]
     q_dim = w_out.shape[0]
     kv_dim = (w_qkv.shape[1] - q_dim) // 2
-    me = lax.axis_index('sp')
-    other = me + 1 - 2 * lax.rem(me, 2)
     pair = [(i, i ^ 1) for i in range(ranks)]
     qh, kh = q_dim // 2, kv_dim // 2
 
     hidden_wide = hidden.astype(F32)
     inv_rms = lax.rsqrt(jnp.mean(hidden_wide * hidden_wide, axis=-1, keepdims=True) + NORM_EPS)
     normed = (hidden_wide * inv_rms * norm_weight).astype(BF16)
-    gathered, o_all, g_all = attend(normed, grad_out, w_qkv, w_out, half_tables(positions, long_factor), ranks)
-    o_pair = lax.ppermute(lax.dynamic_index_in_dim(o_all, other, 0, keepdims=False), 'sp', pair)
-    g_pair = lax.ppermute(lax.dynamic_index_in_dim(g_all, other, 0, keepdims=False), 'sp', pair)
-
-    half = (qh + 2 * kh) // 2
-    q_left = qh - half
-    dwq_struct = jax.ShapeDtypeStruct(w_qkv.shape, F32)
-    dwo_struct = jax.ShapeDtypeStruct(w_out.shape, F32)
+    gathered, o_all, g_all, o_send, g_send = attend(normed, grad_out, w_qkv, w_out,
+                                                    half_tables(positions, long_factor), ranks)
+    o_pair = lax.ppermute(o_send, 'sp', pair)
+    g_pair = lax.ppermute(g_send, 'sp', pair)
 
     def own_cols(base, stride):
         def where(row, rows, width):
@@ -646,25 +687,26 @@
     def same(row, rows, width):
         return (pl.ds(row, rows), pl.ds(0, width))
 
+    dwq_struct = jax.ShapeDtypeStruct(w_qkv.shape, F32)
+    dwo_struct = jax.ShapeDtypeStruct(w_out.shape, F32)
+    dwq, send_q = weight_grad(gathered, g_all, ("plane", 0), ("cols", 0, qh), (dim, qh), 4,
+                              [(0, 0, qh, own_cols(0, qh)), (1, 0, qh, same)], dwq_struct, None, [], [], "wgrad_q")
+    recv_q = lax.ppermute(send_q, 'sp', pair)
     dwo, send_o = weight_grad(o_all, gathered, ("cols", 0, qh), ("plane", 1), (qh, dim), 4,
-                              [(0, 0, dim, own_rows(qh)), (1, 0, dim, same)], dwo_struct, None, None, [], "wgrad_out")
+                              [(0, 0, dim, own_rows(qh)), (1, 0, dim, same)], dwo_struct, None, [], [dwq, o_pair, g_pair],
+                              "wgrad_out")
     recv_o = lax.ppermute(send_o, 'sp', pair)
-    dwq, send_a = weight_grad(gathered, g_all, ("plane", 0), ("cols", 0, half), (dim, half), 4,
-                              [(0, 0, half, own_cols(0, qh)), (1, 0, half, same)], dwq_struct, None, None, [dwo],
-                              "wgrad_qkv_a")
-    recv_a = lax.ppermute(send_a, 'sp', pair)
-    dwq, send_b, dwo = weight_grad(gathered, g_all, ("plane", 0), ("cols", half, half), (dim, half), 4,
-                                   [(0, 0, q_left, own_cols(half, qh)), (0, q_left, kh, own_cols(q_dim, kh)),
-                                    (0, q_left + kh, kh, own_cols(q_dim + kv_dim, kh)), (1, 0, half, same)],
-                                   dwq_struct, dwq, (recv_o, dwo, [(0, dim, peer_rows(qh))]), [o_pair, g_pair], "wgrad_qkv_b")
-    recv_b = lax.ppermute(send_b, 'sp', pair)
-    grad_hidden, grad_norm, dwq = hidden_grad(
-        hidden, grad_out, inv_rms.reshape(nb * tl, 1), norm_weight[None], w_qkv, g_all, g_pair, recv_a, dwq,
-        [qh, kh, kh], [(0, half, peer_cols(0, qh))])
-    out_hidden, dwq = project_out(
-        hidden, w_out, o_all, o_pair, recv_b, dwq, [qh],
-        [(0, q_left, peer_cols(half, qh)), (q_left, kh, peer_cols(q_dim, kh)), (q_left + kh, kh, peer_cols(q_dim + kv_dim, kh))])
+    grad_hidden, grad_norm = hidden_grad(hidden, grad_out, inv_rms.reshape(nb * tl, 1), norm_weight[None], w_qkv, g_all,
+                                         g_pair, [qh, kh, kh], dwo)
+    dwq, send_kv, dwo = weight_grad(gathered, g_all, ("plane", 0), ("cols", qh, 2 * kh), (dim, 2 * kh), 4,
+                                    [(0, 0, kh, own_cols(q_dim, kh)), (0, kh, kh, own_cols(q_dim + kv_dim, kh)),
+                                     (1, 0, 2 * kh, same)], dwq_struct, dwq,
+                                    [(recv_o, dwo, [(0, dim, peer_rows(qh))]), (recv_q, None, [(0, qh, peer_cols(0, qh))])],
+                                    [grad_norm], "wgrad_kv")
+    recv_kv = lax.ppermute(send_kv, 'sp', pair)
     grad_norm = group_sum(grad_norm.reshape(-1, 128), ranks).reshape(-1)
+    out_hidden = project_out(hidden, w_out, o_all, o_pair, [qh], send_kv)
+    dwq = place(recv_kv, dwq, [(0, kh, peer_cols(q_dim, kh)), (kh, kh, peer_cols(q_dim + kv_dim, kh))], 8)
     return out_hidden, grad_hidden, grad_norm, dwq, dwo
 
 

time: 890 us -> 865 us (0.972)
  Pallas kernels: 857 us -> 838 us
  local copies, waits for them, and re-layouts: 11 us -> 1.88 us
    pallas_call x1, Pallas kernels: 498 us -> 470 us  [attend(): pl.pallas_call(functools.partial(attend_kernel, ranks, slots, group, hd,...]
    pallas_call x1, Pallas kernels: 6.01 us -> 19.6 us  [group_sum(): pl.pallas_call(functools.partial(group_sum_kernel, ranks), in_specs=[ANY]...]
    squeeze x2 -> x0, local copies, waits for them, and re-layouts: 9.14 us -> none  [the longest x1 5.31 us: block_body(): lax.dynamic_index_in_dim(g_all, other, 0, keepdims=False)]
    pallas_call x2 -> x3, Pallas kernels: 95.2 us -> 97 us  [the longest x1 53.5 us: hidden_grad(): pl.pallas_call(functools.partial(hidden_grad_kernel, parts), grid=(dim //...]
  transfers between devices with their start and end apart: 5 -> 5, of which waited for: 0 -> 0; matrix products, arithmetic and copies ran while one was open for 1% -> 0% of each run, Pallas kernels for 26% -> 33%
where the time goes in v3:
time: 865 us; the launch traced here: 860 us
  Pallas kernels  838 us (97%)
  other arithmetic  14.3 us (2%)
    pallas_call x1, Pallas kernels, attend(): pl.pallas_call(functools.partial(attend_kernel, ranks, slots, group, hd,...  470 us
    pallas_call x3, Pallas kernels, weight_grad(): pl.pallas_call(functools.partial(weight_grad_kernel, nb, left_at, right_a...  252 us
    pallas_call x1, Pallas kernels, hidden_grad(): pl.pallas_call(functools.partial(hidden_grad_kernel, parts), grid=(dim //...  53.5 us
    pallas_call x1, Pallas kernels, project_out(): pl.pallas_call(functools.partial(project_out_kernel, parts), grid=(dim //...  27.1 us
    pallas_call x1, Pallas kernels, group_sum(): pl.pallas_call(functools.partial(group_sum_kernel, ranks), in_specs=[ANY]...  19.6 us
  transfers between devices with their start and end apart: 5, of which 0 were waited for; matrix products, arithmetic and copies ran while one was open for 0% of the time, Pallas kernels for 33%

profile of v3, /device:TPU:113, one launch (start us, length us, event | category | flops | bytes accessed | tf_op | source)
XLA Modules:
  0.0 860.1 jit_solution(5201259746259033420)
XLA Ops:
  0.6 0.7 convert_element_type.14
  1.3 0.7 multiply_divide_fusion
  2.0 4.1 fusion
  6.1 0.0 copy-start
  6.1 0.2 fusion.3
  6.3 0.7 pad_maximum_fusion.tab_ref
  7.0 0.0 copy-done
  7.0 8.0 fusion.2.rn_ref
  15.0 469.6 %attend.1 = (bf16[2,8,16,64,3072]{4,3,2,1,0:T(8,128)(2,1)}, bf16[8,16,64,1536]{3,2,1,0:T(8,128)(2,1)}, bf16[8,16,64,2560]{3,2,1,0:T(8,128)(2,1)}, bf16[16,64,1536]{2,1,0:T(8,128)(2,1)}, bf16[16,64,2560]{2,1,0:T(8,128)(2,1)}) custom-call(bf16[16,64,3072]{2,1,0:T(8,128)(2,1)} %fusion.2.rn_ref, bf16[16,64,3072]{2,1,0:T(8,128)(2,1)} %dy_ref.3, ...), custom_call_target="tpu_custom_call" | custom-call | flops 283467841536 | bytes 268435456 | tf_op jit(solution)/shard_map/attend/pallas_call | solution.py:293
  484.6 3.3 collective-permute-start.1
  487.9 0.1 collective-permute-start
  488.0 91.4 %wgrad_q.1 = (f32[3072,5120]{1,0:T(8,128)}, f32[3072,1536]{1,0:T(8,128)}) custom-call(bf16[2,8,16,64,3072]{4,3,2,1,0:T(8,128)(2,1)} %get-tuple-element.21.refs_0_.refs_1_, bf16[8,16,64,2560]{3,2,1,0:T(8,128)(2,1)} %get-tuple-element.22.refs_1_.gm_ref), custom_call_target="tpu_custom_call" | custom-call | flops 77309411328 | bytes 113246208 | tf_op jit(solution)/shard_map/wgrad_q/pallas_call | solution.py:464
  579.4 0.5 collective-permute-start.3
  579.9 0.0 collective-permute-done.refs_3_.op_ref
  579.9 0.0 collective-permute-done.1.refs_4_.gp_ref
  579.9 0.0 copy-start.1
  579.9 90.2 %wgrad_out.1 = (f32[3072,3072]{1,0:T(8,128)}, f32[1536,3072]{1,0:T(8,128)}) custom-call(bf16[8,16,64,1536]{3,2,1,0:T(8,128)(2,1)} %get-tuple-element.19.refs_0_.om_ref, bf16[2,8,16,64,3072]{4,3,2,1,0:T(8,128)(2,1)} %get-tuple-element.21.refs_0_.refs_1_, f32[3072,5120]{1,0:T(8,128)} %get-tuple-element.23.refs_2_.refs_5_, ...), custom_call_target="tpu_custom_call" | custom-call | flops 77309411328 | bytes 113246208 | tf_op jit(solution)/shard_map/wgrad_out/pallas_call | solution.py:464
  670.1 0.2 collective-permute-start.2
  670.3 0.0 copy-done.1
  670.3 1.3 rsqrt.20.inv_ref
  671.6 53.5 %hidden_grad.1 = (bf16[16,64,3072]{2,1,0:T(8,128)(2,1)}, f32[1,3072]{1,0:T(1,128)}) custom-call(bf16[3072,5120]{1,0:T(8,128)(2,1)} %w_ref.2, bf16[16,64,3072]{2,1,0:T(8,128)(2,1)} %x_ref.3, f32[1024,1]{1,0:T(8,128)} %rsqrt.20.inv_ref, f32[1,3072]{1,0:T(1,128)} %bitcast.3, bf16[8,16,64,2560]{3,2,1,0:T(8,128)(2,1)} %get-tuple-element.22.refs_1_.gm_ref, ...), custom_call_target="tpu_custom_call" | custom-call | flops 32212254720 | bytes 31457280 | tf_op jit(solution)/shard_map/hidden_grad/pallas_call | solution.py:547
  725.1 0.0 collective-permute-done.3.refs_4_
  725.1 0.0 collective-permute-done.2.refs_2_
  725.1 70.5 %wgrad_kv.1 = (f32[3072,5120]{1,0:T(8,128)}, f32[3072,1024]{1,0:T(8,128)}, f32[3072,3072]{1,0:T(8,128)}) custom-call(bf16[2,8,16,64,3072]{4,3,2,1,0:T(8,128)(2,1)} %get-tuple-element.21.refs_0_.refs_1_, bf16[8,16,64,2560]{3,2,1,0:T(8,128)(2,1)} %get-tuple-element.22.refs_1_.gm_ref, ...), custom_call_target="tpu_custom_call", output_to_operand_aliasing={{2}: (3, {}), {0}: (5, {})} | custom-call | flops 51539607552 | bytes 92274688 | tf_op jit(solution)/shard_map/wgrad_kv/pallas_call | solution.py:464
  795.6 0.5 collective-permute-start.4
  796.1 19.6 %group_sum.1 = f32[24,128]{1,0:T(8,128)} custom-call(f32[24,128]{1,0:T(8,128)} %bitcast.4), custom_call_target="tpu_custom_call" | custom-call | flops 24576 | bytes 196608 | tf_op jit(solution)/shard_map/group_sum/pallas_call | solution.py:648
  815.7 27.1 %project_out.1 = bf16[16,64,3072]{2,1,0:T(8,128)(2,1)} custom-call(bf16[3072,3072]{1,0:T(8,128)(2,1)} %w_ref.3, bf16[16,64,3072]{2,1,0:T(8,128)(2,1)} %x_ref.3, bf16[8,16,64,1536]{3,2,1,0:T(8,128)(2,1)} %get-tuple-element.19.refs_0_.om_ref, bf16[16,64,1536]{2,1,0:T(8,128)(2,1)} %collective-permute-done.refs_3_.op_ref, f32[3072,1024]{1,0:T(8,128)} %get-tuple-element.29.order_ref), custom_call_target="tpu_custom_call" | custom-call | flops 19327352832 | bytes 18874368 | tf_op jit(solution)/shard_map/project_out/pallas_call | solution.py:583
  842.8 0.0 collective-permute-done.4.recv_ref
  842.8 0.0 copy-start.2
  842.8 16.4 %place.1 = f32[3072,5120]{1,0:T(8,128)} custom-call(f32[3072,1024]{1,0:T(8,128)} %collective-permute-done.4.recv_ref, f32[3072,5120]{1,0:T(8,128)} %get-tuple-element.31.full_in), custom_call_target="tpu_custom_call", output_to_operand_aliasing={{}: (1, {})} | custom-call | flops 3145728 | bytes 25165824 | tf_op jit(solution)/shard_map/place/pallas_call | solution.py:609
  859.2 0.0 copy-done.2
  859.3 0.6 copy.20
  (1 shorter events, 0.0 us)
Async XLA Ops:
  6.1 0.9 copy-start
  484.6 95.3 %collective-permute-start.1 = (bf16[16,64,2560]{2,1,0:T(8,128)(2,1)}, bf16[16,64,2560]{2,1,0:T(8,128)(2,1)}, u32[]{:S(2)}, u32[]{:S(2)}) collective-permute-start(bf16[16,64,2560]{2,1,0:T(8,128)(2,1)} %get-tuple-element.24), channel_id=1, source_target_pairs={{0,1},{1,0},{2,3},{3,2},{4,5},{5,4},{6,7},{7,6},{8,9},{9,8},{10,11... | collective-permute-start | bytes 15728648 | tf_op jit(solution)/shard_map/ppermute | solution.py:675
  487.9 92.0 %collective-permute-start = (bf16[16,64,1536]{2,1,0:T(8,128)(2,1)}, bf16[16,64,1536]{2,1,0:T(8,128)(2,1)}, u32[]{:S(2)}, u32[]{:S(2)}) collective-permute-start(bf16[16,64,1536]{2,1,0:T(8,128)(2,1)} %get-tuple-element.20), channel_id=1, source_target_pairs={{0,1},{1,0},{2,3},{3,2},{4,5},{5,4},{6,7},{7,6},{8,9},{9,8},{10,11... | collective-permute-start | bytes 9437192 | tf_op jit(solution)/shard_map/ppermute | solution.py:674
  579.4 145.7 %collective-permute-start.3 = (f32[3072,1536]{1,0:T(8,128)}, f32[3072,1536]{1,0:T(8,128)}, u32[]{:S(2)}, u32[]{:S(2)}) collective-permute-start(f32[3072,1536]{1,0:T(8,128)} %get-tuple-element.27), channel_id=1, source_target_pairs={{0,1},{1,0},{2,3},{3,2},{4,5},{5,4},{6,7},{7,6},{8,9},{9,8},{10,11... | collective-permute-start | bytes 56623112 | tf_op jit(solution)/shard_map/ppermute | solution.py:694
  579.9 90.4 %copy-start.1 = (f32[16,64]{1,0:T(8,128)S(1)}, f32[16,64]{1,0:T(8,128)}, u32[]{:S(2)}) copy-start(f32[16,64]{1,0:T(8,128)} %copy-done) | copy-start | bytes 12292
  670.1 54.9 %collective-permute-start.2 = (f32[1536,3072]{1,0:T(8,128)}, f32[1536,3072]{1,0:T(8,128)}, u32[]{:S(2)}, u32[]{:S(2)}) collective-permute-start(f32[1536,3072]{1,0:T(8,128)} %get-tuple-element.25), channel_id=1, source_target_pairs={{0,1},{1,0},{2,3},{3,2},{4,5},{5,4},{6,7},{7,6},{8,9},{9,8},{10,11... | collective-permute-start | bytes 56623112 | tf_op jit(solution)/shard_map/ppermute | solution.py:698
  795.6 47.2 %collective-permute-start.4 = (f32[3072,1024]{1,0:T(8,128)}, f32[3072,1024]{1,0:T(8,128)}, u32[]{:S(2)}, u32[]{:S(2)}) collective-permute-start(f32[3072,1024]{1,0:T(8,128)} %get-tuple-element.29.order_ref), channel_id=1, source_target_pairs={{0,1},{1,0},{2,3},{3,2},{4,5},{5,4},{6,7},{7,6},{8,9},{9,8},{10,11... | collective-permute-start | bytes 37748744 | tf_op jit(solution)/shard_map/ppermute | solution.py:706
  842.8 16.5 %copy-start.2 = (f32[24,128]{1,0:T(8,128)S(1)}, f32[24,128]{1,0:T(8,128)}, u32[]{:S(2)}) copy-start(f32[24,128]{1,0:T(8,128)} %group_sum.1) | copy-start | bytes 36868

commit v4 on v3

--- a/solution.py
+++ b/solution.py
@@ -46,11 +46,11 @@
     return jnp.concatenate([jnp.cos(angles) * ROPE_SCALE, jnp.sin(angles) * ROPE_SCALE], axis=-1)
 
 
-def attend_kernel(ranks, slots, group, hd, nb, rn_ref, dy_ref, wqkv_ref, wout_ref, tab_ref, gath_ref, o_ref, dqkv_ref, osend_ref, gsend_ref,
+def attend_kernel(ranks, slots, group, hd, nb, x_ref, gain_ref, dy_ref, wqkv_ref, wout_ref, tab_ref, gath_ref, rn_ref, inv_ref, o_ref, dqkv_ref, osend_ref, gsend_ref,
                   wq_s, wo_s, rbuf, dbuf, tabs, cos_s, sin_s, qkv_s, do_s, qs, dos, ks, ps, dss, sc, gps,
-                  ssem, rsem, tsend, trecv, wsem, lsem, gsem):
+                  ssem, rsem, tsend, trecv, wsem, lsem, gsem, xsem, nsem):
     b = pl.program_id(0)
-    tl, dim = rn_ref.shape[1], rn_ref.shape[2]
+    tl, dim = dy_ref.shape[1], dy_ref.shape[2]
     seq = ranks * tl
     q_cols, k_cols = slots * group * hd, slots * hd
     q_dim, kv_dim = 2 * q_cols, 2 * k_cols
@@ -68,10 +68,30 @@
     def both(rank, at):
         return gath_ref.at[:, rank, at]
 
+    def direct_part(at, which):
+        source = dy_ref if which else rn_ref
+        for kind, target in ((0, right), (1, left), (4, peer)):
+            rcopy(source.at[at], gath_ref.at[which, me, at], kind, at, target).start()
+
     def direct(at):
-        for kind, target in ((0, right), (1, left), (4, peer)):
-            rcopy(rn_ref.at[at], gath_ref.at[0, me, at], kind, at, target).start()
-            rcopy(dy_ref.at[at], gath_ref.at[1, me, at], kind, at, target).start()
+        direct_part(at, 0)
+        direct_part(at, 1)
+
+    def x_load(at):
+        slot = lax.rem(at, ranks)
+        return pltpu.make_async_copy(x_ref.at[at], dbuf.at[slot], xsem.at[slot])
+
+    def norm_store(at):
+        slot = lax.rem(at, ranks)
+        return pltpu.make_async_copy(rbuf.at[slot], rn_ref.at[at], nsem.at[slot])
+
+    def norm(at):
+        slot = lax.rem(at, ranks)
+        x_load(at).wait()
+        wide = dbuf[slot].astype(F32)
+        inv = lax.rsqrt(jnp.mean(wide * wide, axis=1, keepdims=True) + NORM_EPS)
+        inv_ref[pl.ds(pl.multiple_of(at * tl, tl), tl)] = inv
+        rbuf[slot] = (wide * inv * gain_ref[...]).astype(BF16)
 
     def relay_near(at):
         rcopy(both(left, at), both(left, at), 0, at, me).wait_recv()
@@ -122,13 +142,53 @@
             copy.start()
         own_table = pltpu.make_async_copy(tab_ref, tabs.at[me], wsem.at[4])
         own_table.start()
+        first = min(nb, ranks)
+        for at in range(first):
+            x_load(at).start()
         barrier = pltpu.get_barrier_semaphore()
         for step in range(1, ranks):
             pl.semaphore_signal(barrier, inc=1, device_id={'sp': lax.rem(me + step, ranks)}, device_id_type=MESH)
         pl.semaphore_wait(barrier, ranks - 1)
-        direct(0)
+        direct_part(0, 1)
+        norm(0)
+        norm(1)
+        norm_store(0).start()
+        norm_store(1).start()
+        norm_store(0).wait()
+        direct_part(0, 0)
         for step in range(1, ranks):
             table_copy(lax.rem(me + step, ranks)).start()
+
+        def norm_more(at, carry):
+            norm(at)
+
+            @pl.when(at >= 3)
+            def _():
+                norm_store(at - 1).start()
+            return carry
+        lax.fori_loop(2, first, norm_more, 0)
+        norm_store(first - 1).start()
+        if nb > ranks:
+            norm_store(1).wait()
+            for at in range(2, ranks):
+                norm_store(at).wait()
+            for at in range(ranks, nb):
+                x_load(at).start()
+
+            def norm_rest(at, carry):
+                norm(at)
+
+                @pl.when(at >= ranks + 1)
+                def _():
+                    norm_store(at - 1).start()
+                return carry
+            lax.fori_loop(ranks, nb, norm_rest, 0)
+            norm_store(nb - 1).start()
+            for at in range(ranks, nb):
+                norm_store(at).wait()
+        else:
+            for at in range(1, nb):
+                norm_store(at).wait()
         relay_near(0)
         direct(1)
         direct(2)
@@ -280,8 +340,8 @@
         lax.fori_loop(0, nb, drain, 0)
 
 
-def attend(normed, grad_out, w_qkv, w_out, table, ranks):
-    nb, tl, dim = normed.shape
+def attend(hidden, norm_weight, grad_out, w_qkv, w_out, table, ranks):
+    nb, tl, dim = hidden.shape
     hd = table.shape[1]
     seq = ranks * tl
     q_cols, k_cols = w_out.shape[0] // 2, (w_qkv.shape[1] - w_out.shape[0]) // 4
@@ -293,11 +353,12 @@
     return pl.pallas_call(
         functools.partial(attend_kernel, ranks, slots, group, hd, nb),
         grid=(nb,),
-        in_specs=[ANY] * 5,
-        out_specs=[ANY, pl.BlockSpec((ranks, 1, tl, q_cols), lambda b: (0, b, 0, 0)),
+        in_specs=[ANY, pl.BlockSpec((1, dim), lambda b: (0, 0), pipeline_mode=pl.Buffered(1))] + [ANY] * 4,
+        out_specs=[ANY, ANY, pl.BlockSpec((nb * tl, 1), lambda b: (0, 0)), pl.BlockSpec((ranks, 1, tl, q_cols), lambda b: (0, b, 0, 0)),
                    pl.BlockSpec((ranks, 1, tl, cols), lambda b: (0, b, 0, 0)),
                    pl.BlockSpec((1, tl, q_cols), lambda b: (b, 0, 0)), pl.BlockSpec((1, tl, cols), lambda b: (b, 0, 0))],
-        out_shape=[jax.ShapeDtypeStruct((2, ranks, nb, tl, dim), BF16),
+        out_shape=[jax.ShapeDtypeStruct((2, ranks, nb, tl, dim), BF16), jax.ShapeDtypeStruct((nb, tl, dim), BF16),
+                   jax.ShapeDtypeStruct((nb * tl, 1), F32),
                    jax.ShapeDtypeStruct((ranks, nb, tl, q_cols), BF16),
                    jax.ShapeDtypeStruct((ranks, nb, tl, cols), BF16),
                    jax.ShapeDtypeStruct((nb, tl, q_cols), BF16), jax.ShapeDtypeStruct((nb, tl, cols), BF16)],
@@ -311,13 +372,14 @@
                         pltpu.VMEM((lanes, group * QB, seq), F32), pltpu.VMEM((lanes, group * QB, seq), BF16),
                         pltpu.SemaphoreType.DMA((8, nb)), pltpu.SemaphoreType.DMA((8, nb)),
                         pltpu.SemaphoreType.DMA((ranks,)), pltpu.SemaphoreType.DMA((ranks,)),
-                        pltpu.SemaphoreType.DMA((5,)), pltpu.SemaphoreType.DMA((2,)), pltpu.SemaphoreType.DMA((2,))],
+                        pltpu.SemaphoreType.DMA((5,)), pltpu.SemaphoreType.DMA((2,)), pltpu.SemaphoreType.DMA((2,)),
+                        pltpu.SemaphoreType.DMA((ranks,)), pltpu.SemaphoreType.DMA((ranks,))],
         compiler_params=pltpu.CompilerParams(dimension_semantics=("arbitrary",), vmem_limit_bytes=VMEM_LIMIT,
                                              collective_id=0, has_side_effects=True),
         cost_estimate=pl.CostEstimate(flops=flops, bytes_accessed=2 * nb * seq * (4 * dim + cols + q_cols),
                                       transcendentals=nb * slots * group * seq * seq),
         name="attend",
-    )(normed, grad_out, w_qkv, w_out, table)
+    )(hidden, norm_weight, grad_out, w_qkv, w_out, table)
 
 
 class Placer:
@@ -593,16 +655,32 @@
     )(w_out, hidden, o_all, o_pair, order)
 
 
-def place_kernel(steps, place_pieces, recv_ref, full_in, full_ref, bounce, sems):
+def place_kernel(steps, place_pieces, recv_ref, full_in, full_ref, bounce, tsem, psem):
     del full_in
-    placer = Placer(recv_ref, full_ref, bounce, sems, steps, place_pieces)
-    placer.first()
-
-    def body(step, carry):
-        placer.step(step)
-        return carry
-    lax.fori_loop(0, steps, body, 0)
-    placer.last()
+    depth, rows = bounce.shape[0], bounce.shape[1]
+
+    def take(n):
+        return pltpu.make_async_copy(recv_ref.at[pl.ds(n * rows, rows)], bounce.at[n % depth], tsem.at[n % depth])
+
+    def put(n):
+        return [pltpu.make_async_copy(bounce.at[n % depth, :, pl.ds(col, width)], full_ref.at[dst(n * rows, rows, width)],
+                                      psem.at[m, n % depth]) for m, (col, width, dst) in enumerate(place_pieces)]
+
+    for n in range(min(depth, steps)):
+        take(n).start()
+    waited = 0
+    for n in range(steps):
+        take(n).wait()
+        for copy in put(n):
+            copy.start()
+        if n >= depth // 2 and waited + depth < steps:
+            for copy in put(waited):
+                copy.wait()
+            take(waited + depth).start()
+            waited += 1
+    for n in range(waited, steps):
+        for copy in put(n):
+            copy.wait()
 
 
 def place(recv, full, place_pieces, steps):
@@ -611,8 +689,8 @@
         in_specs=[ANY, ANY],
         out_specs=ANY,
         out_shape=jax.ShapeDtypeStruct(full.shape, F32),
-        scratch_shapes=[pltpu.VMEM((2, recv.shape[0] // steps, recv.shape[1]), F32),
-                        pltpu.SemaphoreType.DMA((1 + len(place_pieces), 2))],
+        scratch_shapes=[pltpu.VMEM((8, recv.shape[0] // steps, recv.shape[1]), F32), pltpu.SemaphoreType.DMA((8,)),
+                        pltpu.SemaphoreType.DMA((len(place_pieces), 8))],
         input_output_aliases={1: 0},
         compiler_params=pltpu.CompilerParams(vmem_limit_bytes=VMEM_LIMIT),
         cost_estimate=pl.CostEstimate(flops=recv.size, bytes_accessed=8 * recv.size, transcendentals=0),
@@ -666,11 +744,8 @@
     pair = [(i, i ^ 1) for i in range(ranks)]
     qh, kh = q_dim // 2, kv_dim // 2
 
-    hidden_wide = hidden.astype(F32)
-    inv_rms = lax.rsqrt(jnp.mean(hidden_wide * hidden_wide, axis=-1, keepdims=True) + NORM_EPS)
-    normed = (hidden_wide * inv_rms * norm_weight).astype(BF16)
-    gathered, o_all, g_all, o_send, g_send = attend(normed, grad_out, w_qkv, w_out,
-                                                    half_tables(positions, long_factor), ranks)
+    gathered, _, inv_rms, o_all, g_all, o_send, g_send = attend(hidden, norm_weight[None], grad_out, w_qkv, w_out,
+                                                                half_tables(positions, long_factor), ranks)
     o_pair = lax.ppermute(o_send, 'sp', pair)
     g_pair = lax.ppermute(g_send, 'sp', pair)
 
@@ -689,25 +764,25 @@
 
     dwq_struct = jax.ShapeDtypeStruct(w_qkv.shape, F32)
     dwo_struct = jax.ShapeDtypeStruct(w_out.shape, F32)
-    dwq, send_q = weight_grad(gathered, g_all, ("plane", 0), ("cols", 0, qh), (dim, qh), 4,
+    dwq, send_q = weight_grad(gathered, g_all, ("plane", 0), ("cols", 0, qh), (dim, qh), 8,
                               [(0, 0, qh, own_cols(0, qh)), (1, 0, qh, same)], dwq_struct, None, [], [], "wgrad_q")
     recv_q = lax.ppermute(send_q, 'sp', pair)
-    dwo, send_o = weight_grad(o_all, gathered, ("cols", 0, qh), ("plane", 1), (qh, dim), 4,
+    dwo, send_o = weight_grad(o_all, gathered, ("cols", 0, qh), ("plane", 1), (qh, dim), 6,
                               [(0, 0, dim, own_rows(qh)), (1, 0, dim, same)], dwo_struct, None, [], [dwq, o_pair, g_pair],
                               "wgrad_out")
     recv_o = lax.ppermute(send_o, 'sp', pair)
-    grad_hidden, grad_norm = hidden_grad(hidden, grad_out, inv_rms.reshape(nb * tl, 1), norm_weight[None], w_qkv, g_all,
+    grad_hidden, grad_norm = hidden_grad(hidden, grad_out, inv_rms, norm_weight[None], w_qkv, g_all,
                                          g_pair, [qh, kh, kh], dwo)
-    dwq, send_kv, dwo = weight_grad(gathered, g_all, ("plane", 0), ("cols", qh, 2 * kh), (dim, 2 * kh), 4,
+    grad_norm = group_sum(grad_norm.reshape(-1, 128), ranks)
+    dwq, send_kv, dwo = weight_grad(gathered, g_all, ("plane", 0), ("cols", qh, 2 * kh), (dim, 2 * kh), 8,
                                     [(0, 0, kh, own_cols(q_dim, kh)), (0, kh, kh, own_cols(q_dim + kv_dim, kh)),
                                      (1, 0, 2 * kh, same)], dwq_struct, dwq,
                                     [(recv_o, dwo, [(0, dim, peer_rows(qh))]), (recv_q, None, [(0, qh, peer_cols(0, qh))])],
                                     [grad_norm], "wgrad_kv")
     recv_kv = lax.ppermute(send_kv, 'sp', pair)
-    grad_norm = group_sum(grad_norm.reshape(-1, 128), ranks).reshape(-1)
     out_hidden = project_out(hidden, w_out, o_all, o_pair, [qh], send_kv)
-    dwq = place(recv_kv, dwq, [(0, kh, peer_cols(q_dim, kh)), (kh, kh, peer_cols(q_dim + kv_dim, kh))], 8)
-    return out_hidden, grad_hidden, grad_norm, dwq, dwo
+    dwq = place(recv_kv, dwq, [(0, kh, peer_cols(q_dim, kh)), (kh, kh, peer_cols(q_dim + kv_dim, kh))], 16)
+    return out_hidden, grad_hidden, grad_norm.reshape(-1), dwq, dwo
 
 
 def solution(mesh):

time: 865 us -> 835 us (0.965)
  Pallas kernels: 838 us -> 816 us
  other arithmetic: 14.3 us -> 2.22 us
    pallas_call x1, Pallas kernels: 19.6 us -> 6.33 us  [group_sum(): pl.pallas_call(functools.partial(group_sum_kernel, ranks), in_specs=[ANY]...]
  transfers between devices with their start and end apart: 5 -> 5, of which waited for: 0 -> 0; matrix products, arithmetic and copies ran while one was open for 0% -> 0% of each run, Pallas kernels for 33% -> 32%
where the time goes in v4:
time: 835 us; the launch traced here: 824 us
  Pallas kernels  816 us (98%)
    pallas_call x1, Pallas kernels, attend(): pl.pallas_call(functools.partial(attend_kernel, ranks, slots, group, hd,...  470 us
    pallas_call x3, Pallas kernels, weight_grad(): pl.pallas_call(functools.partial(weight_grad_kernel, nb, left_at, right_a...  249 us
    pallas_call x1, Pallas kernels, hidden_grad(): pl.pallas_call(functools.partial(hidden_grad_kernel, parts), grid=(dim //...  53.5 us
    pallas_call x1, Pallas kernels, project_out(): pl.pallas_call(functools.partial(project_out_kernel, parts), grid=(dim //...  27.1 us
  transfers between devices with their start and end apart: 5, of which 0 were waited for; matrix products, arithmetic and copies ran while one was open for 0% of the time, Pallas kernels for 32%

profile of v4, /device:TPU:113, one launch (start us, length us, event | category | flops | bytes accessed | tf_op | source)
XLA Modules:
  0.0 824.3 jit_solution(2734363695720162001)
XLA Ops:
  0.6 0.7 convert_element_type.6
  1.3 0.7 multiply_divide_fusion
  2.0 0.2 fusion
  2.2 0.7 pad_maximum_fusion.tab_ref
  2.9 470.3 %attend.1 = (bf16[2,8,16,64,3072]{4,3,2,1,0:T(8,128)(2,1)}, bf16[16,64,3072]{2,1,0:T(8,128)(2,1)}, f32[1024,1]{1,0:T(8,128)}, bf16[8,16,64,1536]{3,2,1,0:T(8,128...) custom-call(bf16[16,64,3072]{2,1,0:T(8,128)(2,1)} %x_ref.5, ...), custom_call_target="tpu_custom_call" | custom-call | flops 283467841536 | bytes 268435456 | tf_op jit(solution)/shard_map/attend/pallas_call | solution.py:353
  473.2 3.3 collective-permute-start.1
  476.5 0.1 collective-permute-start
  476.6 90.2 %wgrad_q.1 = (f32[3072,5120]{1,0:T(8,128)}, f32[3072,1536]{1,0:T(8,128)}) custom-call(bf16[2,8,16,64,3072]{4,3,2,1,0:T(8,128)(2,1)} %get-tuple-element.22.refs_0_.refs_1_, bf16[8,16,64,2560]{3,2,1,0:T(8,128)(2,1)} %get-tuple-element.23.refs_1_.gm_ref), custom_call_target="tpu_custom_call" | custom-call | flops 77309411328 | bytes 113246208 | tf_op jit(solution)/shard_map/wgrad_q/pallas_call | solution.py:526
  566.8 0.5 collective-permute-start.3
  567.3 0.0 collective-permute-done.refs_3_.op_ref
  567.3 0.0 collective-permute-done.1.refs_4_.gp_ref
  567.3 89.5 %wgrad_out.1 = (f32[3072,3072]{1,0:T(8,128)}, f32[1536,3072]{1,0:T(8,128)}) custom-call(bf16[8,16,64,1536]{3,2,1,0:T(8,128)(2,1)} %get-tuple-element.20.refs_0_.om_ref, bf16[2,8,16,64,3072]{4,3,2,1,0:T(8,128)(2,1)} %get-tuple-element.22.refs_0_.refs_1_, f32[3072,5120]{1,0:T(8,128)} %get-tuple-element.24.refs_2_.refs_5_, ...), custom_call_target="tpu_custom_call" | custom-call | flops 77309411328 | bytes 113246208 | tf_op jit(solution)/shard_map/wgrad_out/pallas_call | solution.py:526
  656.8 0.2 collective-permute-start.2
  656.9 53.5 %hidden_grad.1 = (bf16[16,64,3072]{2,1,0:T(8,128)(2,1)}, f32[1,3072]{1,0:T(1,128)}) custom-call(bf16[3072,5120]{1,0:T(8,128)(2,1)} %w_ref.2, bf16[16,64,3072]{2,1,0:T(8,128)(2,1)} %x_ref.5, f32[1024,1]{1,0:T(8,128)} %get-tuple-element.29.inv_ref, f32[1,3072]{1,0:T(1,128)} %bitcast.5, bf16[8,16,64,2560]{3,2,1,0:T(8,128)(2,1)} %get-tuple-element.23.refs_1_.gm_ref, ...), custom_call_target="tpu_custom_call" | custom-call | flops 32212254720 | bytes 31457280 | tf_op jit(solution)/shard_map/hidden_grad/pallas_call | solution.py:609
  710.4 6.3 group_sum.1.refs_6_
  716.8 0.0 collective-permute-done.3.refs_4_
  716.8 0.0 collective-permute-done.2.refs_2_
  716.8 69.7 %wgrad_kv.1 = (f32[3072,5120]{1,0:T(8,128)}, f32[3072,1024]{1,0:T(8,128)}, f32[3072,3072]{1,0:T(8,128)}) custom-call(bf16[2,8,16,64,3072]{4,3,2,1,0:T(8,128)(2,1)} %get-tuple-element.22.refs_0_.refs_1_, bf16[8,16,64,2560]{3,2,1,0:T(8,128)(2,1)} %get-tuple-element.23.refs_1_.gm_ref, ...), custom_call_target="tpu_custom_call", output_to_operand_aliasing={{2}: (3, {}), {0}: (5, {})} | custom-call | flops 51539607552 | bytes 92274688 | tf_op jit(solution)/shard_map/wgrad_kv/pallas_call | solution.py:526
  786.6 0.4 collective-permute-start.4
  787.0 27.1 %project_out.1 = bf16[16,64,3072]{2,1,0:T(8,128)(2,1)} custom-call(bf16[3072,3072]{1,0:T(8,128)(2,1)} %w_ref.3, bf16[16,64,3072]{2,1,0:T(8,128)(2,1)} %x_ref.5, bf16[8,16,64,1536]{3,2,1,0:T(8,128)(2,1)} %get-tuple-element.20.refs_0_.om_ref, bf16[16,64,1536]{2,1,0:T(8,128)(2,1)} %collective-permute-done.refs_3_.op_ref, f32[3072,1024]{1,0:T(8,128)} %get-tuple-element.31.order_ref), custom_call_target="tpu_custom_call" | custom-call | flops 19327352832 | bytes 18874368 | tf_op jit(solution)/shard_map/project_out/pallas_call | solution.py:645
  814.1 0.0 collective-permute-done.4.recv_ref
  814.1 0.0 copy-start
  814.1 9.1 %place.1 = f32[3072,5120]{1,0:T(8,128)} custom-call(f32[3072,1024]{1,0:T(8,128)} %collective-permute-done.4.recv_ref, f32[3072,5120]{1,0:T(8,128)} %get-tuple-element.33.full_in), custom_call_target="tpu_custom_call", output_to_operand_aliasing={{}: (1, {})} | custom-call | flops 3145728 | bytes 25165824 | tf_op jit(solution)/shard_map/place/pallas_call | solution.py:687
  823.2 0.0 copy-done
  823.3 0.6 copy.19
Async XLA Ops:
  473.2 94.1 %collective-permute-start.1 = (bf16[16,64,2560]{2,1,0:T(8,128)(2,1)}, bf16[16,64,2560]{2,1,0:T(8,128)(2,1)}, u32[]{:S(2)}, u32[]{:S(2)}) collective-permute-start(bf16[16,64,2560]{2,1,0:T(8,128)(2,1)} %get-tuple-element.25), channel_id=1, source_target_pairs={{0,1},{1,0},{2,3},{3,2},{4,5},{5,4},{6,7},{7,6},{8,9},{9,8},{10,11... | collective-permute-start | bytes 15728648 | tf_op jit(solution)/shard_map/ppermute | solution.py:750
  476.5 90.8 %collective-permute-start = (bf16[16,64,1536]{2,1,0:T(8,128)(2,1)}, bf16[16,64,1536]{2,1,0:T(8,128)(2,1)}, u32[]{:S(2)}, u32[]{:S(2)}) collective-permute-start(bf16[16,64,1536]{2,1,0:T(8,128)(2,1)} %get-tuple-element.21), channel_id=1, source_target_pairs={{0,1},{1,0},{2,3},{3,2},{4,5},{5,4},{6,7},{7,6},{8,9},{9,8},{10,11... | collective-permute-start | bytes 9437192 | tf_op jit(solution)/shard_map/ppermute | solution.py:749
  566.8 150.0 %collective-permute-start.3 = (f32[3072,1536]{1,0:T(8,128)}, f32[3072,1536]{1,0:T(8,128)}, u32[]{:S(2)}, u32[]{:S(2)}) collective-permute-start(f32[3072,1536]{1,0:T(8,128)} %get-tuple-element.28), channel_id=1, source_target_pairs={{0,1},{1,0},{2,3},{3,2},{4,5},{5,4},{6,7},{7,6},{8,9},{9,8},{10,11... | collective-permute-start | bytes 56623112 | tf_op jit(solution)/shard_map/ppermute | solution.py:769
  656.8 60.0 %collective-permute-start.2 = (f32[1536,3072]{1,0:T(8,128)}, f32[1536,3072]{1,0:T(8,128)}, u32[]{:S(2)}, u32[]{:S(2)}) collective-permute-start(f32[1536,3072]{1,0:T(8,128)} %get-tuple-element.26), channel_id=1, source_target_pairs={{0,1},{1,0},{2,3},{3,2},{4,5},{5,4},{6,7},{7,6},{8,9},{9,8},{10,11... | collective-permute-start | bytes 56623112 | tf_op jit(solution)/shard_map/ppermute | solution.py:773
  786.6 27.5 %collective-permute-start.4 = (f32[3072,1024]{1,0:T(8,128)}, f32[3072,1024]{1,0:T(8,128)}, u32[]{:S(2)}, u32[]{:S(2)}) collective-permute-start(f32[3072,1024]{1,0:T(8,128)} %get-tuple-element.31.order_ref), channel_id=1, source_target_pairs={{0,1},{1,0},{2,3},{3,2},{4,5},{5,4},{6,7},{7,6},{8,9},{9,8},{10,11... | collective-permute-start | bytes 37748744 | tf_op jit(solution)/shard_map/ppermute | solution.py:782
  814.1 9.1 %copy-start = (f32[24,128]{1,0:T(8,128)S(1)}, f32[24,128]{1,0:T(8,128)}, u32[]{:S(2)}) copy-start(f32[24,128]{1,0:T(8,128)} %group_sum.1.refs_6_) | copy-start | bytes 36868
